TPU v7x, 32 devices: a whole 2x2x4 slice. The times are simulated.
32 devices in a mesh: grp: 2 (over y), mesh: 16 (over z, x, core).
Axes of the slice: x: 2, y: 2, z: 4, core: 2. Of those that a mesh axis runs over, the one named last changes fastest.
Arguments:
- state: float32 [2, 5, 256, 4096], P('grp', None, 'mesh'), may hold values from -6 to 6
- burn_rate: float32 [2, 256, 4096], P('grp', 'mesh'), may hold values from 0.1 to 1
- face_map: int32 [2, 16, 1024], P('grp', 'mesh'), may hold values from 0 to 1023, as said below
Outputs:
- new_state: float32 [2, 5, 256, 4096], P('grp', None, 'mesh')
- head: float32 [2, 256, 4096], P('grp', 'mesh')
Inputs may be any that keep to these rules, and one draw needn't show every extreme that they name: `face_map`: entry k * 64 + j of a mesh names the cell of its partner's interface plane that feeds its ghost cell (k, j).
All inputs are finite; a program needn't handle non-finite values.
Results may differ from a plain program's by a relative error of at most 0.00025.
Values sent between devices are 32-bit elements; how exact they have to be, the bound alone decides.
No kernel may reach another device: no remote copies, remote signals or barrier semaphores. Data moves between devices by JAX's collectives and lax.ppermute only.
A program may use at most 64 MiB of HBM per device.

v0:
```python
import jax
import jax.numpy as jnp
from jax import lax
from jax.sharding import PartitionSpec as P

NX = 64
NY = 64
FIELDS = 5
SECTIONS = 2
ITERS = 3


COURANT = 0.1
DIFFUSION = 0.05
STOICHIOMETRY = 2.0
EXPANSION = 1.0


def with_halo(block, sides, width):
    for axis, dim in sides:
        count = lax.axis_size(axis)
        forward = [(i, i + 1) for i in range(count - 1)]
        backward = [(target, source) for source, target in forward]
        low = lax.ppermute(
            lax.slice_in_dim(block, block.shape[dim] - width, None, axis=dim), axis, forward
        )
        high = lax.ppermute(lax.slice_in_dim(block, 0, width, axis=dim), axis, backward)
        block = jnp.concatenate([low, block, high], axis=dim)
    return block


def from_partner(block, axis, bit):
    count = lax.axis_size(axis)
    route = []
    for low in range(count):
        high = low | 1 << bit
        if high != low and high < count:
            route += [(low, high), (high, low)]
    return lax.ppermute(block, axis, route)


def sine_table(length):
    places = jnp.arange(length, dtype=jnp.float32) + 1.0
    angles = jnp.pi * places[:, None] * places[None, :] / (length + 1)
    return jnp.sin(angles) * jnp.sqrt(2.0 / (length + 1))


def mode_values(length):
    places = jnp.arange(length, dtype=jnp.float32) + 1.0
    return 2.0 - 2.0 * jnp.cos(jnp.pi * places / (length + 1))


def poisson_solve(source):
    table_z = sine_table(source.shape[1])
    table_x = sine_table(source.shape[2])
    table_y = sine_table(source.shape[3])
    precise = lax.Precision.HIGHEST
    spectral = jnp.einsum("ck,mkij->mcij", table_z, source, precision=precise)
    spectral = jnp.einsum("ai,mcij->mcaj", table_x, spectral, precision=precise)
    spectral = jnp.einsum("mcaj,jb->mcab", spectral, table_y, precision=precise)
    modes = (
        mode_values(source.shape[1])[:, None, None]
        + mode_values(source.shape[2])[None, :, None]
        + mode_values(source.shape[3])[None, None, :]
    )
    spectral = spectral / modes[None]
    solved = jnp.einsum("ck,mcab->mkab", table_z, spectral, precision=precise)
    solved = jnp.einsum("ai,mkab->mkib", table_x, solved, precision=precise)
    return jnp.einsum("mkib,jb->mkij", solved, table_y, precision=precise)


def tendency(zpadded, x_low, x_high, burning):
    centre = zpadded[:, 2:-2]
    xpadded = jnp.concatenate([x_low[:, :, None, :], centre, x_high[:, :, None, :]], axis=2)
    ypadded = jnp.pad(centre, ((0, 0), (0, 0), (0, 0), (1, 1)))
    east, west = (xpadded[:, :, 2:], xpadded[:, :, :-2])
    north, south = (ypadded[..., 2:], ypadded[..., :-2])
    above, below = (zpadded[:, 3:-1], zpadded[:, 1:-3])
    above_two, below_two = (zpadded[:, 4:], zpadded[:, :-4])
    grad_x = 0.5 * (east - west)
    grad_y = 0.5 * (north - south)
    grad_z = (8.0 * (above - below) - (above_two - below_two)) / 12.0
    laplace = east + west + north + south + above + below - 6.0 * centre
    advection = centre[0] * grad_x + centre[1] * grad_y + centre[2] * grad_z
    reaction = burning * centre[3] * centre[4]
    change = -COURANT * advection + DIFFUSION * laplace
    change = change.at[3].add(-reaction).at[4].add(-STOICHIOMETRY * reaction)
    divergence = grad_x[0] + grad_y[1] + 0.5 * (above[2] - below[2])
    return (change, EXPANSION * reaction - divergence)


def with_ghosts(source, z_low, z_high, x_low, x_high):
    source = source.at[:, 0].add(z_low).at[:, -1].add(z_high)
    return source.at[:, :, 0, :].add(x_low).at[:, :, -1, :].add(x_high)


def correct(fields, pressure, z_low, z_high, x_low, x_high):
    xpadded = jnp.concatenate([x_low[:, None, :], pressure, x_high[:, None, :]], axis=1)
    ypadded = jnp.pad(pressure, ((0, 0), (0, 0), (1, 1)))
    zpadded = jnp.concatenate([z_low[None], pressure, z_high[None]], axis=0)
    grad_x = 0.5 * (xpadded[:, 2:] - xpadded[:, :-2])
    grad_y = 0.5 * (ypadded[..., 2:] - ypadded[..., :-2])
    grad_z = 0.5 * (zpadded[2:] - zpadded[:-2])
    return jnp.concatenate(
        [
            fields[0:1] - grad_x[None],
            fields[1:2] - grad_y[None],
            fields[2:3] - grad_z[None],
            fields[3:],
        ],
        axis=0,
    )


def own_plane(arrays, is_fine):
    plane = jnp.where(is_fine, arrays[..., -1, :], arrays[..., 0, :])
    return plane.reshape(plane.shape[:-2] + (plane.shape[-2] * plane.shape[-1],))


def place_ghost(received, mapping, is_fine):
    picked = jnp.take(received, mapping, axis=-1)
    picked = picked.reshape(received.shape[:-1] + (received.shape[-1] // NY, NY))
    zeros = jnp.zeros_like(picked)
    return (jnp.where(is_fine, zeros, picked), jnp.where(is_fine, picked, zeros))


def shards(state, burn_rate, face_map):
    is_fine = lax.axis_index("grp") == 0
    height = state.shape[2]
    initial = state[0].reshape(FIELDS, height, NX, NY)
    burning = burn_rate[0].reshape(height, NX, NY)
    mapping = face_map[0, 0]

    def head_ghosts(pressure):
        padded = with_halo(pressure[0].reshape(height, NX * NY), (("mesh", 0),), 1)
        received = from_partner(own_plane(pressure, is_fine), "grp", 0)
        x_low, x_high = place_ghost(received, mapping, is_fine)
        return (padded[0].reshape(1, NX, NY), padded[-1].reshape(1, NX, NY), x_low, x_high)

    current = initial
    pressure = jnp.zeros((1, height, NX, NY), state.dtype)
    for section_no in range(SECTIONS):
        padded = with_halo(current.reshape(FIELDS, height, NX * NY), (("mesh", 1),), 2).reshape(
            FIELDS, height + 4, NX, NY
        )
        received = from_partner(own_plane(current, is_fine), "grp", 0)
        x_low, x_high = place_ghost(received, mapping, is_fine)
        change, source = tendency(padded, x_low, x_high, burning)
        if section_no == 0:
            predicted = current + change
        else:
            predicted = 0.5 * (initial + current + change)
        source = source[None]
        zero_pressure = jnp.zeros((1, height, NX, NY), state.dtype)
        zero_layer = jnp.zeros((1, NX, NY), state.dtype)
        zero_side = jnp.zeros((1, height, NY), state.dtype)

        def sweep_once(sweep, carry):
            ghosts = carry[1]
            solved = poisson_solve(with_ghosts(source, ghosts[0], ghosts[1], ghosts[2], ghosts[3]))
            return (solved, head_ghosts(solved))

        pressure, ghosts = lax.fori_loop(
            0, ITERS, sweep_once, (zero_pressure, (zero_layer, zero_layer, zero_side, zero_side))
        )
        current = correct(
            predicted, pressure[0], ghosts[0][0], ghosts[1][0], ghosts[2][0], ghosts[3][0]
        )
    return (current.reshape(1, FIELDS, height, NX * NY), pressure.reshape(1, height, NX * NY))


def solution(mesh):
    placed = (P("grp", None, "mesh", None), P("grp", "mesh", None), P("grp", "mesh", None))
    return jax.shard_map(
        shards,
        mesh=mesh,
        in_specs=placed,
        out_specs=(P("grp", None, "mesh", None), P("grp", "mesh", None)),
        check_vma=False,
    )
```

profile of v0, /device:TPU:24, one launch (start us, length us, event | category | flops | bytes accessed | tf_op | source)
XLA Modules:
  0.0 271.6 jit_solution(7763465361363386352)
XLA Ops:
  4.7 4.5 %collective-permute-start.7 = (f32[5,2,4096]{2,1,0:T(2,128)}, f32[5,2,4096]{2,1,0:T(2,128)}, u32[]{:S(2)}, u32[]{:S(2)}) collective-permute-start(f32[5,2,4096]{2,1,0:T(2,128)} %get-tuple-element.617), channel_id=1, source_target_pairs={{1,0},{2,1},{3,2},{4,3},{5,4},{6,5},{7,6},{8,7},{9,8},{10,9},{11,1... | collective-permute-start | bytes 491528 | tf_op jit(solution)/shard_map/ppermute | solution.py:27
  9.2 2.2 reshape_squeeze.6
  14.1 2.2 fusion.158
  25.7 5.1 %gather_fusion.2 = f32[1024,5]{1,0:T(8,128)} fusion(f32[5,1024]{0,1:T(8,128)} %collective-permute-done.6, s32[1024]{0:T(1024)S(1)} %fusion.152), kind=kCustom, calls=%fused_computation.clone | custom fusion | bytes 45056 | tf_op jit(solution)/shard_map/jit(_take)/gather | solution.py:121
  30.8 2.3 bitcast_select_fusion.2
  38.1 3.0 %constant_dynamic-update-slice_fusion.1 = (f32[5,18,64,64]{3,2,1,0:T(8,128)}, f32[5,18,64,64]{3,2,1,0:T(8,128)}) fusion(f32[5,16,64,64]{3,2,1,0:T(8,128)S(1)} %reshape_squeeze.6, f32[5,18,64,64]{3,2,1,0:T(8,128)} %constant_dynamic-update-slice_fusion.3), kind=kLoop, calls=%fused_computation.258 | loop fusion | bytes 6553600
  43.0 6.7 %fusion.121 = (f32[5,16,64,64]{3,2,1,0:T(8,128)S(1)}, f32[5,16,64,64]{3,2,1,0:T(8,128)S(1)}, f32[5,16,64,64]{3,2,1,0:T(8,128)S(1)}) fusion(f32[5,18,64,64]{3,2,1,0:T(8,128)} %get-tuple-element.609, f32[5,18,64,64]{3,2,1,0:T(8,128)} %constant_dynamic-update-slice_fusion, f32[5,16,64,64]{3,2,1,0:T(8,128)S(1)} %reshape_squeeze.6, ...), kind=kLoop, calls=%fused_computation.181 | loop fusion | flops 7536640 | bytes 11313152 | tf_op jit(solution)/shard_map/add | solution.py:86
  56.9 75.0 %while.54 = (s32[]{:T(128)}, f32[1,16,64,64]{3,2,1,0:T(8,128)}, f32[1,64,64]{2,1,0:T(8,128)S(1)}, f32[1,64,64]{2,1,0:T(8,128)S(1)}, f32[1,16,64]{2,1,0:T(8,128)S...) while((s32[]{:T(128)}, f32[1,16,64,64]{3,2,1,0:T(8,128)}, ...), condition=%wide.region_1.4_spmd, body=%wide.region_0.0_spmd.sunk | while | flops 226700256 | bytes 5959731 | solution.py:163
  67.0 4.5 %collective-permute-start.1 = (f32[1,4096]{1,0:T(1,128)S(1)}, f32[1,4096]{1,0:T(1,128)S(1)}, u32[]{:S(2)}, u32[]{:S(2)}) collective-permute-start(f32[1,4096]{1,0:T(1,128)S(1)} %slice.945), channel_id=1, source_target_pairs={{1,0},{2,1},{3,2},{4,3},{5,4},{6,5},{7,6},{8,7},{9,8},{10,9},{11,1... | collective-permute-start | bytes 49160 | tf_op jit(solution)/shard_map/while/body/eval_jaxpr/ppermute | solution.py:27
  75.3 4.5 %gather_fusion = f32[1024]{0:T(1024)S(1)} fusion(f32[1024]{0:T(1024)S(1)} %bitcast.273, s32[1024]{0:T(1024)S(1)} %fusion.221), kind=kCustom, calls=%fused_computation.1.clone.clone.1 | custom fusion | bytes 12288 | tf_op jit(solution)/shard_map/while/body/eval_jaxpr/jit(_take)/gather | solution.py:121
  91.9 4.5 %collective-permute-start.1 = (f32[1,4096]{1,0:T(1,128)S(1)}, f32[1,4096]{1,0:T(1,128)S(1)}, u32[]{:S(2)}, u32[]{:S(2)}) collective-permute-start(f32[1,4096]{1,0:T(1,128)S(1)} %slice.945), channel_id=1, source_target_pairs={{1,0},{2,1},{3,2},{4,3},{5,4},{6,5},{7,6},{8,7},{9,8},{10,9},{11,1... | collective-permute-start | bytes 49160 | tf_op jit(solution)/shard_map/while/body/eval_jaxpr/ppermute | solution.py:27
  100.2 4.5 %gather_fusion = f32[1024]{0:T(1024)S(1)} fusion(f32[1024]{0:T(1024)S(1)} %bitcast.273, s32[1024]{0:T(1024)S(1)} %fusion.221), kind=kCustom, calls=%fused_computation.1.clone.clone.1 | custom fusion | bytes 12288 | tf_op jit(solution)/shard_map/while/body/eval_jaxpr/jit(_take)/gather | solution.py:121
  116.9 4.5 %collective-permute-start.1 = (f32[1,4096]{1,0:T(1,128)S(1)}, f32[1,4096]{1,0:T(1,128)S(1)}, u32[]{:S(2)}, u32[]{:S(2)}) collective-permute-start(f32[1,4096]{1,0:T(1,128)S(1)} %slice.945), channel_id=1, source_target_pairs={{1,0},{2,1},{3,2},{4,3},{5,4},{6,5},{7,6},{8,7},{9,8},{10,9},{11,1... | collective-permute-start | bytes 49160 | tf_op jit(solution)/shard_map/while/body/eval_jaxpr/ppermute | solution.py:27
  125.1 4.5 %gather_fusion = f32[1024]{0:T(1024)S(1)} fusion(f32[1024]{0:T(1024)S(1)} %bitcast.273, s32[1024]{0:T(1024)S(1)} %fusion.221), kind=kCustom, calls=%fused_computation.1.clone.clone.1 | custom fusion | bytes 12288 | tf_op jit(solution)/shard_map/while/body/eval_jaxpr/jit(_take)/gather | solution.py:121
  131.9 4.4 %multiply_bitcast_fusion.2 = (f32[16,64,64]{2,1,0:T(8,128)}, f32[1,16,64,64]{3,2,1,0:T(8,128)S(1)}, f32[16,64,64]{2,1,0:T(8,128)}, f32[1,16,64,64]{3,2,1,0:T(8,1...) fusion(f32[16,64,64]{2,1,0:T(8,128)} %bitcast.283, f32[16,1,64]{2,1,0:T(1,128)S(1)} %bitcast.302, ...), kind=kLoop, calls=%fused_computation.249 | loop fusion | flops 1048576 | bytes 2662400 | tf_op jit(solution)/shard_map/mul | solution.py:84
  139.1 3.1 %reshape.1127 = f32[5,16,4096]{2,1,0:T(8,128)} reshape(f32[5,16,64,64]{3,2,1,0:T(8,128)} %pad_maximum_fusion.11) | data formatting | bytes 2621440 | tf_op jit(solution)/shard_map/reshape | solution.py:143
  149.9 2.4 collective-permute-start.11
  152.3 3.0 %collective-permute-done.9 = f32[5,1024]{0,1:T(8,128)} collective-permute-done((f32[5,1024]{0,1:T(8,128)}, f32[5,1024]{0,1:T(8,128)}, u32[]{:S(2)}, u32[]{:S(2)}) %collective-permute-start.9) | collective-permute-done | bytes 20512 | tf_op jit(solution)/shard_map/ppermute | solution.py:39
  155.2 5.1 %gather_fusion.3 = f32[1024,5]{1,0:T(8,128)} fusion(f32[5,1024]{0,1:T(8,128)} %collective-permute-done.9, s32[1024]{0:T(1024)S(1)} %fusion.152), kind=kCustom, calls=%fused_computation.2.clone | custom fusion | bytes 45056 | tf_op jit(solution)/shard_map/jit(_take)/gather | solution.py:121
  160.3 2.2 bitcast_select_fusion
  165.0 4.3 %fusion.123 = f32[5,16,64,64]{3,2,1,0:T(8,128)} fusion(f32[5,16,1,64]{3,2,1,0:T(1,128)S(1)} %copy.39, f32[2,16,64,64]{3,2,1,0:T(8,128)} %slice.754, f32[1,16,64,64]{3,2,1,0:T(8,128)} %copy-done.4, f32[1,16,64,64]{3,2,1,0:T(8,128)} %copy-done.2, f32[1,16,64,64]{3,2,1,0:T(8,128)S(1)} %get-tuple-element.577, f32[5,16,1,64]{3,2,1,0:T(1,128)S(1)} %copy.40), kind=kLoop, calls=%fused_computation.192 | loop fusion | flops 2949120 | bytes 2662400 | tf_op jit(solution)/shard_map/sub | solution.py:80
  172.4 2.8 %pad_maximum_fusion = (f32[5,18,64,64]{3,2,1,0:T(8,128)S(1)}, f32[5,18,64,64]{3,2,1,0:T(8,128)S(1)}) fusion(f32[5,2,64,64]{3,2,1,0:T(8,128)S(1)} %concatenate.125, f32[2,16,64,64]{3,2,1,0:T(8,128)} %slice.754, f32[1,16,64,64]{3,2,1,0:T(8,128)} %copy-done.4, f32[1,16,64,64]{3,2,1,0:T(8,128)} %copy-done.2, f32[1,16,64,64]{3,2,1,0:T(8,128)S(1)} %get-tuple-element.577, ...), kind=kLoop, calls=%fused_computation.160 | loop fusion | flops 2949120 | bytes 4587520 | tf_op jit(solution)/shard_map/concatenate | solution.py:28
  176.4 6.1 %fusion.116 = (f32[5,16,64,64]{3,2,1,0:T(8,128)}, f32[5,16,64,64]{3,2,1,0:T(8,128)}) fusion(f32[5,18,64,64]{3,2,1,0:T(8,128)S(1)} %get-tuple-element.607, f32[5,18,64,64]{3,2,1,0:T(8,128)S(1)} %get-tuple-element.606, f32[5,16,64,64]{3,2,1,0:T(8,128)S(1)} %copy-done.6, f32[16,64,64]{2,1,0:T(8,128)} %get-tuple-element.603, f32[16,64,64]{2,1,0:T(8,128)S(1)} %copy-done.19, ...), kind=kLoop, calls=%fused_computation.167 | loop fusion | flops 9502720 | bytes 11313152 | tf_op jit(solution)/shard_map/add | solution.py:86
  189.6 71.8 %while.55 = (s32[]{:T(128)}, f32[1,16,64,64]{3,2,1,0:T(8,128)}, f32[1,64,64]{2,1,0:T(8,128)S(1)}, f32[1,64,64]{2,1,0:T(8,128)S(1)}, f32[1,16,64]{2,1,0:T(8,128)S...) while((s32[]{:T(128)}, f32[1,16,64,64]{3,2,1,0:T(8,128)}, ...), condition=%wide.region_3.6_spmd, body=%wide.region_2.5_spmd.sunk | while | flops 226700256 | bytes 5959731 | solution.py:163
  198.5 4.5 %collective-permute-start.4 = (f32[1,4096]{1,0:T(1,128)S(1)}, f32[1,4096]{1,0:T(1,128)S(1)}, u32[]{:S(2)}, u32[]{:S(2)}) collective-permute-start(f32[1,4096]{1,0:T(1,128)S(1)} %slice.955), channel_id=1, source_target_pairs={{1,0},{2,1},{3,2},{4,3},{5,4},{6,5},{7,6},{8,7},{9,8},{10,9},{11,1... | collective-permute-start | bytes 49160 | tf_op jit(solution)/shard_map/while/body/eval_jaxpr/ppermute | solution.py:27
  206.8 4.5 %gather_fusion.1 = f32[1024]{0:T(1024)S(1)} fusion(f32[1024]{0:T(1024)S(1)} %bitcast.274, s32[1024]{0:T(1024)S(1)} %fusion.240), kind=kCustom, calls=%fused_computation.3.clone.clone.1 | custom fusion | bytes 12288 | tf_op jit(solution)/shard_map/while/body/eval_jaxpr/jit(_take)/gather | solution.py:121
  222.4 4.5 %collective-permute-start.4 = (f32[1,4096]{1,0:T(1,128)S(1)}, f32[1,4096]{1,0:T(1,128)S(1)}, u32[]{:S(2)}, u32[]{:S(2)}) collective-permute-start(f32[1,4096]{1,0:T(1,128)S(1)} %slice.955), channel_id=1, source_target_pairs={{1,0},{2,1},{3,2},{4,3},{5,4},{6,5},{7,6},{8,7},{9,8},{10,9},{11,1... | collective-permute-start | bytes 49160 | tf_op jit(solution)/shard_map/while/body/eval_jaxpr/ppermute | solution.py:27
  230.7 4.5 %gather_fusion.1 = f32[1024]{0:T(1024)S(1)} fusion(f32[1024]{0:T(1024)S(1)} %bitcast.274, s32[1024]{0:T(1024)S(1)} %fusion.240), kind=kCustom, calls=%fused_computation.3.clone.clone.1 | custom fusion | bytes 12288 | tf_op jit(solution)/shard_map/while/body/eval_jaxpr/jit(_take)/gather | solution.py:121
  246.4 4.5 %collective-permute-start.4 = (f32[1,4096]{1,0:T(1,128)S(1)}, f32[1,4096]{1,0:T(1,128)S(1)}, u32[]{:S(2)}, u32[]{:S(2)}) collective-permute-start(f32[1,4096]{1,0:T(1,128)S(1)} %slice.955), channel_id=1, source_target_pairs={{1,0},{2,1},{3,2},{4,3},{5,4},{6,5},{7,6},{8,7},{9,8},{10,9},{11,1... | collective-permute-start | bytes 49160 | tf_op jit(solution)/shard_map/while/body/eval_jaxpr/ppermute | solution.py:27
  254.6 4.5 %gather_fusion.1 = f32[1024]{0:T(1024)S(1)} fusion(f32[1024]{0:T(1024)S(1)} %bitcast.274, s32[1024]{0:T(1024)S(1)} %fusion.240), kind=kCustom, calls=%fused_computation.3.clone.clone.1 | custom fusion | bytes 12288 | tf_op jit(solution)/shard_map/while/body/eval_jaxpr/jit(_take)/gather | solution.py:121
  263.4 3.3 %fusion.131 = (f32[1,16,64,64]{3,2,1,0:T(8,128)S(1)}, f32[1,16,64,64]{3,2,1,0:T(8,128)S(1)}, f32[1,16,64,64]{3,2,1,0:T(8,128)S(1)}) fusion(f32[16,64,64]{2,1,0:T(8,128)} %bitcast.279, f32[16,1,64]{2,1,0:T(1,128)S(1)} %bitcast.300, f32[16,1,64]{2,1,0:T(1,128)S(1)} %bitcast.301, f32[5,16,64,64]{3,2,1,0:T(8,128)} %copy-done.10, ...), kind=kLoop, calls=%fused_computation.204 | loop fusion | flops 851968 | bytes 1875968 | tf_op jit(solution)/shard_map/sub | solution.py:106
  268.5 3.1 %reshape.1128 = f32[1,5,16,4096]{3,2,1,0:T(8,128)} reshape(f32[5,16,64,64]{3,2,1,0:T(8,128)} %pad_maximum_fusion.12) | data formatting | bytes 2621440 | tf_op jit(solution)/shard_map/reshape | solution.py:169
  (349 shorter events, 149.3 us)
Async XLA Ops:
  2.8 33.4 %collective-permute-start.8 = (f32[5,2,4096]{2,1,0:T(2,128)}, f32[5,2,4096]{2,1,0:T(2,128)}, u32[]{:S(2)}, u32[]{:S(2)}) collective-permute-start(f32[5,2,4096]{2,1,0:T(2,128)} %get-tuple-element.618), channel_id=1, source_target_pairs={{0,1},{1,2},{2,3},{3,4},{4,5},{5,6},{6,7},{7,8},{8,9},{9,10},{10,1... | collective-permute-start | bytes 491528 | tf_op jit(solution)/shard_map/ppermute | solution.py:24
  4.7 36.4 %collective-permute-start.7 = (f32[5,2,4096]{2,1,0:T(2,128)}, f32[5,2,4096]{2,1,0:T(2,128)}, u32[]{:S(2)}, u32[]{:S(2)}) collective-permute-start(f32[5,2,4096]{2,1,0:T(2,128)} %get-tuple-element.617), channel_id=1, source_target_pairs={{1,0},{2,1},{3,2},{4,3},{5,4},{6,5},{7,6},{8,7},{9,8},{10,9},{11,1... | collective-permute-start | bytes 491528 | tf_op jit(solution)/shard_map/ppermute | solution.py:27
  12.6 13.1 %collective-permute-start.6 = (f32[5,1024]{0,1:T(8,128)}, f32[5,1024]{0,1:T(8,128)}, u32[]{:S(2)}, u32[]{:S(2)}) collective-permute-start(f32[5,1024]{0,1:T(8,128)} %bitcast.49), channel_id=1, source_target_pairs={{0,16},{16,0},{1,17},{17,1},{2,18},{18,2},{3,19},{19,3},{4,20},{20... | collective-permute-start | bytes 61448 | tf_op jit(solution)/shard_map/ppermute | solution.py:39
  23.4 26.3 %copy-start.12 = (f32[1,16,64,64]{3,2,1,0:T(8,128)}, f32[1,16,64,64]{3,2,1,0:T(8,128)S(1)}, u32[]{:S(2)}) copy-start(f32[1,16,64,64]{3,2,1,0:T(8,128)S(1)} %reshape_squeeze.7) | copy-start | bytes 786436
  43.0 6.7 %copy-start.17 = (f32[1,16,64,64]{3,2,1,0:T(8,128)S(1)}, f32[1,16,64,64]{3,2,1,0:T(8,128)}, u32[]{:S(2)}) copy-start(f32[1,16,64,64]{3,2,1,0:T(8,128)} %squeeze.64) | copy-start | bytes 786436
  64.9 17.2 %copy-start.14 = (f32[16,64,64]{2,1,0:T(8,128)}, f32[16,64,64]{2,1,0:T(8,128)S(1)}, u32[]{:S(2)}) copy-start(f32[16,64,64]{2,1,0:T(8,128)S(1)} %fusion.218) | copy-start | bytes 786436 | tf_op jit(solution)/shard_map/while
  65.0 15.0 %collective-permute-start = (f32[1,4096]{1,0:T(1,128)S(1)}, f32[1,4096]{1,0:T(1,128)S(1)}, u32[]{:S(2)}, u32[]{:S(2)}) collective-permute-start(f32[1,4096]{1,0:T(1,128)S(1)} %slice.944), channel_id=1, source_target_pairs={{0,1},{1,2},{2,3},{3,4},{4,5},{5,6},{6,7},{7,8},{8,9},{9,10},{10,1... | collective-permute-start | bytes 49160 | tf_op jit(solution)/shard_map/while/body/eval_jaxpr/ppermute | solution.py:24
  67.0 14.3 %collective-permute-start.1 = (f32[1,4096]{1,0:T(1,128)S(1)}, f32[1,4096]{1,0:T(1,128)S(1)}, u32[]{:S(2)}, u32[]{:S(2)}) collective-permute-start(f32[1,4096]{1,0:T(1,128)S(1)} %slice.945), channel_id=1, source_target_pairs={{1,0},{2,1},{3,2},{4,3},{5,4},{6,5},{7,6},{8,7},{9,8},{10,9},{11,1... | collective-permute-start | bytes 49160 | tf_op jit(solution)/shard_map/while/body/eval_jaxpr/ppermute | solution.py:27
  71.7 3.6 %collective-permute-start.2 = (f32[1,1024]{1,0:T(1,128)S(1)}, f32[1,1024]{1,0:T(1,128)S(1)}, u32[]{:S(2)}, u32[]{:S(2)}) collective-permute-start(f32[1,1024]{1,0:T(1,128)S(1)} %select_n.349), channel_id=1, source_target_pairs={{0,16},{16,0},{1,17},{17,1},{2,18},{18,2},{3,19},{19,3},{4,20},{20... | collective-permute-start | bytes 12296 | tf_op jit(solution)/shard_map/while/body/eval_jaxpr/ppermute | solution.py:39
  89.8 17.2 %copy-start.14 = (f32[16,64,64]{2,1,0:T(8,128)}, f32[16,64,64]{2,1,0:T(8,128)S(1)}, u32[]{:S(2)}) copy-start(f32[16,64,64]{2,1,0:T(8,128)S(1)} %fusion.218) | copy-start | bytes 786436 | tf_op jit(solution)/shard_map/while
  89.9 15.0 %collective-permute-start = (f32[1,4096]{1,0:T(1,128)S(1)}, f32[1,4096]{1,0:T(1,128)S(1)}, u32[]{:S(2)}, u32[]{:S(2)}) collective-permute-start(f32[1,4096]{1,0:T(1,128)S(1)} %slice.944), channel_id=1, source_target_pairs={{0,1},{1,2},{2,3},{3,4},{4,5},{5,6},{6,7},{7,8},{8,9},{9,10},{10,1... | collective-permute-start | bytes 49160 | tf_op jit(solution)/shard_map/while/body/eval_jaxpr/ppermute | solution.py:24
  91.9 14.3 %collective-permute-start.1 = (f32[1,4096]{1,0:T(1,128)S(1)}, f32[1,4096]{1,0:T(1,128)S(1)}, u32[]{:S(2)}, u32[]{:S(2)}) collective-permute-start(f32[1,4096]{1,0:T(1,128)S(1)} %slice.945), channel_id=1, source_target_pairs={{1,0},{2,1},{3,2},{4,3},{5,4},{6,5},{7,6},{8,7},{9,8},{10,9},{11,1... | collective-permute-start | bytes 49160 | tf_op jit(solution)/shard_map/while/body/eval_jaxpr/ppermute | solution.py:27
  96.6 3.6 %collective-permute-start.2 = (f32[1,1024]{1,0:T(1,128)S(1)}, f32[1,1024]{1,0:T(1,128)S(1)}, u32[]{:S(2)}, u32[]{:S(2)}) collective-permute-start(f32[1,1024]{1,0:T(1,128)S(1)} %select_n.349), channel_id=1, source_target_pairs={{0,16},{16,0},{1,17},{17,1},{2,18},{18,2},{3,19},{19,3},{4,20},{20... | collective-permute-start | bytes 12296 | tf_op jit(solution)/shard_map/while/body/eval_jaxpr/ppermute | solution.py:39
  114.7 17.2 %copy-start.14 = (f32[16,64,64]{2,1,0:T(8,128)}, f32[16,64,64]{2,1,0:T(8,128)S(1)}, u32[]{:S(2)}) copy-start(f32[16,64,64]{2,1,0:T(8,128)S(1)} %fusion.218) | copy-start | bytes 786436 | tf_op jit(solution)/shard_map/while
  114.8 15.0 %collective-permute-start = (f32[1,4096]{1,0:T(1,128)S(1)}, f32[1,4096]{1,0:T(1,128)S(1)}, u32[]{:S(2)}, u32[]{:S(2)}) collective-permute-start(f32[1,4096]{1,0:T(1,128)S(1)} %slice.944), channel_id=1, source_target_pairs={{0,1},{1,2},{2,3},{3,4},{4,5},{5,6},{6,7},{7,8},{8,9},{9,10},{10,1... | collective-permute-start | bytes 49160 | tf_op jit(solution)/shard_map/while/body/eval_jaxpr/ppermute | solution.py:24
  116.9 14.3 %collective-permute-start.1 = (f32[1,4096]{1,0:T(1,128)S(1)}, f32[1,4096]{1,0:T(1,128)S(1)}, u32[]{:S(2)}, u32[]{:S(2)}) collective-permute-start(f32[1,4096]{1,0:T(1,128)S(1)} %slice.945), channel_id=1, source_target_pairs={{1,0},{2,1},{3,2},{4,3},{5,4},{6,5},{7,6},{8,7},{9,8},{10,9},{11,1... | collective-permute-start | bytes 49160 | tf_op jit(solution)/shard_map/while/body/eval_jaxpr/ppermute | solution.py:27
  121.5 3.6 %collective-permute-start.2 = (f32[1,1024]{1,0:T(1,128)S(1)}, f32[1,1024]{1,0:T(1,128)S(1)}, u32[]{:S(2)}, u32[]{:S(2)}) collective-permute-start(f32[1,1024]{1,0:T(1,128)S(1)} %select_n.349), channel_id=1, source_target_pairs={{0,16},{16,0},{1,17},{17,1},{2,18},{18,2},{3,19},{19,3},{4,20},{20... | collective-permute-start | bytes 12296 | tf_op jit(solution)/shard_map/while/body/eval_jaxpr/ppermute | solution.py:39
  144.4 10.9 %collective-permute-start.9 = (f32[5,1024]{0,1:T(8,128)}, f32[5,1024]{0,1:T(8,128)}, u32[]{:S(2)}, u32[]{:S(2)}) collective-permute-start(f32[5,1024]{0,1:T(8,128)} %bitcast.297), channel_id=1, source_target_pairs={{0,16},{16,0},{1,17},{17,1},{2,18},{18,2},{3,19},{19,3},{4,20},{20... | collective-permute-start | bytes 61448 | tf_op jit(solution)/shard_map/ppermute | solution.py:39
  147.9 21.4 %collective-permute-start.10 = (f32[5,2,4096]{2,1,0:T(2,128)S(1)}, f32[5,2,4096]{2,1,0:T(2,128)}, u32[]{:S(2)}, u32[]{:S(2)}) collective-permute-start(f32[5,2,4096]{2,1,0:T(2,128)S(1)} %get-tuple-element.610), channel_id=1, source_target_pairs={{1,0},{2,1},{3,2},{4,3},{5,4},{6,5},{7,6},{8,7},{9,8},{10,9},{11,1... | collective-permute-start | bytes 491528 | tf_op jit(solution)/shard_map/ppermute | solution.py:27
  149.9 20.6 %collective-permute-start.11 = (f32[5,2,4096]{2,1,0:T(2,128)}, f32[5,2,4096]{2,1,0:T(2,128)}, u32[]{:S(2)}, u32[]{:S(2)}) collective-permute-start(f32[5,2,4096]{2,1,0:T(2,128)} %get-tuple-element.611), channel_id=1, source_target_pairs={{0,1},{1,2},{2,3},{3,4},{4,5},{5,6},{6,7},{7,8},{8,9},{9,10},{10,1... | collective-permute-start | bytes 491528 | tf_op jit(solution)/shard_map/ppermute | solution.py:24
  196.4 17.2 %copy-start.11 = (f32[16,64,64]{2,1,0:T(8,128)}, f32[16,64,64]{2,1,0:T(8,128)S(1)}, u32[]{:S(2)}) copy-start(f32[16,64,64]{2,1,0:T(8,128)S(1)} %fusion.237) | copy-start | bytes 786436 | tf_op jit(solution)/shard_map/while
  196.5 15.0 %collective-permute-start.3 = (f32[1,4096]{1,0:T(1,128)S(1)}, f32[1,4096]{1,0:T(1,128)S(1)}, u32[]{:S(2)}, u32[]{:S(2)}) collective-permute-start(f32[1,4096]{1,0:T(1,128)S(1)} %slice.954), channel_id=1, source_target_pairs={{0,1},{1,2},{2,3},{3,4},{4,5},{5,6},{6,7},{7,8},{8,9},{9,10},{10,1... | collective-permute-start | bytes 49160 | tf_op jit(solution)/shard_map/while/body/eval_jaxpr/ppermute | solution.py:24
  198.5 14.3 %collective-permute-start.4 = (f32[1,4096]{1,0:T(1,128)S(1)}, f32[1,4096]{1,0:T(1,128)S(1)}, u32[]{:S(2)}, u32[]{:S(2)}) collective-permute-start(f32[1,4096]{1,0:T(1,128)S(1)} %slice.955), channel_id=1, source_target_pairs={{1,0},{2,1},{3,2},{4,3},{5,4},{6,5},{7,6},{8,7},{9,8},{10,9},{11,1... | collective-permute-start | bytes 49160 | tf_op jit(solution)/shard_map/while/body/eval_jaxpr/ppermute | solution.py:27
  203.2 3.6 %collective-permute-start.5 = (f32[1,1024]{1,0:T(1,128)S(1)}, f32[1,1024]{1,0:T(1,128)S(1)}, u32[]{:S(2)}, u32[]{:S(2)}) collective-permute-start(f32[1,1024]{1,0:T(1,128)S(1)} %select_n.359), channel_id=1, source_target_pairs={{0,16},{16,0},{1,17},{17,1},{2,18},{18,2},{3,19},{19,3},{4,20},{20... | collective-permute-start | bytes 12296 | tf_op jit(solution)/shard_map/while/body/eval_jaxpr/ppermute | solution.py:39
  220.3 17.2 %copy-start.11 = (f32[16,64,64]{2,1,0:T(8,128)}, f32[16,64,64]{2,1,0:T(8,128)S(1)}, u32[]{:S(2)}) copy-start(f32[16,64,64]{2,1,0:T(8,128)S(1)} %fusion.237) | copy-start | bytes 786436 | tf_op jit(solution)/shard_map/while
  220.4 15.0 %collective-permute-start.3 = (f32[1,4096]{1,0:T(1,128)S(1)}, f32[1,4096]{1,0:T(1,128)S(1)}, u32[]{:S(2)}, u32[]{:S(2)}) collective-permute-start(f32[1,4096]{1,0:T(1,128)S(1)} %slice.954), channel_id=1, source_target_pairs={{0,1},{1,2},{2,3},{3,4},{4,5},{5,6},{6,7},{7,8},{8,9},{9,10},{10,1... | collective-permute-start | bytes 49160 | tf_op jit(solution)/shard_map/while/body/eval_jaxpr/ppermute | solution.py:24
  222.4 14.3 %collective-permute-start.4 = (f32[1,4096]{1,0:T(1,128)S(1)}, f32[1,4096]{1,0:T(1,128)S(1)}, u32[]{:S(2)}, u32[]{:S(2)}) collective-permute-start(f32[1,4096]{1,0:T(1,128)S(1)} %slice.955), channel_id=1, source_target_pairs={{1,0},{2,1},{3,2},{4,3},{5,4},{6,5},{7,6},{8,7},{9,8},{10,9},{11,1... | collective-permute-start | bytes 49160 | tf_op jit(solution)/shard_map/while/body/eval_jaxpr/ppermute | solution.py:27
  227.1 3.6 %collective-permute-start.5 = (f32[1,1024]{1,0:T(1,128)S(1)}, f32[1,1024]{1,0:T(1,128)S(1)}, u32[]{:S(2)}, u32[]{:S(2)}) collective-permute-start(f32[1,1024]{1,0:T(1,128)S(1)} %select_n.359), channel_id=1, source_target_pairs={{0,16},{16,0},{1,17},{17,1},{2,18},{18,2},{3,19},{19,3},{4,20},{20... | collective-permute-start | bytes 12296 | tf_op jit(solution)/shard_map/while/body/eval_jaxpr/ppermute | solution.py:39
  244.2 17.2 %copy-start.11 = (f32[16,64,64]{2,1,0:T(8,128)}, f32[16,64,64]{2,1,0:T(8,128)S(1)}, u32[]{:S(2)}) copy-start(f32[16,64,64]{2,1,0:T(8,128)S(1)} %fusion.237) | copy-start | bytes 786436 | tf_op jit(solution)/shard_map/while
  244.4 15.0 %collective-permute-start.3 = (f32[1,4096]{1,0:T(1,128)S(1)}, f32[1,4096]{1,0:T(1,128)S(1)}, u32[]{:S(2)}, u32[]{:S(2)}) collective-permute-start(f32[1,4096]{1,0:T(1,128)S(1)} %slice.954), channel_id=1, source_target_pairs={{0,1},{1,2},{2,3},{3,4},{4,5},{5,6},{6,7},{7,8},{8,9},{9,10},{10,1... | collective-permute-start | bytes 49160 | tf_op jit(solution)/shard_map/while/body/eval_jaxpr/ppermute | solution.py:24
  246.4 14.3 %collective-permute-start.4 = (f32[1,4096]{1,0:T(1,128)S(1)}, f32[1,4096]{1,0:T(1,128)S(1)}, u32[]{:S(2)}, u32[]{:S(2)}) collective-permute-start(f32[1,4096]{1,0:T(1,128)S(1)} %slice.955), channel_id=1, source_target_pairs={{1,0},{2,1},{3,2},{4,3},{5,4},{6,5},{7,6},{8,7},{9,8},{10,9},{11,1... | collective-permute-start | bytes 49160 | tf_op jit(solution)/shard_map/while/body/eval_jaxpr/ppermute | solution.py:27
  251.0 3.6 %collective-permute-start.5 = (f32[1,1024]{1,0:T(1,128)S(1)}, f32[1,1024]{1,0:T(1,128)S(1)}, u32[]{:S(2)}, u32[]{:S(2)}) collective-permute-start(f32[1,1024]{1,0:T(1,128)S(1)} %select_n.359), channel_id=1, source_target_pairs={{0,16},{16,0},{1,17},{17,1},{2,18},{18,2},{3,19},{19,3},{4,20},{20... | collective-permute-start | bytes 12296 | tf_op jit(solution)/shard_map/while/body/eval_jaxpr/ppermute | solution.py:39
  (20 other events, 72.0 us)
where the time goes:
time: 273 us; the launch traced here: 272 us
  local copies, waits for them, and re-layouts  100 us (37%)
  starting transfers between devices  61.7 us (23%)
  other arithmetic  55 us (20%)
  matrix products  36 us (13%)
  waiting for transfers between devices  16.7 us (6%)
    gather x8, local copies, waits for them, and re-layouts, place_ghost(): picked = jnp.take(received, mapping, axis=-1)  37.3 us
    ppermute x8, starting transfers between devices, with_halo(): lax.ppermute(lax.slice_in_dim(block, 0, width, axis=dim), axis, backward)  33.7 us
    ppermute x8, waiting for transfers between devices, from_partner(): return lax.ppermute(block, axis, route)  16.7 us
    ppermute x8, starting transfers between devices, with_halo(): lax.ppermute(lax.slice_in_dim(block, block.shape[dim] - width, None, axis...  15.8 us
    add x2, other arithmetic, tendency(): change = -COURANT * advection + DIFFUSION * laplace  12.8 us
    ppermute x8, starting transfers between devices, from_partner(): return lax.ppermute(block, axis, route)  12.2 us
    unnamed x44, local copies, waits for them, and re-layouts  9.34 us
    dot_general x6, matrix products, poisson_solve(): solved = jnp.einsum('ai,mkab->mkib', table_x, solved, precision=precise)  6.89 us
  transfers between devices with their start and end apart: 24, of which 8 were waited for; matrix products, arithmetic and copies ran while one was open for 31% of the time, Pallas kernels for 0%

commit v1 on v0

v1 whole, which is shorter than its diff:
```python
import functools
import math

import jax
import jax.numpy as jnp
import numpy as np
from jax import lax
from jax.experimental import pallas as pl
from jax.experimental.pallas import tpu as pltpu
from jax.sharding import PartitionSpec as P

NX = 64
NY = 64
FIELDS = 5
SECTIONS = 2
ITERS = 3

COURANT = 0.1
DIFFUSION = 0.05
STOICHIOMETRY = 2.0
EXPANSION = 1.0

LANES = 128
HALF = NY
TILES = NX // 2
ROWS = 32
ZERO_ROW = 8
F32 = jnp.float32
BF16 = jnp.bfloat16


def sine(n):
    i = np.arange(n, dtype=np.float64) + 1
    return np.sqrt(2.0 / (n + 1)) * np.sin(np.pi * i[:, None] * i[None, :] / (n + 1))


def modes(n):
    i = np.arange(n, dtype=np.float64) + 1
    return 2.0 - 2.0 * np.cos(np.pi * i / (n + 1))


def both(low, high):
    return np.concatenate([np.broadcast_to(low, low.shape[:-1] + (HALF,)), np.broadcast_to(high, high.shape[:-1] + (HALF,))], axis=-1)


def split(table):
    table = np.asarray(table, np.float32)
    high = table.astype(BF16)
    low = (table - high.astype(np.float32)).astype(BF16)
    return high, low


def tables(height):
    sz, sx, sy = sine(height), sine(NX), sine(NY)
    lz, lx, ly = modes(height), modes(NX), modes(NY)
    half = height // 2
    coef = both(sz[0::2, :half, None], sz[1::2, :half, None])
    edge = coef[:, 0]
    lam = lx[None, :, None] + both(lz[0::2, None, None], lz[1::2, None, None]) + np.concatenate([ly, ly])[None, None, :]
    inv = 1.0 / lam
    cross = edge[:, None, :] * sx[:, 0][None, :, None] * inv
    diag_z = (edge[:, None, :] ** 2 * inv).sum(0)
    diag_x = (sx[:, 0][None, :, None] ** 2 * inv).sum(1)
    order = np.concatenate([np.arange(0, NX, 2), np.arange(1, NX, 2)])
    fwd_hi, fwd_lo = split(sx[:, order])
    bwd_hi, bwd_lo = split(sx[order, :])
    ky = np.kron(np.eye(2), sy)
    ky_hi, ky_lo = split(ky)
    to_a = np.zeros((half, half, LANES))
    to_b = np.zeros((half, half, LANES))
    from_a = np.zeros((half, half, LANES))
    from_b = np.zeros((half, half, LANES))
    for r in range(half):
        to_a[r] = both(sz[0::2, r][:, None], sz[1::2, half + r][:, None])
        to_b[r] = both(sz[0::2, half + r][:, None], sz[1::2, r][:, None])
        from_a[r] = both(sz[2 * r, :half][:, None], sz[2 * r + 1, half:][:, None])
        from_b[r] = both(sz[2 * r + 1, :half][:, None], sz[2 * r, half:][:, None])
    f = lambda a: np.ascontiguousarray(a, dtype=np.float32)
    return dict(
        coef=f(coef.reshape(half * half, LANES)),
        inv=f(inv),
        cross=f(cross),
        diag_z=f(diag_z),
        diag_x=f(diag_x),
        col_x=f(np.broadcast_to(sx[:, :1], (NX, LANES))),
        edge=f(edge),
        fwd=np.concatenate([fwd_hi, fwd_hi, fwd_lo], axis=1),
        bwd=np.concatenate([bwd_hi, bwd_hi, bwd_lo], axis=1),
        ky2=np.concatenate([ky_hi, ky_hi], axis=0),
        ky_lo=ky_lo,
        plane=f(np.stack([to_a, to_b, from_a, from_b])),
    )


def lower_half(shape):
    return lax.broadcasted_iota(jnp.int32, shape, len(shape) - 1) < HALF


def swap_halves(v):
    return pltpu.roll(v, HALF, axis=v.ndim - 1)


def hi_lo(v):
    high = v.astype(BF16)
    return high, (v - high.astype(F32)).astype(BF16)


def y_transform(v, ky2, ky_lo):
    high, low = hi_lo(v)
    return jnp.dot(jnp.concatenate([high, low], axis=1), ky2[...], preferred_element_type=F32) + jnp.dot(
        high, ky_lo[...], preferred_element_type=F32
    )


def x_transform(table, v):
    high, low = hi_lo(v)
    return jnp.dot(table[...], jnp.concatenate([high, low, high], axis=0), preferred_element_type=F32)


def mix_rows(v, a, b):
    swapped = swap_halves(v)
    out = jnp.zeros_like(v)
    for r in range(v.shape[0]):
        out = out + a[r] * v[r : r + 1] + b[r] * swapped[r : r + 1]
    return out


def gather(plane, mapping):
    half = plane.shape[0]
    bits = int(math.log2(half))
    ybits = int(math.log2(NY))
    row = (mapping >> ybits) & (half - 1)
    lane = ((mapping >> (ybits + bits)) << ybits) | (mapping & (NY - 1))
    out = jnp.zeros_like(plane)
    for r in range(half):
        source = jnp.broadcast_to(plane[r : r + 1], plane.shape)
        out = jnp.where(row == r, jnp.take_along_axis(source, lane, axis=1), out)
    return out


def position():
    is_fine = lax.axis_index("grp") == 0
    even = lax.rem(lax.axis_index("mesh"), 2) == 0
    return is_fine, even


def row_sign(is_fine, shape):
    odd = lax.rem(lax.broadcasted_iota(jnp.int32, shape, 0), 2) == 1
    return jnp.where(jnp.logical_and(odd, is_fine), -1.0, 1.0).astype(F32)


def pack_trace(full):
    n = full.shape[0] // 2
    return jnp.where(lower_half((n, LANES)), full[:n], full[n:])


def unpack_trace(packed):
    swapped = swap_halves(packed)
    low = lower_half(packed.shape)
    return jnp.concatenate([jnp.where(low, packed, swapped), jnp.where(low, swapped, packed)], axis=0)


def send_traces(u, even, to_even, to_odd):
    other = swap_halves(u)
    low = lower_half(u.shape)
    evens = jnp.where(low, u, other)
    odds = jnp.where(low, other, u)
    sign = jnp.where(even, 1.0, -1.0).astype(F32)
    to_even[...] = pack_trace(evens - sign * odds)
    to_odd[...] = pack_trace(evens + sign * odds)


def ghost_low_high(from_even, from_odd, even):
    a, b = unpack_trace(from_even[...]), unpack_trace(from_odd[...])
    return jnp.where(even, b, a), jnp.where(even, a, b)


def send_plane(y, tab, plane_out):
    cells = mix_rows(y_transform(y, tab["ky2"], tab["ky_lo"]), tab["plane"].at[2], tab["plane"].at[3])
    plane_out[...] = cells


def x_ghost_tiles(ghost, is_fine):
    swapped = swap_halves(ghost)
    west = jnp.concatenate([swapped, ghost], axis=0)
    east = jnp.concatenate([ghost, swapped], axis=0)
    zero = jnp.zeros_like(west)
    return jnp.where(is_fine, zero, west), jnp.where(is_fine, east, zero)


def east_west(centre, before, after, low):
    east = swap_halves(jnp.where(low, after, centre))
    west = swap_halves(jnp.where(low, centre, before))
    return east, west


def north_south(centre):
    y = lax.broadcasted_iota(jnp.int32, centre.shape, 1) & (NY - 1)
    north = jnp.where(y == NY - 1, 0.0, pltpu.roll(centre, LANES - 1, axis=1))
    south = jnp.where(y == 0, 0.0, pltpu.roll(centre, 1, axis=1))
    return north, south


def strided(first, count, stride):
    return pl.ds(first, count, stride=stride)


def pack_kernel(height, state, to_even, to_odd, planes):
    is_fine, even = position()
    half = height // 2
    low = lower_half((half, LANES))
    for f in range(FIELDS):
        first = state[f, :, 0:LANES]
        last = state[f, :, (TILES - 1) * LANES : TILES * LANES]
        fine = jnp.where(low, swap_halves(last[:half]), last[half:])
        coarse = jnp.where(low, first[:half], swap_halves(first[half:]))
        planes[f * half : (f + 1) * half] = jnp.where(is_fine, fine, coarse)

    def tile(t, _):
        lanes = pl.ds(pl.multiple_of(t * LANES, LANES), LANES)
        for f in range(FIELDS):
            value = state[f, :, lanes]
            for k in range(2):
                bottom = value[k : k + 1]
                top = value[height - 2 + k : height - 1 + k]
                row = pl.ds((2 * f + k) * TILES + t, 1)
                to_even[row] = jnp.where(even, top, bottom)
                to_odd[row] = jnp.where(even, bottom, top)
        return 0

    lax.fori_loop(0, TILES, tile, 0)


NAMES_SOLVE = ("coef", "inv", "edge", "col_x", "fwd", "ky2", "ky_lo", "plane")


def begin_kernel(height, second, *refs):
    refs = list(refs)
    take = lambda n: [refs.pop(0) for _ in range(n)]
    current, burn, from_even, from_odd, planes, mapping = take(6)
    initial = take(1)[0] if second else None
    tab = dict(zip(NAMES_SOLVE, take(len(NAMES_SOLVE))))
    predicted, spectrum, trace, facet, to_even, to_odd, plane_out = take(7)
    pad, source, folded, mixed = take(4)
    is_fine, even = position()
    half = height // 2
    tile_low = lower_half((height, LANES))

    for f in range(FIELDS):
        ghost = gather(planes[f * half : (f + 1) * half], mapping[...])
        west, east = x_ghost_tiles(ghost, is_fine)
        pad[f, ZERO_ROW : ZERO_ROW + height] = west
        last = (TILES + 1) * ROWS + ZERO_ROW
        pad[f, last : last + height] = east
        for k in range(2):
            rows = slice((2 * f + k) * TILES, (2 * f + k + 1) * TILES)
            below = jnp.where(even, from_odd[rows], from_even[rows])
            above = jnp.where(even, from_even[rows], from_odd[rows])
            pad[f, strided(ROWS + ZERO_ROW - 2 + k, TILES, ROWS)] = below
            pad[f, strided(ROWS + ZERO_ROW + height + k, TILES, ROWS)] = above

    def copy(t, _):
        lanes = pl.ds(pl.multiple_of(t * LANES, LANES), LANES)
        row = pl.multiple_of((t + 1) * ROWS + ZERO_ROW, 8)
        for f in range(FIELDS):
            pad[f, pl.ds(row, height)] = current[f, :, lanes]
        return 0

    lax.fori_loop(0, TILES, copy, 0)

    def tile(t, _):
        lanes = pl.ds(pl.multiple_of(t * LANES, LANES), LANES)
        base = pl.multiple_of((t + 1) * ROWS, ROWS)

        def at(f, dz=0, dt=0):
            window = pad[f, pl.ds(pl.multiple_of(base + dt * ROWS, ROWS), ROWS)]
            return window[ZERO_ROW + dz : ZERO_ROW + dz + height]

        u, v, w = at(0), at(1), at(2)
        fuel, oxygen = at(3), at(4)
        reaction = burn[:, lanes] * fuel * oxygen
        cu = u * (-0.5 * COURANT)
        cv = v * (-0.5 * COURANT)
        cw = w * (-COURANT / 12.0)
        divergence = None
        for f in range(FIELDS):
            centre = (u, v, w, fuel, oxygen)[f]
            east, west = east_west(centre, at(f, 0, -1), at(f, 0, 1), tile_low)
            north, south = north_south(centre)
            above, below = at(f, 1), at(f, -1)
            above_two, below_two = at(f, 2), at(f, -2)
            dx, dy, dz = east - west, north - south, above - below
            change = cu * dx + cv * dy + cw * (8.0 * dz - (above_two - below_two))
            change = change + DIFFUSION * ((east + west) + (north + south) + (above + below) - 6.0 * centre)
            if f == 3:
                change = change - reaction
            if f == 4:
                change = change - STOICHIOMETRY * reaction
            if f == 0:
                divergence = dx
            if f == 1:
                divergence = divergence + dy
            if f == 2:
                divergence = divergence + dz
            if second:
                predicted[f, :, lanes] = 0.5 * (initial[f, :, lanes] + centre + change)
            else:
                predicted[f, :, lanes] = centre + change
        source[pl.ds(pl.multiple_of(t * height, height), height)] = EXPANSION * reaction - 0.5 * divergence
        return 0

    lax.fori_loop(0, TILES, tile, 0)

    low = lower_half((TILES, LANES))
    for q in range(half):
        a = source[strided(q, TILES, height)]
        b = source[strided(height - 1 - q, TILES, height)]
        total, delta = a + b, a - b
        folded[q, 0:TILES] = jnp.where(low, total, swap_halves(delta))
        folded[q, TILES : 2 * TILES] = jnp.where(low, swap_halves(total), delta)

    z_mix(folded, mixed, tab["coef"], half, False)
    wide = jnp.concatenate([mixed[p] for p in range(half)], axis=1)
    wide = x_transform(tab["fwd"], wide)
    tall = jnp.concatenate([wide[:, p * LANES : (p + 1) * LANES] for p in range(half)], axis=0)
    mixed[...] = y_transform(tall, tab["ky2"], tab["ky_lo"]).reshape(half, NX, LANES)

    sign = row_sign(is_fine, (NX, LANES))
    column = tab["col_x"][...] * sign
    u0 = jnp.zeros((NX, LANES), F32)
    for p in range(half):
        solved = mixed[p] * tab["inv"][p]
        spectrum[p] = solved
        u0 = u0 + tab["edge"][p : p + 1] * solved
        facet[p : p + 1] = jnp.sum(column * solved, axis=0, keepdims=True)
    trace[...] = u0
    send_traces(u0, even, to_even, to_odd)
    send_plane(facet[...], tab, plane_out)


def z_mix(src, dst, coef, half, inverse):
    def chunk(r, _):
        rows = pl.ds(pl.multiple_of(r * 8, 8), 8)
        parts = [src[j, rows] for j in range(half)]
        for i in range(half):
            total = None
            for j in range(half):
                k = j * half + i if inverse else i * half + j
                term = coef[k : k + 1] * parts[j]
                total = term if total is None else total + term
            dst[i, rows] = total
        return 0

    lax.fori_loop(0, NX // 8, chunk, 0)


NAMES_STEP = ("cross", "diag_z", "diag_x", "ky2", "ky_lo", "plane")


def ghost_modes(plane, mapping, tab):
    cells = gather(plane[...], mapping[...])
    return y_transform(mix_rows(cells, tab["plane"].at[0], tab["plane"].at[1]), tab["ky2"], tab["ky_lo"])


def step_kernel(height, *refs):
    refs = list(refs)
    take = lambda n: [refs.pop(0) for _ in range(n)]
    from_even, from_odd, plane_in, mapping, trace, facet = take(6)
    tab = dict(zip(NAMES_STEP, take(len(NAMES_STEP))))
    layers_out, side_out, to_even, to_odd, plane_out = take(5)
    (facet_next,) = take(1)
    is_fine, even = position()
    half = height // 2
    low_ghost, high_ghost = ghost_low_high(from_even, from_odd, even)
    layers = jnp.where(lower_half((NX, LANES)), low_ghost + high_ghost, low_ghost - high_ghost)
    side = ghost_modes(plane_in, mapping, tab)
    layers_out[...] = layers
    side_out[...] = side
    sign = row_sign(is_fine, (NX, LANES))
    signed = sign * layers
    cross_sum = jnp.zeros((NX, LANES), F32)
    for p in range(half):
        cross = tab["cross"][p]
        cross_sum = cross_sum + cross * side[p : p + 1]
        facet_next[p : p + 1] = jnp.sum(cross * signed, axis=0, keepdims=True)
    u = trace[...] + tab["diag_z"][...] * layers + sign * cross_sum
    send_traces(u, even, to_even, to_odd)
    send_plane(facet[...] + tab["diag_x"][...] * side + facet_next[...], tab, plane_out)


NAMES_END = ("coef", "inv", "edge", "col_x", "bwd", "ky2", "ky_lo")


def end_kernel(height, final, *refs):
    refs = list(refs)
    take = lambda n: [refs.pop(0) for _ in range(n)]
    from_even, from_odd, plane_in, mapping, spectrum, layers, side, predicted = take(8)
    tab = dict(zip(NAMES_END, take(len(NAMES_END))))
    state = take(1)[0]
    if final:
        (head,) = take(1)
    else:
        to_even, to_odd, planes = take(3)
    tall, mixed, unmixed, pad = take(4)
    is_fine, even = position()
    half = height // 2
    sign = row_sign(is_fine, (NX, LANES))
    column = tab["col_x"][...] * sign
    for p in range(half):
        push = tab["edge"][p : p + 1] * layers[...] + column * side[p : p + 1]
        tall[p * NX : (p + 1) * NX] = spectrum[p] + push * tab["inv"][p]
    low_ghost, high_ghost = ghost_low_high(from_even, from_odd, even)
    tall[half * NX : (half + 1) * NX] = jnp.where(lower_half((NX, LANES)), low_ghost, high_ghost)

    cells = y_transform(tall[...], tab["ky2"], tab["ky_lo"])
    wide = jnp.concatenate([cells[p * NX : (p + 1) * NX] for p in range(half + 1)], axis=1)
    wide = x_transform(tab["bwd"], wide)
    for p in range(half):
        mixed[p] = wide[:, p * LANES : (p + 1) * LANES]
    z_mix(mixed, unmixed, tab["coef"], half, True)

    low = lower_half((TILES, LANES))

    def unfold(v):
        top, bottom = v[:TILES], v[TILES:]
        return jnp.where(low, top, swap_halves(bottom)), jnp.where(low, swap_halves(top), bottom)

    first = ROWS + ZERO_ROW
    below, above = unfold(wide[:, half * LANES : (half + 1) * LANES])
    pad[strided(first - 1, TILES, ROWS)] = below
    pad[strided(first + height, TILES, ROWS)] = above
    for q in range(half):
        evens, odds = unfold(unmixed[q])
        pad[strided(first + q, TILES, ROWS)] = evens + odds
        pad[strided(first + height - 1 - q, TILES, ROWS)] = evens - odds
    west, east = x_ghost_tiles(gather(plane_in[...], mapping[...]), is_fine)
    pad[ZERO_ROW : ZERO_ROW + height] = west
    last = (TILES + 1) * ROWS + ZERO_ROW
    pad[last : last + height] = east

    tile_low = lower_half((height, LANES))

    def tile(t, _):
        lanes = pl.ds(pl.multiple_of(t * LANES, LANES), LANES)
        base = pl.multiple_of((t + 1) * ROWS, ROWS)

        def at(dz=0, dt=0):
            window = pad[pl.ds(pl.multiple_of(base + dt * ROWS, ROWS), ROWS)]
            return window[ZERO_ROW + dz : ZERO_ROW + dz + height]

        centre = at()
        east, west = east_west(centre, at(0, -1), at(0, 1), tile_low)
        north, south = north_south(centre)
        slopes = (east - west, north - south, at(1) - at(-1))
        for f in range(FIELDS):
            value = predicted[f, :, lanes]
            if f < 3:
                value = value - 0.5 * slopes[f]
            state[f, :, lanes] = value
            if not final:
                for k in range(2):
                    bottom = value[k : k + 1]
                    top = value[height - 2 + k : height - 1 + k]
                    row = pl.ds((2 * f + k) * TILES + t, 1)
                    to_even[row] = jnp.where(even, top, bottom)
                    to_odd[row] = jnp.where(even, bottom, top)
        if final:
            head[:, lanes] = centre
        return 0

    lax.fori_loop(0, TILES, tile, 0)
    if not final:
        half_low = lower_half((half, LANES))
        for f in range(FIELDS):
            first = state[f, :, 0:LANES]
            last = state[f, :, (TILES - 1) * LANES : TILES * LANES]
            fine = jnp.where(half_low, swap_halves(last[:half]), last[half:])
            coarse = jnp.where(half_low, first[:half], swap_halves(first[half:]))
            planes[f * half : (f + 1) * half] = jnp.where(is_fine, fine, coarse)


def swap_pairs(x, parity):
    count = lax.axis_size("mesh")
    route = []
    for low in range(parity, count - 1, 2):
        route += [(low, low + 1), (low + 1, low)]
    return lax.ppermute(x, "mesh", route)


def swap_partner(x):
    return lax.ppermute(x, "grp", [(0, 1), (1, 0)])


def exchange(to_even, to_odd, plane):
    return swap_pairs(to_even, 0), swap_pairs(to_odd, 1), swap_partner(plane)


def shards(state, burn_rate, face_map):
    height = state.shape[2]
    half = height // 2
    cells = NX * NY
    tab = {name: jnp.asarray(value) for name, value in tables(height).items()}
    shape = lambda *s: jax.ShapeDtypeStruct(s, F32)
    halo = shape(2 * FIELDS * TILES, LANES)
    trace_packed = shape(NX // 2, LANES)
    plane = shape(half, LANES)
    initial = state[0]
    burning = burn_rate[0]
    by_row = face_map[0, 0].reshape(height, NY)
    mapping = jnp.concatenate([by_row[:half], by_row[half:]], axis=1)

    to_even, to_odd, planes = pl.pallas_call(
        functools.partial(pack_kernel, height),
        out_shape=(halo, halo, shape(FIELDS * half, LANES)),
        name="pack",
    )(initial)
    current = initial
    for section in range(SECTIONS):
        second = section > 0
        final = section == SECTIONS - 1
        from_even, from_odd, planes_in = exchange(to_even, to_odd, planes)
        args = (current, burning, from_even, from_odd, planes_in, mapping) + ((initial,) if second else ())
        predicted, spectrum, trace, facet, to_even, to_odd, plane_out = pl.pallas_call(
            functools.partial(begin_kernel, height, second),
            out_shape=(
                shape(FIELDS, height, cells),
                shape(half, NX, LANES),
                shape(NX, LANES),
                plane,
                trace_packed,
                trace_packed,
                plane,
            ),
            scratch_shapes=[
                pltpu.VMEM((FIELDS, (TILES + 2) * ROWS, LANES), F32),
                pltpu.VMEM((TILES * height, LANES), F32),
                pltpu.VMEM((half, NX, LANES), F32),
                pltpu.VMEM((half, NX, LANES), F32),
            ],
            name="begin",
        )(*args, *(tab[n] for n in NAMES_SOLVE))
        for _ in range(ITERS - 1):
            received = exchange(to_even, to_odd, plane_out)
            layers, side, to_even, to_odd, plane_out = pl.pallas_call(
                functools.partial(step_kernel, height),
                out_shape=(shape(NX, LANES), plane, trace_packed, trace_packed, plane),
                scratch_shapes=[pltpu.VMEM((half, LANES), F32)],
                name="step",
            )(*received, mapping, trace, facet, *(tab[n] for n in NAMES_STEP))
        received = exchange(to_even, to_odd, plane_out)
        outs = pl.pallas_call(
            functools.partial(end_kernel, height, final),
            out_shape=(shape(FIELDS, height, cells),)
            + ((shape(height, cells),) if final else (halo, halo, shape(FIELDS * half, LANES))),
            scratch_shapes=[
                pltpu.VMEM(((half + 1) * NX, LANES), F32),
                pltpu.VMEM((half, NX, LANES), F32),
                pltpu.VMEM((half, NX, LANES), F32),
                pltpu.VMEM(((TILES + 2) * ROWS, LANES), F32),
            ],
            name="end",
        )(*received, mapping, spectrum, layers, side, predicted, *(tab[n] for n in NAMES_END))
        current = outs[0]
        if not final:
            to_even, to_odd, planes = outs[1:]
    return current[None], outs[1][None]


def solution(mesh):
    placed = (P("grp", None, "mesh", None), P("grp", "mesh", None), P("grp", "mesh", None))
    return jax.shard_map(
        shards,
        mesh=mesh,
        in_specs=placed,
        out_specs=(P("grp", None, "mesh", None), P("grp", "mesh", None)),
        check_vma=False,
    )
```

time: 273 us -> 107 us (0.39)
  local copies, waits for them, and re-layouts: 100 us -> 6.29 us
  other arithmetic: 55 us -> 0.67 us
  Pallas kernels: 0 us -> 40 us
  matrix products: 36 us -> 0 us
  starting transfers between devices: 61.7 us -> 31 us
  waiting for transfers between devices: 16.7 us -> 28.2 us
    pallas_call x0 -> x9, Pallas kernels: none -> 40 us  [the longest x2 16.3 us: shards(): pl.pallas_call(functools.partial(begin_kernel, height, second), out_shape...]
    gather x8 -> x0, local copies, waits for them, and re-layouts: 37.3 us -> none  [place_ghost(): picked = jnp.take(received, mapping, axis=-1)]
    dot_general x36 -> x0, matrix products: 36 us -> none  [the longest x6 6.89 us: poisson_solve(): solved = jnp.einsum('ai,mkab->mkib', table_x, solved, precision=precise)]
    ppermute x24, starting transfers between devices: 61.7 us -> 31 us  [the longest x16 25.4 us: swap_pairs(): return lax.ppermute(x, 'mesh', route)]
    add x33 -> x0, other arithmetic: 14.4 us -> none  [the longest x2 12.8 us: tendency(): change = -COURANT * advection + DIFFUSION * laplace]
    sub x16 -> x0, other arithmetic: 11.8 us -> none  [the longest x1 4.29 us: tendency(): grad_x = 0.5 * (east - west)]
    ppermute x24, waiting for transfers between devices: 16.7 us -> 28.2 us  [the longest x8 23.4 us: swap_partner(): return lax.ppermute(x, 'grp', [(0, 1), (1, 0)])]
    select_n x24 -> x0, local copies, waits for them, and re-layouts: 9.04 us -> none  [the longest x8 3.56 us: place_ghost(): jnp.where(is_fine, zeros, picked)]
  transfers between devices with their start and end apart: 24 -> 24, of which waited for: 8 -> 9; matrix products, arithmetic and copies ran while one was open for 31% -> 1% of each run, Pallas kernels for 0% -> 0%
where the time goes in v1:
time: 107 us
  Pallas kernels  40 us (37%)
  starting transfers between devices  31 us (29%)
  waiting for transfers between devices  28.2 us (26%)
  local copies, waits for them, and re-layouts  6.29 us (6%)
    ppermute x16, starting transfers between devices, swap_pairs(): return lax.ppermute(x, 'mesh', route)  25.4 us
    ppermute x8, waiting for transfers between devices, swap_partner(): return lax.ppermute(x, 'grp', [(0, 1), (1, 0)])  23.4 us
    pallas_call x2, Pallas kernels, shards(): pl.pallas_call(functools.partial(begin_kernel, height, second), out_shape...  16.3 us
    pallas_call x2, Pallas kernels, shards(): pl.pallas_call(functools.partial(end_kernel, height, final), out_shape=(s...  12.4 us
    pallas_call x4, Pallas kernels, shards(): pl.pallas_call(functools.partial(step_kernel, height), out_shape=(shape(N...  8.84 us
    unnamed x50, local copies, waits for them, and re-layouts  6.12 us
    ppermute x8, starting transfers between devices, swap_partner(): return lax.ppermute(x, 'grp', [(0, 1), (1, 0)])  5.52 us
    ppermute x16, waiting for transfers between devices, swap_pairs(): return lax.ppermute(x, 'mesh', route)  4.84 us
  transfers between devices with their start and end apart: 24, of which 9 were waited for; matrix products, arithmetic and copies ran while one was open for 1% of the time, Pallas kernels for 0%

profile of v1, /device:TPU:24, one launch (start us, length us, event | category | flops | bytes accessed | tf_op | source)
XLA Modules:
  0.0 106.9 jit_solution(15903714404822980888)
XLA Ops:
  0.6 2.5 %pack.1 = (f32[320,128]{1,0:T(8,128)}, f32[320,128]{1,0:T(8,128)}, f32[40,128]{1,0:T(8,128)}) custom-call(f32[5,16,4096]{2,1,0:T(8,128)} %bitcast.4), custom_call_target="tpu_custom_call" | custom-call | tf_op jit(solution)/shard_map/pack/pallas_call | solution.py:512
  3.1 1.5 %collective-permute-start.2 = (f32[40,128]{1,0:T(8,128)}, f32[40,128]{1,0:T(8,128)S(1)}, u32[]{:S(2)}, u32[]{:S(2)}) collective-permute-start(f32[40,128]{1,0:T(8,128)} %get-tuple-element.43), channel_id=1, source_target_pairs={{0,16},{16,0},{1,17},{17,1},{2,18},{18,2},{3,19},{19,3},{4,20},{20... | collective-permute-start | bytes 61448 | tf_op jit(solution)/shard_map/ppermute | solution.py:491
  4.6 3.4 %collective-permute-start.1 = (f32[320,128]{1,0:T(8,128)}, f32[320,128]{1,0:T(8,128)S(1)}, u32[]{:S(2)}, u32[]{:S(2)}) collective-permute-start(f32[320,128]{1,0:T(8,128)} %get-tuple-element.42), channel_id=1, source_target_pairs={{1,2},{2,1},{3,4},{4,3},{5,6},{6,5},{7,8},{8,7},{9,10},{10,9},{11,... | collective-permute-start | bytes 491528 | tf_op jit(solution)/shard_map/ppermute | solution.py:487
  8.2 0.7 pad_add_fusion.refs_5_.refs_3_
  8.9 3.6 %collective-permute-done.1.refs_3_ = f32[320,128]{1,0:T(8,128)S(1)} collective-permute-done((f32[320,128]{1,0:T(8,128)}, f32[320,128]{1,0:T(8,128)S(1)}, u32[]{:S(2)}, u32[]{:S(2)}) %collective-permute-start.1) | collective-permute-done | bytes 163872 | tf_op jit(solution)/shard_map/ppermute | solution.py:487
  12.5 0.7 copy-done.1
  13.1 7.9 %begin.2 = (f32[5,16,4096]{2,1,0:T(8,128)}, f32[8,64,128]{2,1,0:T(8,128)}, f32[64,128]{1,0:T(8,128)}, f32[8,128]{1,0:T(8,128)}, f32[32,128]{1,0:T(8,128)}, /*index=5*/f32[32,128]{1,0:T(8,128)}, f32[8,128]{1,0:T(8,128)}) custom-call(f32[5,16,4096]{2,1,0:T(8,128)} %bitcast.5, f32[16,4096]{1,0:T(8,128)} %bitcast.7, f32[320,128]{1,0:T(8,128)} %copy-done, ...), custom_call_target="tpu_custom_call" | custom-call | tf_op jit(solution)/shard_map/begin/pallas_call | solution.py:523
  21.0 1.3 %collective-permute-start.3 = (f32[32,128]{1,0:T(8,128)}, f32[32,128]{1,0:T(8,128)S(1)}, u32[]{:S(2)}, u32[]{:S(2)}) collective-permute-start(f32[32,128]{1,0:T(8,128)} %get-tuple-element.44), channel_id=1, source_target_pairs={{0,1},{1,0},{2,3},{3,2},{4,5},{5,4},{6,7},{7,6},{8,9},{9,8},{10,11... | collective-permute-start | bytes 49160 | tf_op jit(solution)/shard_map/ppermute | solution.py:487
  22.3 2.9 %collective-permute-start.4 = (f32[32,128]{1,0:T(8,128)}, f32[32,128]{1,0:T(8,128)S(1)}, u32[]{:S(2)}, u32[]{:S(2)}) collective-permute-start(f32[32,128]{1,0:T(8,128)} %get-tuple-element.45), channel_id=1, source_target_pairs={{1,2},{2,1},{3,4},{4,3},{5,6},{6,5},{7,8},{8,7},{9,10},{10,9},{11,... | collective-permute-start | bytes 49160 | tf_op jit(solution)/shard_map/ppermute | solution.py:487
  25.8 3.3 %collective-permute-done.5.refs_2_ = f32[8,128]{1,0:T(8,128)S(1)} collective-permute-done((f32[8,128]{1,0:T(8,128)}, f32[8,128]{1,0:T(8,128)S(1)}, u32[]{:S(2)}, u32[]{:S(2)}) %collective-permute-start.5) | collective-permute-done | bytes 4128 | tf_op jit(solution)/shard_map/ppermute | solution.py:491
  29.7 2.2 %step.4 = (f32[64,128]{1,0:T(8,128)}, f32[8,128]{1,0:T(8,128)}, f32[32,128]{1,0:T(8,128)}, f32[32,128]{1,0:T(8,128)}, f32[8,128]{1,0:T(8,128)}) custom-call(f32[32,128]{1,0:T(8,128)} %copy-done.13, f32[32,128]{1,0:T(8,128)} %copy-done.16, f32[8,128]{1,0:T(8,128)} %copy-done.22, s32[8,128]{1,0:T(8,128)} %pad_add_fusion.refs_5_.refs_3_, ...), custom_call_target="tpu_custom_call" | custom-call | tf_op jit(solution)/shard_map/step/pallas_call | solution.py:544
  31.9 2.6 %collective-permute-start.7 = (f32[32,128]{1,0:T(8,128)}, f32[32,128]{1,0:T(8,128)S(1)}, u32[]{:S(2)}, u32[]{:S(2)}) collective-permute-start(f32[32,128]{1,0:T(8,128)} %get-tuple-element.50), channel_id=1, source_target_pairs={{1,2},{2,1},{3,4},{4,3},{5,6},{6,5},{7,8},{8,7},{9,10},{10,9},{11,... | collective-permute-start | bytes 49160 | tf_op jit(solution)/shard_map/ppermute | solution.py:487
  35.1 3.3 %collective-permute-done.8.refs_2_ = f32[8,128]{1,0:T(8,128)S(1)} collective-permute-done((f32[8,128]{1,0:T(8,128)}, f32[8,128]{1,0:T(8,128)S(1)}, u32[]{:S(2)}, u32[]{:S(2)}) %collective-permute-start.8) | collective-permute-done | bytes 4128 | tf_op jit(solution)/shard_map/ppermute | solution.py:491
  39.6 2.2 %step.5 = (f32[64,128]{1,0:T(8,128)}, f32[8,128]{1,0:T(8,128)}, f32[32,128]{1,0:T(8,128)}, f32[32,128]{1,0:T(8,128)}, f32[8,128]{1,0:T(8,128)}) custom-call(f32[32,128]{1,0:T(8,128)} %copy-done.12, f32[32,128]{1,0:T(8,128)} %copy-done.14, f32[8,128]{1,0:T(8,128)} %copy-done.21, s32[8,128]{1,0:T(8,128)} %pad_add_fusion.refs_5_.refs_3_, ...), custom_call_target="tpu_custom_call" | custom-call | tf_op jit(solution)/shard_map/step/pallas_call | solution.py:544
  41.8 3.4 %collective-permute-start.10 = (f32[32,128]{1,0:T(8,128)}, f32[32,128]{1,0:T(8,128)S(1)}, u32[]{:S(2)}, u32[]{:S(2)}) collective-permute-start(f32[32,128]{1,0:T(8,128)} %get-tuple-element.53), channel_id=1, source_target_pairs={{1,2},{2,1},{3,4},{4,3},{5,6},{6,5},{7,8},{8,7},{9,10},{10,9},{11,... | collective-permute-start | bytes 49160 | tf_op jit(solution)/shard_map/ppermute | solution.py:487
  45.7 3.3 %collective-permute-done.11.refs_2_ = f32[8,128]{1,0:T(8,128)S(1)} collective-permute-done((f32[8,128]{1,0:T(8,128)}, f32[8,128]{1,0:T(8,128)S(1)}, u32[]{:S(2)}, u32[]{:S(2)}) %collective-permute-start.11) | collective-permute-done | bytes 4128 | tf_op jit(solution)/shard_map/ppermute | solution.py:491
  49.7 6.3 %end.2 = (f32[5,16,4096]{2,1,0:T(8,128)}, f32[320,128]{1,0:T(8,128)}, f32[320,128]{1,0:T(8,128)}, f32[40,128]{1,0:T(8,128)}) custom-call(f32[32,128]{1,0:T(8,128)} %copy-done.8, f32[32,128]{1,0:T(8,128)} %copy-done.9, f32[8,128]{1,0:T(8,128)} %copy-done.20, s32[8,128]{1,0:T(8,128)} %pad_add_fusion.refs_5_.refs_3_, f32[8,64,128]{2,1,0:T(8,128)} %get-tuple-element.55.refs_4_, ...), custom_call_target="tpu_custom_call" | custom-call | tf_op jit(solution)/shard_map/end/pallas_call | solution.py:551
  56.0 2.6 %collective-permute-start.13 = (f32[320,128]{1,0:T(8,128)}, f32[320,128]{1,0:T(8,128)S(1)}, u32[]{:S(2)}, u32[]{:S(2)}) collective-permute-start(f32[320,128]{1,0:T(8,128)} %get-tuple-element.61), channel_id=1, source_target_pairs={{1,2},{2,1},{3,4},{4,3},{5,6},{6,5},{7,8},{8,7},{9,10},{10,9},{11,... | collective-permute-start | bytes 491528 | tf_op jit(solution)/shard_map/ppermute | solution.py:487
  59.1 3.5 %collective-permute-done.14.refs_4_ = f32[40,128]{1,0:T(8,128)S(1)} collective-permute-done((f32[40,128]{1,0:T(8,128)}, f32[40,128]{1,0:T(8,128)S(1)}, u32[]{:S(2)}, u32[]{:S(2)}) %collective-permute-start.14) | collective-permute-done | bytes 20512 | tf_op jit(solution)/shard_map/ppermute | solution.py:491
  62.6 1.2 %collective-permute-done.13.refs_3_ = f32[320,128]{1,0:T(8,128)S(1)} collective-permute-done((f32[320,128]{1,0:T(8,128)}, f32[320,128]{1,0:T(8,128)S(1)}, u32[]{:S(2)}, u32[]{:S(2)}) %collective-permute-start.13) | collective-permute-done | bytes 163872 | tf_op jit(solution)/shard_map/ppermute | solution.py:487
  63.8 0.7 copy-done.3
  64.5 8.4 %begin.3 = (f32[5,16,4096]{2,1,0:T(8,128)}, f32[8,64,128]{2,1,0:T(8,128)}, f32[64,128]{1,0:T(8,128)}, f32[8,128]{1,0:T(8,128)}, f32[32,128]{1,0:T(8,128)}, /*index=5*/f32[32,128]{1,0:T(8,128)}, f32[8,128]{1,0:T(8,128)}) custom-call(f32[5,16,4096]{2,1,0:T(8,128)} %get-tuple-element.59.refs_0_, f32[16,4096]{1,0:T(8,128)} %bitcast.8, f32[320,128]{1,0:T(8,128)} %copy-done.2, ...), custom_call_target="tpu_custom_call" | custom-call | tf_op jit(solution)/shard_map/begin/pallas_call | solution.py:523
  72.8 1.2 %collective-permute-start.15 = (f32[32,128]{1,0:T(8,128)}, f32[32,128]{1,0:T(8,128)S(1)}, u32[]{:S(2)}, u32[]{:S(2)}) collective-permute-start(f32[32,128]{1,0:T(8,128)} %get-tuple-element.63), channel_id=1, source_target_pairs={{0,1},{1,0},{2,3},{3,2},{4,5},{5,4},{6,7},{7,6},{8,9},{9,8},{10,11... | collective-permute-start | bytes 49160 | tf_op jit(solution)/shard_map/ppermute | solution.py:487
  74.1 2.2 %collective-permute-start.16 = (f32[32,128]{1,0:T(8,128)}, f32[32,128]{1,0:T(8,128)S(1)}, u32[]{:S(2)}, u32[]{:S(2)}) collective-permute-start(f32[32,128]{1,0:T(8,128)} %get-tuple-element.64), channel_id=1, source_target_pairs={{1,2},{2,1},{3,4},{4,3},{5,6},{6,5},{7,8},{8,7},{9,10},{10,9},{11,... | collective-permute-start | bytes 49160 | tf_op jit(solution)/shard_map/ppermute | solution.py:487
  76.9 3.3 %collective-permute-done.17.refs_2_ = f32[8,128]{1,0:T(8,128)S(1)} collective-permute-done((f32[8,128]{1,0:T(8,128)}, f32[8,128]{1,0:T(8,128)S(1)}, u32[]{:S(2)}, u32[]{:S(2)}) %collective-permute-start.17) | collective-permute-done | bytes 4128 | tf_op jit(solution)/shard_map/ppermute | solution.py:491
  80.8 2.2 %step.6 = (f32[64,128]{1,0:T(8,128)}, f32[8,128]{1,0:T(8,128)}, f32[32,128]{1,0:T(8,128)}, f32[32,128]{1,0:T(8,128)}, f32[8,128]{1,0:T(8,128)}) custom-call(f32[32,128]{1,0:T(8,128)} %copy-done.15, f32[32,128]{1,0:T(8,128)} %copy-done.17, f32[8,128]{1,0:T(8,128)} %copy-done.23, s32[8,128]{1,0:T(8,128)} %pad_add_fusion.refs_5_.refs_3_, ...), custom_call_target="tpu_custom_call" | custom-call | tf_op jit(solution)/shard_map/step/pallas_call | solution.py:544
  83.0 3.2 %collective-permute-start.19 = (f32[32,128]{1,0:T(8,128)}, f32[32,128]{1,0:T(8,128)S(1)}, u32[]{:S(2)}, u32[]{:S(2)}) collective-permute-start(f32[32,128]{1,0:T(8,128)} %get-tuple-element.69), channel_id=1, source_target_pairs={{1,2},{2,1},{3,4},{4,3},{5,6},{6,5},{7,8},{8,7},{9,10},{10,9},{11,... | collective-permute-start | bytes 49160 | tf_op jit(solution)/shard_map/ppermute | solution.py:487
  86.8 3.3 %collective-permute-done.20.refs_2_ = f32[8,128]{1,0:T(8,128)S(1)} collective-permute-done((f32[8,128]{1,0:T(8,128)}, f32[8,128]{1,0:T(8,128)S(1)}, u32[]{:S(2)}, u32[]{:S(2)}) %collective-permute-start.20) | collective-permute-done | bytes 4128 | tf_op jit(solution)/shard_map/ppermute | solution.py:491
  91.3 2.2 %step.7 = (f32[64,128]{1,0:T(8,128)}, f32[8,128]{1,0:T(8,128)}, f32[32,128]{1,0:T(8,128)}, f32[32,128]{1,0:T(8,128)}, f32[8,128]{1,0:T(8,128)}) custom-call(f32[32,128]{1,0:T(8,128)} %copy-done.10, f32[32,128]{1,0:T(8,128)} %copy-done.11, f32[8,128]{1,0:T(8,128)} %copy-done.19, s32[8,128]{1,0:T(8,128)} %pad_add_fusion.refs_5_.refs_3_, ...), custom_call_target="tpu_custom_call" | custom-call | tf_op jit(solution)/shard_map/step/pallas_call | solution.py:544
  93.6 2.7 %collective-permute-start.22 = (f32[32,128]{1,0:T(8,128)}, f32[32,128]{1,0:T(8,128)S(1)}, u32[]{:S(2)}, u32[]{:S(2)}) collective-permute-start(f32[32,128]{1,0:T(8,128)} %get-tuple-element.72), channel_id=1, source_target_pairs={{1,2},{2,1},{3,4},{4,3},{5,6},{6,5},{7,8},{8,7},{9,10},{10,9},{11,... | collective-permute-start | bytes 49160 | tf_op jit(solution)/shard_map/ppermute | solution.py:487
  96.9 3.3 %collective-permute-done.23.refs_2_ = f32[8,128]{1,0:T(8,128)S(1)} collective-permute-done((f32[8,128]{1,0:T(8,128)}, f32[8,128]{1,0:T(8,128)S(1)}, u32[]{:S(2)}, u32[]{:S(2)}) %collective-permute-start.23) | collective-permute-done | bytes 4128 | tf_op jit(solution)/shard_map/ppermute | solution.py:491
  100.8 6.1 %end.3 = (f32[5,16,4096]{2,1,0:T(8,128)}, f32[16,4096]{1,0:T(8,128)}) custom-call(f32[32,128]{1,0:T(8,128)} %copy-done.6, f32[32,128]{1,0:T(8,128)} %copy-done.7, f32[8,128]{1,0:T(8,128)} %copy-done.18, s32[8,128]{1,0:T(8,128)} %pad_add_fusion.refs_5_.refs_3_, f32[8,64,128]{2,1,0:T(8,128)} %get-tuple-element.74.refs_4_, ...), custom_call_target="tpu_custom_call" | custom-call | tf_op jit(solution)/shard_map/end/pallas_call | solution.py:551
  (79 shorter events, 9.0 us)
Async XLA Ops:
  0.6 7.4 %copy-start.24 = (s32[1,1,1024]{2,1,0:T(1,128)S(1)}, s32[1,1,1024]{2,1,0:T(1,128)}, u32[]{:S(2)}) copy-start(s32[1,1,1024]{2,1,0:T(1,128)} %param.17) | copy-start | bytes 12292
  3.1 5.8 %collective-permute-start.2 = (f32[40,128]{1,0:T(8,128)}, f32[40,128]{1,0:T(8,128)S(1)}, u32[]{:S(2)}, u32[]{:S(2)}) collective-permute-start(f32[40,128]{1,0:T(8,128)} %get-tuple-element.43), channel_id=1, source_target_pairs={{0,16},{16,0},{1,17},{17,1},{2,18},{18,2},{3,19},{19,3},{4,20},{20... | collective-permute-start | bytes 61448 | tf_op jit(solution)/shard_map/ppermute | solution.py:491
  4.6 4.3 %collective-permute-start = (f32[320,128]{1,0:T(8,128)}, f32[320,128]{1,0:T(8,128)S(1)}, u32[]{:S(2)}, u32[]{:S(2)}) collective-permute-start(f32[320,128]{1,0:T(8,128)} %get-tuple-element.41), channel_id=1, source_target_pairs={{0,1},{1,0},{2,3},{3,2},{4,5},{5,4},{6,7},{7,6},{8,9},{9,8},{10,11... | collective-permute-start | bytes 491528 | tf_op jit(solution)/shard_map/ppermute | solution.py:487
  4.6 7.8 %collective-permute-start.1 = (f32[320,128]{1,0:T(8,128)}, f32[320,128]{1,0:T(8,128)S(1)}, u32[]{:S(2)}, u32[]{:S(2)}) collective-permute-start(f32[320,128]{1,0:T(8,128)} %get-tuple-element.42), channel_id=1, source_target_pairs={{1,2},{2,1},{3,4},{4,3},{5,6},{6,5},{7,8},{8,7},{9,10},{10,9},{11,... | collective-permute-start | bytes 491528 | tf_op jit(solution)/shard_map/ppermute | solution.py:487
  8.9 3.6 %copy-start.4 = (f32[40,128]{1,0:T(8,128)}, f32[40,128]{1,0:T(8,128)S(1)}, u32[]{:S(2)}) copy-start(f32[40,128]{1,0:T(8,128)S(1)} %collective-permute-done.2.refs_4_) | copy-start | bytes 61444
  8.9 3.6 %copy-start = (f32[320,128]{1,0:T(8,128)}, f32[320,128]{1,0:T(8,128)S(1)}, u32[]{:S(2)}) copy-start(f32[320,128]{1,0:T(8,128)S(1)} %collective-permute-done.refs_2_) | copy-start | bytes 491524
  12.5 0.7 copy-start.1
  21.0 8.0 %collective-permute-start.3 = (f32[32,128]{1,0:T(8,128)}, f32[32,128]{1,0:T(8,128)S(1)}, u32[]{:S(2)}, u32[]{:S(2)}) collective-permute-start(f32[32,128]{1,0:T(8,128)} %get-tuple-element.44), channel_id=1, source_target_pairs={{0,1},{1,0},{2,3},{3,2},{4,5},{5,4},{6,7},{7,6},{8,9},{9,8},{10,11... | collective-permute-start | bytes 49160 | tf_op jit(solution)/shard_map/ppermute | solution.py:487
  22.3 6.8 %collective-permute-start.4 = (f32[32,128]{1,0:T(8,128)}, f32[32,128]{1,0:T(8,128)S(1)}, u32[]{:S(2)}, u32[]{:S(2)}) collective-permute-start(f32[32,128]{1,0:T(8,128)} %get-tuple-element.45), channel_id=1, source_target_pairs={{1,2},{2,1},{3,4},{4,3},{5,6},{6,5},{7,8},{8,7},{9,10},{10,9},{11,... | collective-permute-start | bytes 49160 | tf_op jit(solution)/shard_map/ppermute | solution.py:487
  25.2 3.9 %collective-permute-start.5 = (f32[8,128]{1,0:T(8,128)}, f32[8,128]{1,0:T(8,128)S(1)}, u32[]{:S(2)}, u32[]{:S(2)}) collective-permute-start(f32[8,128]{1,0:T(8,128)} %get-tuple-element.46), channel_id=1, source_target_pairs={{0,16},{16,0},{1,17},{17,1},{2,18},{18,2},{3,19},{19,3},{4,20},{20... | collective-permute-start | bytes 12296 | tf_op jit(solution)/shard_map/ppermute | solution.py:491
  31.9 6.5 %collective-permute-start.6 = (f32[32,128]{1,0:T(8,128)}, f32[32,128]{1,0:T(8,128)S(1)}, u32[]{:S(2)}, u32[]{:S(2)}) collective-permute-start(f32[32,128]{1,0:T(8,128)} %get-tuple-element.49), channel_id=1, source_target_pairs={{0,1},{1,0},{2,3},{3,2},{4,5},{5,4},{6,7},{7,6},{8,9},{9,8},{10,11... | collective-permute-start | bytes 49160 | tf_op jit(solution)/shard_map/ppermute | solution.py:487
  31.9 6.5 %collective-permute-start.7 = (f32[32,128]{1,0:T(8,128)}, f32[32,128]{1,0:T(8,128)S(1)}, u32[]{:S(2)}, u32[]{:S(2)}) collective-permute-start(f32[32,128]{1,0:T(8,128)} %get-tuple-element.50), channel_id=1, source_target_pairs={{1,2},{2,1},{3,4},{4,3},{5,6},{6,5},{7,8},{8,7},{9,10},{10,9},{11,... | collective-permute-start | bytes 49160 | tf_op jit(solution)/shard_map/ppermute | solution.py:487
  34.5 3.9 %collective-permute-start.8 = (f32[8,128]{1,0:T(8,128)}, f32[8,128]{1,0:T(8,128)S(1)}, u32[]{:S(2)}, u32[]{:S(2)}) collective-permute-start(f32[8,128]{1,0:T(8,128)} %get-tuple-element.51), channel_id=1, source_target_pairs={{0,16},{16,0},{1,17},{17,1},{2,18},{18,2},{3,19},{19,3},{4,20},{20... | collective-permute-start | bytes 12296 | tf_op jit(solution)/shard_map/ppermute | solution.py:491
  41.8 7.3 %collective-permute-start.9 = (f32[32,128]{1,0:T(8,128)}, f32[32,128]{1,0:T(8,128)S(1)}, u32[]{:S(2)}, u32[]{:S(2)}) collective-permute-start(f32[32,128]{1,0:T(8,128)} %get-tuple-element.52), channel_id=1, source_target_pairs={{0,1},{1,0},{2,3},{3,2},{4,5},{5,4},{6,7},{7,6},{8,9},{9,8},{10,11... | collective-permute-start | bytes 49160 | tf_op jit(solution)/shard_map/ppermute | solution.py:487
  41.8 7.3 %collective-permute-start.10 = (f32[32,128]{1,0:T(8,128)}, f32[32,128]{1,0:T(8,128)S(1)}, u32[]{:S(2)}, u32[]{:S(2)}) collective-permute-start(f32[32,128]{1,0:T(8,128)} %get-tuple-element.53), channel_id=1, source_target_pairs={{1,2},{2,1},{3,4},{4,3},{5,6},{6,5},{7,8},{8,7},{9,10},{10,9},{11,... | collective-permute-start | bytes 49160 | tf_op jit(solution)/shard_map/ppermute | solution.py:487
  45.2 3.9 %collective-permute-start.11 = (f32[8,128]{1,0:T(8,128)}, f32[8,128]{1,0:T(8,128)S(1)}, u32[]{:S(2)}, u32[]{:S(2)}) collective-permute-start(f32[8,128]{1,0:T(8,128)} %get-tuple-element.54), channel_id=1, source_target_pairs={{0,16},{16,0},{1,17},{17,1},{2,18},{18,2},{3,19},{19,3},{4,20},{20... | collective-permute-start | bytes 12296 | tf_op jit(solution)/shard_map/ppermute | solution.py:491
  49.1 0.6 copy-start.8
  55.9 6.6 %collective-permute-start.12 = (f32[320,128]{1,0:T(8,128)}, f32[320,128]{1,0:T(8,128)S(1)}, u32[]{:S(2)}, u32[]{:S(2)}) collective-permute-start(f32[320,128]{1,0:T(8,128)} %get-tuple-element.60), channel_id=1, source_target_pairs={{0,1},{1,0},{2,3},{3,2},{4,5},{5,4},{6,7},{7,6},{8,9},{9,8},{10,11... | collective-permute-start | bytes 491528 | tf_op jit(solution)/shard_map/ppermute | solution.py:487
  56.0 7.9 %collective-permute-start.13 = (f32[320,128]{1,0:T(8,128)}, f32[320,128]{1,0:T(8,128)S(1)}, u32[]{:S(2)}, u32[]{:S(2)}) collective-permute-start(f32[320,128]{1,0:T(8,128)} %get-tuple-element.61), channel_id=1, source_target_pairs={{1,2},{2,1},{3,4},{4,3},{5,6},{6,5},{7,8},{8,7},{9,10},{10,9},{11,... | collective-permute-start | bytes 491528 | tf_op jit(solution)/shard_map/ppermute | solution.py:487
  58.5 4.1 %collective-permute-start.14 = (f32[40,128]{1,0:T(8,128)}, f32[40,128]{1,0:T(8,128)S(1)}, u32[]{:S(2)}, u32[]{:S(2)}) collective-permute-start(f32[40,128]{1,0:T(8,128)} %get-tuple-element.62), channel_id=1, source_target_pairs={{0,16},{16,0},{1,17},{17,1},{2,18},{18,2},{3,19},{19,3},{4,20},{20... | collective-permute-start | bytes 61448 | tf_op jit(solution)/shard_map/ppermute | solution.py:491
  62.6 1.2 %copy-start.5 = (f32[40,128]{1,0:T(8,128)}, f32[40,128]{1,0:T(8,128)S(1)}, u32[]{:S(2)}) copy-start(f32[40,128]{1,0:T(8,128)S(1)} %collective-permute-done.14.refs_4_) | copy-start | bytes 61444
  62.6 1.2 %copy-start.2 = (f32[320,128]{1,0:T(8,128)}, f32[320,128]{1,0:T(8,128)S(1)}, u32[]{:S(2)}) copy-start(f32[320,128]{1,0:T(8,128)S(1)} %collective-permute-done.12.refs_2_) | copy-start | bytes 491524
  63.8 0.7 copy-start.3
  72.8 7.4 %collective-permute-start.15 = (f32[32,128]{1,0:T(8,128)}, f32[32,128]{1,0:T(8,128)S(1)}, u32[]{:S(2)}, u32[]{:S(2)}) collective-permute-start(f32[32,128]{1,0:T(8,128)} %get-tuple-element.63), channel_id=1, source_target_pairs={{0,1},{1,0},{2,3},{3,2},{4,5},{5,4},{6,7},{7,6},{8,9},{9,8},{10,11... | collective-permute-start | bytes 49160 | tf_op jit(solution)/shard_map/ppermute | solution.py:487
  74.1 6.2 %collective-permute-start.16 = (f32[32,128]{1,0:T(8,128)}, f32[32,128]{1,0:T(8,128)S(1)}, u32[]{:S(2)}, u32[]{:S(2)}) collective-permute-start(f32[32,128]{1,0:T(8,128)} %get-tuple-element.64), channel_id=1, source_target_pairs={{1,2},{2,1},{3,4},{4,3},{5,6},{6,5},{7,8},{8,7},{9,10},{10,9},{11,... | collective-permute-start | bytes 49160 | tf_op jit(solution)/shard_map/ppermute | solution.py:487
  76.3 3.9 %collective-permute-start.17 = (f32[8,128]{1,0:T(8,128)}, f32[8,128]{1,0:T(8,128)S(1)}, u32[]{:S(2)}, u32[]{:S(2)}) collective-permute-start(f32[8,128]{1,0:T(8,128)} %get-tuple-element.65), channel_id=1, source_target_pairs={{0,16},{16,0},{1,17},{17,1},{2,18},{18,2},{3,19},{19,3},{4,20},{20... | collective-permute-start | bytes 12296 | tf_op jit(solution)/shard_map/ppermute | solution.py:491
  83.0 7.1 %collective-permute-start.18 = (f32[32,128]{1,0:T(8,128)}, f32[32,128]{1,0:T(8,128)S(1)}, u32[]{:S(2)}, u32[]{:S(2)}) collective-permute-start(f32[32,128]{1,0:T(8,128)} %get-tuple-element.68), channel_id=1, source_target_pairs={{0,1},{1,0},{2,3},{3,2},{4,5},{5,4},{6,7},{7,6},{8,9},{9,8},{10,11... | collective-permute-start | bytes 49160 | tf_op jit(solution)/shard_map/ppermute | solution.py:487
  83.0 7.1 %collective-permute-start.19 = (f32[32,128]{1,0:T(8,128)}, f32[32,128]{1,0:T(8,128)S(1)}, u32[]{:S(2)}, u32[]{:S(2)}) collective-permute-start(f32[32,128]{1,0:T(8,128)} %get-tuple-element.69), channel_id=1, source_target_pairs={{1,2},{2,1},{3,4},{4,3},{5,6},{6,5},{7,8},{8,7},{9,10},{10,9},{11,... | collective-permute-start | bytes 49160 | tf_op jit(solution)/shard_map/ppermute | solution.py:487
  86.2 3.9 %collective-permute-start.20 = (f32[8,128]{1,0:T(8,128)}, f32[8,128]{1,0:T(8,128)S(1)}, u32[]{:S(2)}, u32[]{:S(2)}) collective-permute-start(f32[8,128]{1,0:T(8,128)} %get-tuple-element.70), channel_id=1, source_target_pairs={{0,16},{16,0},{1,17},{17,1},{2,18},{18,2},{3,19},{19,3},{4,20},{20... | collective-permute-start | bytes 12296 | tf_op jit(solution)/shard_map/ppermute | solution.py:491
  93.5 6.6 %collective-permute-start.21 = (f32[32,128]{1,0:T(8,128)}, f32[32,128]{1,0:T(8,128)S(1)}, u32[]{:S(2)}, u32[]{:S(2)}) collective-permute-start(f32[32,128]{1,0:T(8,128)} %get-tuple-element.71), channel_id=1, source_target_pairs={{0,1},{1,0},{2,3},{3,2},{4,5},{5,4},{6,7},{7,6},{8,9},{9,8},{10,11... | collective-permute-start | bytes 49160 | tf_op jit(solution)/shard_map/ppermute | solution.py:487
  93.6 6.6 %collective-permute-start.22 = (f32[32,128]{1,0:T(8,128)}, f32[32,128]{1,0:T(8,128)S(1)}, u32[]{:S(2)}, u32[]{:S(2)}) collective-permute-start(f32[32,128]{1,0:T(8,128)} %get-tuple-element.72), channel_id=1, source_target_pairs={{1,2},{2,1},{3,4},{4,3},{5,6},{6,5},{7,8},{8,7},{9,10},{10,9},{11,... | collective-permute-start | bytes 49160 | tf_op jit(solution)/shard_map/ppermute | solution.py:487
  96.3 3.9 %collective-permute-start.23 = (f32[8,128]{1,0:T(8,128)}, f32[8,128]{1,0:T(8,128)S(1)}, u32[]{:S(2)}, u32[]{:S(2)}) collective-permute-start(f32[8,128]{1,0:T(8,128)} %get-tuple-element.73), channel_id=1, source_target_pairs={{0,16},{16,0},{1,17},{17,1},{2,18},{18,2},{3,19},{19,3},{4,20},{20... | collective-permute-start | bytes 12296 | tf_op jit(solution)/shard_map/ppermute | solution.py:491
  (17 other events, 10.1 us)

commit v2 on v1

--- a/solution.py
+++ b/solution.py
@@ -27,6 +27,7 @@
 ZERO_ROW = 8
 F32 = jnp.float32
 BF16 = jnp.bfloat16
+MIB = 1 << 20
 
 
 def sine(n):
@@ -75,21 +76,49 @@
         to_b[r] = both(sz[0::2, half + r][:, None], sz[1::2, r][:, None])
         from_a[r] = both(sz[2 * r, :half][:, None], sz[2 * r + 1, half:][:, None])
         from_b[r] = both(sz[2 * r + 1, :half][:, None], sz[2 * r, half:][:, None])
-    f = lambda a: np.ascontiguousarray(a, dtype=np.float32)
-    return dict(
-        coef=f(coef.reshape(half * half, LANES)),
-        inv=f(inv),
-        cross=f(cross),
-        diag_z=f(diag_z),
-        diag_x=f(diag_x),
-        col_x=f(np.broadcast_to(sx[:, :1], (NX, LANES))),
-        edge=f(edge),
-        fwd=np.concatenate([fwd_hi, fwd_hi, fwd_lo], axis=1),
-        bwd=np.concatenate([bwd_hi, bwd_hi, bwd_lo], axis=1),
-        ky2=np.concatenate([ky_hi, ky_hi], axis=0),
+    hi = lambda high, low: np.concatenate([high, high, low, np.zeros_like(low)], axis=1)
+    wide = lambda m: np.concatenate([m[:, :LANES], m[:, LANES:]], axis=0)
+    parts = dict(
+        coef=coef.reshape(half * half, LANES),
+        inv=inv.reshape(half * NX, LANES),
+        cross=cross.reshape(half * NX, LANES),
+        diag_z=diag_z,
+        diag_x=diag_x,
+        col_x=np.broadcast_to(sx[:, :1], (NX, LANES)),
+        edge=edge,
+        fwd=wide(hi(fwd_hi, fwd_lo)),
+        bwd=wide(hi(bwd_hi, bwd_lo)),
+        ky_hi=ky_hi,
         ky_lo=ky_lo,
-        plane=f(np.stack([to_a, to_b, from_a, from_b])),
+        plane=np.stack([to_a, to_b, from_a, from_b]).reshape(4 * half * half, LANES),
     )
+    places, at = {}, 0
+    for name, part in parts.items():
+        places[name] = (at, at + part.shape[0])
+        at += part.shape[0]
+    return np.concatenate([np.asarray(p, np.float32) for p in parts.values()], axis=0), places
+
+
+class Tables:
+    def __init__(self, ref, places):
+        self.ref, self.places = ref, places
+
+    def __getitem__(self, name):
+        first, last = self.places[name]
+        return self.ref[first:last]
+
+    def row(self, name, i):
+        first = self.places[name][0] + i
+        return self.ref[first : first + 1]
+
+    def block(self, name, i, n):
+        first = self.places[name][0] + i * n
+        return self.ref[first : first + n]
+
+    def wide(self, name):
+        both_halves = self[name].astype(BF16)
+        n = both_halves.shape[0] // 2
+        return jnp.concatenate([both_halves[:n], both_halves[n:]], axis=1)
 
 
 def lower_half(shape):
@@ -105,23 +134,27 @@
     return high, (v - high.astype(F32)).astype(BF16)
 
 
-def y_transform(v, ky2, ky_lo):
+def y_transform(v, tab):
     high, low = hi_lo(v)
-    return jnp.dot(jnp.concatenate([high, low], axis=1), ky2[...], preferred_element_type=F32) + jnp.dot(
-        high, ky_lo[...], preferred_element_type=F32
-    )
+    table = tab["ky_hi"].astype(BF16)
+    return jnp.dot(
+        jnp.concatenate([high, low], axis=1), jnp.concatenate([table, table], axis=0), preferred_element_type=F32
+    ) + jnp.dot(high, tab["ky_lo"].astype(BF16), preferred_element_type=F32)
 
 
 def x_transform(table, v):
     high, low = hi_lo(v)
-    return jnp.dot(table[...], jnp.concatenate([high, low, high], axis=0), preferred_element_type=F32)
-
-
-def mix_rows(v, a, b):
+    return jnp.dot(table, jnp.concatenate([high, low, high, jnp.zeros_like(high)], axis=0), preferred_element_type=F32)
+
+
+def mix_rows(v, tab, first):
     swapped = swap_halves(v)
+    half = v.shape[0]
     out = jnp.zeros_like(v)
-    for r in range(v.shape[0]):
-        out = out + a[r] * v[r : r + 1] + b[r] * swapped[r : r + 1]
+    for r in range(half):
+        a = tab.block("plane", first * half + r, half)
+        b = tab.block("plane", (first + 1) * half + r, half)
+        out = out + a * v[r : r + 1] + b * swapped[r : r + 1]
     return out
 
 
@@ -176,8 +209,7 @@
 
 
 def send_plane(y, tab, plane_out):
-    cells = mix_rows(y_transform(y, tab["ky2"], tab["ky_lo"]), tab["plane"].at[2], tab["plane"].at[3])
-    plane_out[...] = cells
+    plane_out[...] = mix_rows(y_transform(y, tab), tab, 2)
 
 
 def x_ghost_tiles(ghost, is_fine):
@@ -231,20 +263,18 @@
     lax.fori_loop(0, TILES, tile, 0)
 
 
-NAMES_SOLVE = ("coef", "inv", "edge", "col_x", "fwd", "ky2", "ky_lo", "plane")
-
-
-def begin_kernel(height, second, *refs):
+def begin_kernel(height, places, second, *refs):
     refs = list(refs)
     take = lambda n: [refs.pop(0) for _ in range(n)]
     current, burn, from_even, from_odd, planes, mapping = take(6)
     initial = take(1)[0] if second else None
-    tab = dict(zip(NAMES_SOLVE, take(len(NAMES_SOLVE))))
+    tab = Tables(take(1)[0], places)
     predicted, spectrum, trace, facet, to_even, to_odd, plane_out = take(7)
     pad, source, folded, mixed = take(4)
     is_fine, even = position()
     half = height // 2
     tile_low = lower_half((height, LANES))
+    tiled = pad.reshape(FIELDS, TILES + 2, ROWS, LANES)
 
     for f in range(FIELDS):
         ghost = gather(planes[f * half : (f + 1) * half], mapping[...])
@@ -270,11 +300,9 @@
 
     def tile(t, _):
         lanes = pl.ds(pl.multiple_of(t * LANES, LANES), LANES)
-        base = pl.multiple_of((t + 1) * ROWS, ROWS)
 
         def at(f, dz=0, dt=0):
-            window = pad[f, pl.ds(pl.multiple_of(base + dt * ROWS, ROWS), ROWS)]
-            return window[ZERO_ROW + dz : ZERO_ROW + dz + height]
+            return tiled[f, t + 1 + dt, ZERO_ROW + dz : ZERO_ROW + dz + height]
 
         u, v, w = at(0), at(1), at(2)
         fuel, oxygen = at(3), at(4)
@@ -319,26 +347,26 @@
         folded[q, 0:TILES] = jnp.where(low, total, swap_halves(delta))
         folded[q, TILES : 2 * TILES] = jnp.where(low, swap_halves(total), delta)
 
-    z_mix(folded, mixed, tab["coef"], half, False)
+    z_mix(folded, mixed, tab, half, False)
     wide = jnp.concatenate([mixed[p] for p in range(half)], axis=1)
-    wide = x_transform(tab["fwd"], wide)
+    wide = x_transform(tab.wide("fwd"), wide)
     tall = jnp.concatenate([wide[:, p * LANES : (p + 1) * LANES] for p in range(half)], axis=0)
-    mixed[...] = y_transform(tall, tab["ky2"], tab["ky_lo"]).reshape(half, NX, LANES)
+    mixed[...] = y_transform(tall, tab).reshape(half, NX, LANES)
 
     sign = row_sign(is_fine, (NX, LANES))
-    column = tab["col_x"][...] * sign
+    column = tab["col_x"] * sign
     u0 = jnp.zeros((NX, LANES), F32)
     for p in range(half):
-        solved = mixed[p] * tab["inv"][p]
+        solved = mixed[p] * tab.block("inv", p, NX)
         spectrum[p] = solved
-        u0 = u0 + tab["edge"][p : p + 1] * solved
+        u0 = u0 + tab.row("edge", p) * solved
         facet[p : p + 1] = jnp.sum(column * solved, axis=0, keepdims=True)
     trace[...] = u0
     send_traces(u0, even, to_even, to_odd)
     send_plane(facet[...], tab, plane_out)
 
 
-def z_mix(src, dst, coef, half, inverse):
+def z_mix(src, dst, tab, half, inverse):
     def chunk(r, _):
         rows = pl.ds(pl.multiple_of(r * 8, 8), 8)
         parts = [src[j, rows] for j in range(half)]
@@ -346,7 +374,7 @@
             total = None
             for j in range(half):
                 k = j * half + i if inverse else i * half + j
-                term = coef[k : k + 1] * parts[j]
+                term = tab.row("coef", k) * parts[j]
                 total = term if total is None else total + term
             dst[i, rows] = total
         return 0
@@ -354,48 +382,44 @@
     lax.fori_loop(0, NX // 8, chunk, 0)
 
 
-NAMES_STEP = ("cross", "diag_z", "diag_x", "ky2", "ky_lo", "plane")
-
-
 def ghost_modes(plane, mapping, tab):
     cells = gather(plane[...], mapping[...])
-    return y_transform(mix_rows(cells, tab["plane"].at[0], tab["plane"].at[1]), tab["ky2"], tab["ky_lo"])
-
-
-def step_kernel(height, *refs):
+    return y_transform(mix_rows(cells, tab, 0), tab)
+
+
+def step_kernel(height, places, last, *refs):
     refs = list(refs)
     take = lambda n: [refs.pop(0) for _ in range(n)]
     from_even, from_odd, plane_in, mapping, trace, facet = take(6)
-    tab = dict(zip(NAMES_STEP, take(len(NAMES_STEP))))
-    layers_out, side_out, to_even, to_odd, plane_out = take(5)
+    tab = Tables(take(1)[0], places)
+    layers_out, side_out = take(2) if last else (None, None)
+    to_even, to_odd, plane_out = take(3)
     (facet_next,) = take(1)
     is_fine, even = position()
     half = height // 2
     low_ghost, high_ghost = ghost_low_high(from_even, from_odd, even)
     layers = jnp.where(lower_half((NX, LANES)), low_ghost + high_ghost, low_ghost - high_ghost)
     side = ghost_modes(plane_in, mapping, tab)
-    layers_out[...] = layers
-    side_out[...] = side
+    if last:
+        layers_out[...] = layers
+        side_out[...] = side
     sign = row_sign(is_fine, (NX, LANES))
     signed = sign * layers
     cross_sum = jnp.zeros((NX, LANES), F32)
     for p in range(half):
-        cross = tab["cross"][p]
+        cross = tab.block("cross", p, NX)
         cross_sum = cross_sum + cross * side[p : p + 1]
         facet_next[p : p + 1] = jnp.sum(cross * signed, axis=0, keepdims=True)
-    u = trace[...] + tab["diag_z"][...] * layers + sign * cross_sum
+    u = trace[...] + tab["diag_z"] * layers + sign * cross_sum
     send_traces(u, even, to_even, to_odd)
-    send_plane(facet[...] + tab["diag_x"][...] * side + facet_next[...], tab, plane_out)
-
-
-NAMES_END = ("coef", "inv", "edge", "col_x", "bwd", "ky2", "ky_lo")
-
-
-def end_kernel(height, final, *refs):
+    send_plane(facet[...] + tab["diag_x"] * side + facet_next[...], tab, plane_out)
+
+
+def end_kernel(height, places, final, *refs):
     refs = list(refs)
     take = lambda n: [refs.pop(0) for _ in range(n)]
     from_even, from_odd, plane_in, mapping, spectrum, layers, side, predicted = take(8)
-    tab = dict(zip(NAMES_END, take(len(NAMES_END))))
+    tab = Tables(take(1)[0], places)
     state = take(1)[0]
     if final:
         (head,) = take(1)
@@ -405,19 +429,19 @@
     is_fine, even = position()
     half = height // 2
     sign = row_sign(is_fine, (NX, LANES))
-    column = tab["col_x"][...] * sign
+    column = tab["col_x"] * sign
     for p in range(half):
-        push = tab["edge"][p : p + 1] * layers[...] + column * side[p : p + 1]
-        tall[p * NX : (p + 1) * NX] = spectrum[p] + push * tab["inv"][p]
+        push = tab.row("edge", p) * layers[...] + column * side[p : p + 1]
+        tall[p * NX : (p + 1) * NX] = spectrum[p] + push * tab.block("inv", p, NX)
     low_ghost, high_ghost = ghost_low_high(from_even, from_odd, even)
     tall[half * NX : (half + 1) * NX] = jnp.where(lower_half((NX, LANES)), low_ghost, high_ghost)
 
-    cells = y_transform(tall[...], tab["ky2"], tab["ky_lo"])
+    cells = y_transform(tall[...], tab)
     wide = jnp.concatenate([cells[p * NX : (p + 1) * NX] for p in range(half + 1)], axis=1)
-    wide = x_transform(tab["bwd"], wide)
+    wide = x_transform(tab.wide("bwd"), wide)
     for p in range(half):
         mixed[p] = wide[:, p * LANES : (p + 1) * LANES]
-    z_mix(mixed, unmixed, tab["coef"], half, True)
+    z_mix(mixed, unmixed, tab, half, True)
 
     low = lower_half((TILES, LANES))
 
@@ -439,14 +463,13 @@
     pad[last : last + height] = east
 
     tile_low = lower_half((height, LANES))
+    tiled = pad.reshape(TILES + 2, ROWS, LANES)
 
     def tile(t, _):
         lanes = pl.ds(pl.multiple_of(t * LANES, LANES), LANES)
-        base = pl.multiple_of((t + 1) * ROWS, ROWS)
 
         def at(dz=0, dt=0):
-            window = pad[pl.ds(pl.multiple_of(base + dt * ROWS, ROWS), ROWS)]
-            return window[ZERO_ROW + dz : ZERO_ROW + dz + height]
+            return tiled[t + 1 + dt, ZERO_ROW + dz : ZERO_ROW + dz + height]
 
         centre = at()
         east, west = east_west(centre, at(0, -1), at(0, 1), tile_low)
@@ -499,7 +522,8 @@
     height = state.shape[2]
     half = height // 2
     cells = NX * NY
-    tab = {name: jnp.asarray(value) for name, value in tables(height).items()}
+    table, places = tables(height)
+    table = jnp.asarray(table)
     shape = lambda *s: jax.ShapeDtypeStruct(s, F32)
     halo = shape(2 * FIELDS * TILES, LANES)
     trace_packed = shape(NX // 2, LANES)
@@ -512,6 +536,7 @@
     to_even, to_odd, planes = pl.pallas_call(
         functools.partial(pack_kernel, height),
         out_shape=(halo, halo, shape(FIELDS * half, LANES)),
+        compiler_params=pltpu.CompilerParams(vmem_limit_bytes=8 * MIB),
         name="pack",
     )(initial)
     current = initial
@@ -521,7 +546,7 @@
         from_even, from_odd, planes_in = exchange(to_even, to_odd, planes)
         args = (current, burning, from_even, from_odd, planes_in, mapping) + ((initial,) if second else ())
         predicted, spectrum, trace, facet, to_even, to_odd, plane_out = pl.pallas_call(
-            functools.partial(begin_kernel, height, second),
+            functools.partial(begin_kernel, height, places, second),
             out_shape=(
                 shape(FIELDS, height, cells),
                 shape(half, NX, LANES),
@@ -537,19 +562,22 @@
                 pltpu.VMEM((half, NX, LANES), F32),
                 pltpu.VMEM((half, NX, LANES), F32),
             ],
+            compiler_params=pltpu.CompilerParams(vmem_limit_bytes=16 * MIB),
             name="begin",
-        )(*args, *(tab[n] for n in NAMES_SOLVE))
-        for _ in range(ITERS - 1):
+        )(*args, table)
+        for sweep in range(ITERS - 1):
+            last = sweep == ITERS - 2
             received = exchange(to_even, to_odd, plane_out)
-            layers, side, to_even, to_odd, plane_out = pl.pallas_call(
-                functools.partial(step_kernel, height),
-                out_shape=(shape(NX, LANES), plane, trace_packed, trace_packed, plane),
+            *kept, to_even, to_odd, plane_out = pl.pallas_call(
+                functools.partial(step_kernel, height, places, last),
+                out_shape=((shape(NX, LANES), plane) if last else ()) + (trace_packed, trace_packed, plane),
                 scratch_shapes=[pltpu.VMEM((half, LANES), F32)],
+                compiler_params=pltpu.CompilerParams(vmem_limit_bytes=4 * MIB),
                 name="step",
-            )(*received, mapping, trace, facet, *(tab[n] for n in NAMES_STEP))
+            )(*received, mapping, trace, facet, table)
         received = exchange(to_even, to_odd, plane_out)
         outs = pl.pallas_call(
-            functools.partial(end_kernel, height, final),
+            functools.partial(end_kernel, height, places, final),
             out_shape=(shape(FIELDS, height, cells),)
             + ((shape(height, cells),) if final else (halo, halo, shape(FIELDS * half, LANES))),
             scratch_shapes=[
@@ -558,8 +586,9 @@
                 pltpu.VMEM((half, NX, LANES), F32),
                 pltpu.VMEM(((TILES + 2) * ROWS, LANES), F32),
             ],
+            compiler_params=pltpu.CompilerParams(vmem_limit_bytes=16 * MIB),
             name="end",
-        )(*received, mapping, spectrum, layers, side, predicted, *(tab[n] for n in NAMES_END))
+        )(*received, mapping, spectrum, *kept, predicted, table)
         current = outs[0]
         if not final:
             to_even, to_odd, planes = outs[1:]

time: 107 us -> 84.6 us (0.79)
  Pallas kernels: 40 us -> 21.9 us
  local copies, waits for them, and re-layouts: 6.29 us -> 2.9 us
  waiting for transfers between devices: 28.2 us -> 27.1 us
    pallas_call x8, Pallas kernels: 37.5 us -> 21.5 us  [the longest x2 11.1 us: shards(): pl.pallas_call(functools.partial(begin_kernel, height, places, second), o...]
    unnamed x50 -> x12, local copies, waits for them, and re-layouts: 6.12 us -> 2.73 us
    pallas_call x1, Pallas kernels: 2.48 us -> 0.43 us  [shards(): pl.pallas_call(functools.partial(pack_kernel, height), out_shape=(halo, h...]
    ppermute x8, waiting for transfers between devices: 23.4 us -> 21.9 us  [swap_partner(): return lax.ppermute(x, 'grp', [(0, 1), (1, 0)])]
  transfers between devices with their start and end apart: 24 -> 24, of which waited for: 9 -> 9; matrix products, arithmetic and copies ran while one was open for 1% -> 0% of each run, Pallas kernels for 0% -> 0%
where the time goes in v2:
time: 84.6 us; the launch traced here: 84.3 us
  starting transfers between devices  31.5 us (37%)
  waiting for transfers between devices  27.1 us (32%)
  Pallas kernels  21.9 us (26%)
  local copies, waits for them, and re-layouts  2.9 us (3%)
    ppermute x16, starting transfers between devices, swap_pairs(): return lax.ppermute(x, 'mesh', route)  25.9 us
    ppermute x8, waiting for transfers between devices, swap_partner(): return lax.ppermute(x, 'grp', [(0, 1), (1, 0)])  21.9 us
    pallas_call x2, Pallas kernels, shards(): pl.pallas_call(functools.partial(begin_kernel, height, places, second), o...  11.1 us
    pallas_call x2, Pallas kernels, shards(): pl.pallas_call(functools.partial(end_kernel, height, places, final), out_...  8.34 us
    ppermute x8, starting transfers between devices, swap_partner(): return lax.ppermute(x, 'grp', [(0, 1), (1, 0)])  5.59 us
    ppermute x16, waiting for transfers between devices, swap_pairs(): return lax.ppermute(x, 'mesh', route)  5.23 us
    unnamed x12, local copies, waits for them, and re-layouts  2.73 us
    pallas_call x4, Pallas kernels, shards(): pl.pallas_call(functools.partial(step_kernel, height, places, last), out_...  1.98 us
  transfers between devices with their start and end apart: 24, of which 9 were waited for; matrix products, arithmetic and copies ran while one was open for 0% of the time, Pallas kernels for 0%

profile of v2, /device:TPU:24, one launch (start us, length us, event | category | flops | bytes accessed | tf_op | source)
XLA Modules:
  0.0 84.3 jit_solution(10243891099445267398)
XLA Ops:
  0.7 1.4 %copy-done.1 = f32[1,5,16,4096]{3,2,1,0:T(8,128)S(1)} copy-done((f32[1,5,16,4096]{3,2,1,0:T(8,128)S(1)}, f32[1,5,16,4096]{3,2,1,0:T(8,128)}, u32[]{:S(2)}) %copy-start.1) | copy-done | bytes 1310744
  2.5 1.6 %collective-permute-start.2 = (f32[40,128]{1,0:T(8,128)S(1)}, f32[40,128]{1,0:T(8,128)S(1)}, u32[]{:S(2)}, u32[]{:S(2)}) collective-permute-start(f32[40,128]{1,0:T(8,128)S(1)} %get-tuple-element.43), channel_id=1, source_target_pairs={{0,16},{16,0},{1,17},{17,1},{2,18},{18,2},{3,19},{19,3},{4,20},{20... | collective-permute-start | bytes 61448 | tf_op jit(solution)/shard_map/ppermute | solution.py:514
  4.1 3.4 %collective-permute-start.1 = (f32[320,128]{1,0:T(8,128)S(1)}, f32[320,128]{1,0:T(8,128)S(1)}, u32[]{:S(2)}, u32[]{:S(2)}) collective-permute-start(f32[320,128]{1,0:T(8,128)S(1)} %get-tuple-element.42), channel_id=1, source_target_pairs={{1,2},{2,1},{3,4},{4,3},{5,6},{6,5},{7,8},{8,7},{9,10},{10,9},{11,... | collective-permute-start | bytes 491528 | tf_op jit(solution)/shard_map/ppermute | solution.py:510
  7.7 4.0 %collective-permute-done.1.refs_3_ = f32[320,128]{1,0:T(8,128)S(1)} collective-permute-done((f32[320,128]{1,0:T(8,128)S(1)}, f32[320,128]{1,0:T(8,128)S(1)}, u32[]{:S(2)}, u32[]{:S(2)}) %collective-permute-start.1) | collective-permute-done | bytes 163872 | tf_op jit(solution)/shard_map/ppermute | solution.py:510
  11.7 1.3 %copy-done.2 = f32[1,5,16,4096]{3,2,1,0:T(8,128)S(1)} copy-done((f32[1,5,16,4096]{3,2,1,0:T(8,128)S(1)}, f32[1,5,16,4096]{3,2,1,0:T(8,128)}, u32[]{:S(2)}) %copy-start.2) | copy-done | bytes 1310744
  13.0 5.5 %begin.2 = (f32[5,16,4096]{2,1,0:T(8,128)S(1)}, f32[8,64,128]{2,1,0:T(8,128)S(1)}, f32[64,128]{1,0:T(8,128)S(1)}, f32[8,128]{1,0:T(8,128)S(1)}, f32[32,128]{1,0:...) custom-call(f32[5,16,4096]{2,1,0:T(8,128)S(1)} %bitcast.5, f32[16,4096]{1,0:T(8,128)S(1)} %bitcast.7, ...), custom_call_target="tpu_custom_call" | custom-call | tf_op jit(solution)/shard_map/begin/pallas_call | solution.py:548
  18.6 1.3 %collective-permute-start.3 = (f32[32,128]{1,0:T(8,128)S(1)}, f32[32,128]{1,0:T(8,128)S(1)}, u32[]{:S(2)}, u32[]{:S(2)}) collective-permute-start(f32[32,128]{1,0:T(8,128)S(1)} %get-tuple-element.44), channel_id=1, source_target_pairs={{0,1},{1,0},{2,3},{3,2},{4,5},{5,4},{6,7},{7,6},{8,9},{9,8},{10,11... | collective-permute-start | bytes 49160 | tf_op jit(solution)/shard_map/ppermute | solution.py:510
  19.9 2.9 %collective-permute-start.4 = (f32[32,128]{1,0:T(8,128)S(1)}, f32[32,128]{1,0:T(8,128)S(1)}, u32[]{:S(2)}, u32[]{:S(2)}) collective-permute-start(f32[32,128]{1,0:T(8,128)S(1)} %get-tuple-element.45), channel_id=1, source_target_pairs={{1,2},{2,1},{3,4},{4,3},{5,6},{6,5},{7,8},{8,7},{9,10},{10,9},{11,... | collective-permute-start | bytes 49160 | tf_op jit(solution)/shard_map/ppermute | solution.py:510
  22.8 0.6 collective-permute-start.5
  23.3 3.1 %collective-permute-done.5.refs_2_ = f32[8,128]{1,0:T(8,128)S(1)} collective-permute-done((f32[8,128]{1,0:T(8,128)S(1)}, f32[8,128]{1,0:T(8,128)S(1)}, u32[]{:S(2)}, u32[]{:S(2)}) %collective-permute-start.5) | collective-permute-done | bytes 4128 | tf_op jit(solution)/shard_map/ppermute | solution.py:514
  27.0 2.6 %collective-permute-start.7 = (f32[32,128]{1,0:T(8,128)S(1)}, f32[32,128]{1,0:T(8,128)S(1)}, u32[]{:S(2)}, u32[]{:S(2)}) collective-permute-start(f32[32,128]{1,0:T(8,128)S(1)} %get-tuple-element.50), channel_id=1, source_target_pairs={{1,2},{2,1},{3,4},{4,3},{5,6},{6,5},{7,8},{8,7},{9,10},{10,9},{11,... | collective-permute-start | bytes 49160 | tf_op jit(solution)/shard_map/ppermute | solution.py:510
  30.2 3.1 %collective-permute-done.8.refs_2_ = f32[8,128]{1,0:T(8,128)S(1)} collective-permute-done((f32[8,128]{1,0:T(8,128)S(1)}, f32[8,128]{1,0:T(8,128)S(1)}, u32[]{:S(2)}, u32[]{:S(2)}) %collective-permute-start.8) | collective-permute-done | bytes 4128 | tf_op jit(solution)/shard_map/ppermute | solution.py:514
  33.9 3.4 %collective-permute-start.10 = (f32[32,128]{1,0:T(8,128)S(1)}, f32[32,128]{1,0:T(8,128)S(1)}, u32[]{:S(2)}, u32[]{:S(2)}) collective-permute-start(f32[32,128]{1,0:T(8,128)S(1)} %get-tuple-element.53), channel_id=1, source_target_pairs={{1,2},{2,1},{3,4},{4,3},{5,6},{6,5},{7,8},{8,7},{9,10},{10,9},{11,... | collective-permute-start | bytes 49160 | tf_op jit(solution)/shard_map/ppermute | solution.py:510
  37.2 0.6 collective-permute-start.11
  37.8 3.1 %collective-permute-done.11.refs_2_ = f32[8,128]{1,0:T(8,128)S(1)} collective-permute-done((f32[8,128]{1,0:T(8,128)S(1)}, f32[8,128]{1,0:T(8,128)S(1)}, u32[]{:S(2)}, u32[]{:S(2)}) %collective-permute-start.11) | collective-permute-done | bytes 4128 | tf_op jit(solution)/shard_map/ppermute | solution.py:514
  40.9 3.7 %end.2 = (f32[5,16,4096]{2,1,0:T(8,128)S(1)}, f32[320,128]{1,0:T(8,128)S(1)}, f32[320,128]{1,0:T(8,128)S(1)}, f32[40,128]{1,0:T(8,128)S(1)}) custom-call(f32[32,128]{1,0:T(8,128)S(1)} %collective-permute-done.9.refs_0_, f32[32,128]{1,0:T(8,128)S(1)} %collective-permute-done.10.refs_1_, f32[8,128]{1,0:T(8,128)S(1)} %collective-permute-done.11.refs_2_, ...), custom_call_target="tpu_custom_call" | custom-call | tf_op jit(solution)/shard_map/end/pallas_call | solution.py:579
  44.7 2.6 %collective-permute-start.13 = (f32[320,128]{1,0:T(8,128)S(1)}, f32[320,128]{1,0:T(8,128)S(1)}, u32[]{:S(2)}, u32[]{:S(2)}) collective-permute-start(f32[320,128]{1,0:T(8,128)S(1)} %get-tuple-element.61), channel_id=1, source_target_pairs={{1,2},{2,1},{3,4},{4,3},{5,6},{6,5},{7,8},{8,7},{9,10},{10,9},{11,... | collective-permute-start | bytes 491528 | tf_op jit(solution)/shard_map/ppermute | solution.py:510
  47.2 0.6 collective-permute-start.14
  47.8 3.3 %collective-permute-done.14.refs_4_ = f32[40,128]{1,0:T(8,128)S(1)} collective-permute-done((f32[40,128]{1,0:T(8,128)S(1)}, f32[40,128]{1,0:T(8,128)S(1)}, u32[]{:S(2)}, u32[]{:S(2)}) %collective-permute-start.14) | collective-permute-done | bytes 20512 | tf_op jit(solution)/shard_map/ppermute | solution.py:514
  51.1 1.2 %collective-permute-done.13.refs_3_ = f32[320,128]{1,0:T(8,128)S(1)} collective-permute-done((f32[320,128]{1,0:T(8,128)S(1)}, f32[320,128]{1,0:T(8,128)S(1)}, u32[]{:S(2)}, u32[]{:S(2)}) %collective-permute-start.13) | collective-permute-done | bytes 163872 | tf_op jit(solution)/shard_map/ppermute | solution.py:510
  52.3 5.6 %begin.3 = (f32[5,16,4096]{2,1,0:T(8,128)S(1)}, f32[8,64,128]{2,1,0:T(8,128)S(1)}, f32[64,128]{1,0:T(8,128)S(1)}, f32[8,128]{1,0:T(8,128)S(1)}, f32[32,128]{1,0:...) custom-call(f32[5,16,4096]{2,1,0:T(8,128)S(1)} %get-tuple-element.59.refs_0_, f32[16,4096]{1,0:T(8,128)S(1)} %bitcast.8, ...), custom_call_target="tpu_custom_call" | custom-call | tf_op jit(solution)/shard_map/begin/pallas_call | solution.py:548
  57.9 1.3 %collective-permute-start.15 = (f32[32,128]{1,0:T(8,128)S(1)}, f32[32,128]{1,0:T(8,128)S(1)}, u32[]{:S(2)}, u32[]{:S(2)}) collective-permute-start(f32[32,128]{1,0:T(8,128)S(1)} %get-tuple-element.63), channel_id=1, source_target_pairs={{0,1},{1,0},{2,3},{3,2},{4,5},{5,4},{6,7},{7,6},{8,9},{9,8},{10,11... | collective-permute-start | bytes 49160 | tf_op jit(solution)/shard_map/ppermute | solution.py:510
  59.2 2.3 %collective-permute-start.16 = (f32[32,128]{1,0:T(8,128)S(1)}, f32[32,128]{1,0:T(8,128)S(1)}, u32[]{:S(2)}, u32[]{:S(2)}) collective-permute-start(f32[32,128]{1,0:T(8,128)S(1)} %get-tuple-element.64), channel_id=1, source_target_pairs={{1,2},{2,1},{3,4},{4,3},{5,6},{6,5},{7,8},{8,7},{9,10},{10,9},{11,... | collective-permute-start | bytes 49160 | tf_op jit(solution)/shard_map/ppermute | solution.py:510
  61.5 0.6 collective-permute-start.17
  62.1 3.1 %collective-permute-done.17.refs_2_ = f32[8,128]{1,0:T(8,128)S(1)} collective-permute-done((f32[8,128]{1,0:T(8,128)S(1)}, f32[8,128]{1,0:T(8,128)S(1)}, u32[]{:S(2)}, u32[]{:S(2)}) %collective-permute-start.17) | collective-permute-done | bytes 4128 | tf_op jit(solution)/shard_map/ppermute | solution.py:514
  65.8 3.2 %collective-permute-start.19 = (f32[32,128]{1,0:T(8,128)S(1)}, f32[32,128]{1,0:T(8,128)S(1)}, u32[]{:S(2)}, u32[]{:S(2)}) collective-permute-start(f32[32,128]{1,0:T(8,128)S(1)} %get-tuple-element.69), channel_id=1, source_target_pairs={{1,2},{2,1},{3,4},{4,3},{5,6},{6,5},{7,8},{8,7},{9,10},{10,9},{11,... | collective-permute-start | bytes 49160 | tf_op jit(solution)/shard_map/ppermute | solution.py:510
  69.0 0.6 collective-permute-start.20
  69.5 3.1 %collective-permute-done.20.refs_2_ = f32[8,128]{1,0:T(8,128)S(1)} collective-permute-done((f32[8,128]{1,0:T(8,128)S(1)}, f32[8,128]{1,0:T(8,128)S(1)}, u32[]{:S(2)}, u32[]{:S(2)}) %collective-permute-start.20) | collective-permute-done | bytes 4128 | tf_op jit(solution)/shard_map/ppermute | solution.py:514
  73.2 2.7 %collective-permute-start.22 = (f32[32,128]{1,0:T(8,128)S(1)}, f32[32,128]{1,0:T(8,128)S(1)}, u32[]{:S(2)}, u32[]{:S(2)}) collective-permute-start(f32[32,128]{1,0:T(8,128)S(1)} %get-tuple-element.72), channel_id=1, source_target_pairs={{1,2},{2,1},{3,4},{4,3},{5,6},{6,5},{7,8},{8,7},{9,10},{10,9},{11,... | collective-permute-start | bytes 49160 | tf_op jit(solution)/shard_map/ppermute | solution.py:510
  76.0 0.6 collective-permute-start.23
  76.5 3.1 %collective-permute-done.23.refs_2_ = f32[8,128]{1,0:T(8,128)S(1)} collective-permute-done((f32[8,128]{1,0:T(8,128)S(1)}, f32[8,128]{1,0:T(8,128)S(1)}, u32[]{:S(2)}, u32[]{:S(2)}) %collective-permute-start.23) | collective-permute-done | bytes 4128 | tf_op jit(solution)/shard_map/ppermute | solution.py:514
  79.6 4.6 %end.3 = (f32[5,16,4096]{2,1,0:T(8,128)}, f32[16,4096]{1,0:T(8,128)}) custom-call(f32[32,128]{1,0:T(8,128)S(1)} %collective-permute-done.21.refs_0_, f32[32,128]{1,0:T(8,128)S(1)} %collective-permute-done.22.refs_1_, f32[8,128]{1,0:T(8,128)S(1)} %collective-permute-done.23.refs_2_, s32[8,128]{1,0:T(8,128)S(1)} %pad_add_fusion.refs_5_.refs_3_, ...), custom_call_target="tpu_custom_call" | custom-call | tf_op jit(solution)/shard_map/end/pallas_call | solution.py:579
  (41 shorter events, 3.7 us)
Async XLA Ops:
  0.6 11.1 %copy-start = (f32[2000,128]{1,0:T(8,128)S(1)}, f32[2000,128]{1,0:T(8,128)}, u32[]{:S(2)}) copy-start(f32[2000,128]{1,0:T(8,128)} %constant.2.clone.refs_6_.refs_8_.refs_7_) | copy-start | bytes 3072004
  0.6 1.4 %copy-start.1 = (f32[1,5,16,4096]{3,2,1,0:T(8,128)S(1)}, f32[1,5,16,4096]{3,2,1,0:T(8,128)}, u32[]{:S(2)}) copy-start(f32[1,5,16,4096]{3,2,1,0:T(8,128)} %param.4) | copy-start | bytes 3932164
  2.0 5.4 %copy-start.5 = (s32[1,1,1024]{2,1,0:T(1,128)S(1)}, s32[1,1,1024]{2,1,0:T(1,128)}, u32[]{:S(2)}) copy-start(s32[1,1,1024]{2,1,0:T(1,128)} %param.6) | copy-start | bytes 12292
  2.0 9.7 %copy-start.4 = (f32[1,16,4096]{2,1,0:T(8,128)S(1)}, f32[1,16,4096]{2,1,0:T(8,128)}, u32[]{:S(2)}) copy-start(f32[1,16,4096]{2,1,0:T(8,128)} %param.5) | copy-start | bytes 786436
  2.5 5.2 %collective-permute-start.2 = (f32[40,128]{1,0:T(8,128)S(1)}, f32[40,128]{1,0:T(8,128)S(1)}, u32[]{:S(2)}, u32[]{:S(2)}) collective-permute-start(f32[40,128]{1,0:T(8,128)S(1)} %get-tuple-element.43), channel_id=1, source_target_pairs={{0,16},{16,0},{1,17},{17,1},{2,18},{18,2},{3,19},{19,3},{4,20},{20... | collective-permute-start | bytes 61448 | tf_op jit(solution)/shard_map/ppermute | solution.py:514
  4.1 3.7 %collective-permute-start = (f32[320,128]{1,0:T(8,128)S(1)}, f32[320,128]{1,0:T(8,128)S(1)}, u32[]{:S(2)}, u32[]{:S(2)}) collective-permute-start(f32[320,128]{1,0:T(8,128)S(1)} %get-tuple-element.41), channel_id=1, source_target_pairs={{0,1},{1,0},{2,3},{3,2},{4,5},{5,4},{6,7},{7,6},{8,9},{9,8},{10,11... | collective-permute-start | bytes 491528 | tf_op jit(solution)/shard_map/ppermute | solution.py:510
  4.1 7.6 %collective-permute-start.1 = (f32[320,128]{1,0:T(8,128)S(1)}, f32[320,128]{1,0:T(8,128)S(1)}, u32[]{:S(2)}, u32[]{:S(2)}) collective-permute-start(f32[320,128]{1,0:T(8,128)S(1)} %get-tuple-element.42), channel_id=1, source_target_pairs={{1,2},{2,1},{3,4},{4,3},{5,6},{6,5},{7,8},{8,7},{9,10},{10,9},{11,... | collective-permute-start | bytes 491528 | tf_op jit(solution)/shard_map/ppermute | solution.py:510
  11.7 1.3 %copy-start.2 = (f32[1,5,16,4096]{3,2,1,0:T(8,128)S(1)}, f32[1,5,16,4096]{3,2,1,0:T(8,128)}, u32[]{:S(2)}) copy-start(f32[1,5,16,4096]{3,2,1,0:T(8,128)} %param.4) | copy-start | bytes 3932164
  18.6 7.9 %collective-permute-start.3 = (f32[32,128]{1,0:T(8,128)S(1)}, f32[32,128]{1,0:T(8,128)S(1)}, u32[]{:S(2)}, u32[]{:S(2)}) collective-permute-start(f32[32,128]{1,0:T(8,128)S(1)} %get-tuple-element.44), channel_id=1, source_target_pairs={{0,1},{1,0},{2,3},{3,2},{4,5},{5,4},{6,7},{7,6},{8,9},{9,8},{10,11... | collective-permute-start | bytes 49160 | tf_op jit(solution)/shard_map/ppermute | solution.py:510
  19.9 6.6 %collective-permute-start.4 = (f32[32,128]{1,0:T(8,128)S(1)}, f32[32,128]{1,0:T(8,128)S(1)}, u32[]{:S(2)}, u32[]{:S(2)}) collective-permute-start(f32[32,128]{1,0:T(8,128)S(1)} %get-tuple-element.45), channel_id=1, source_target_pairs={{1,2},{2,1},{3,4},{4,3},{5,6},{6,5},{7,8},{8,7},{9,10},{10,9},{11,... | collective-permute-start | bytes 49160 | tf_op jit(solution)/shard_map/ppermute | solution.py:510
  22.8 3.7 %collective-permute-start.5 = (f32[8,128]{1,0:T(8,128)S(1)}, f32[8,128]{1,0:T(8,128)S(1)}, u32[]{:S(2)}, u32[]{:S(2)}) collective-permute-start(f32[8,128]{1,0:T(8,128)S(1)} %get-tuple-element.46), channel_id=1, source_target_pairs={{0,16},{16,0},{1,17},{17,1},{2,18},{18,2},{3,19},{19,3},{4,20},{20... | collective-permute-start | bytes 12296 | tf_op jit(solution)/shard_map/ppermute | solution.py:514
  27.0 6.3 %collective-permute-start.6 = (f32[32,128]{1,0:T(8,128)S(1)}, f32[32,128]{1,0:T(8,128)S(1)}, u32[]{:S(2)}, u32[]{:S(2)}) collective-permute-start(f32[32,128]{1,0:T(8,128)S(1)} %get-tuple-element.49), channel_id=1, source_target_pairs={{0,1},{1,0},{2,3},{3,2},{4,5},{5,4},{6,7},{7,6},{8,9},{9,8},{10,11... | collective-permute-start | bytes 49160 | tf_op jit(solution)/shard_map/ppermute | solution.py:510
  27.0 6.2 %collective-permute-start.7 = (f32[32,128]{1,0:T(8,128)S(1)}, f32[32,128]{1,0:T(8,128)S(1)}, u32[]{:S(2)}, u32[]{:S(2)}) collective-permute-start(f32[32,128]{1,0:T(8,128)S(1)} %get-tuple-element.50), channel_id=1, source_target_pairs={{1,2},{2,1},{3,4},{4,3},{5,6},{6,5},{7,8},{8,7},{9,10},{10,9},{11,... | collective-permute-start | bytes 49160 | tf_op jit(solution)/shard_map/ppermute | solution.py:510
  29.6 3.7 %collective-permute-start.8 = (f32[8,128]{1,0:T(8,128)S(1)}, f32[8,128]{1,0:T(8,128)S(1)}, u32[]{:S(2)}, u32[]{:S(2)}) collective-permute-start(f32[8,128]{1,0:T(8,128)S(1)} %get-tuple-element.51), channel_id=1, source_target_pairs={{0,16},{16,0},{1,17},{17,1},{2,18},{18,2},{3,19},{19,3},{4,20},{20... | collective-permute-start | bytes 12296 | tf_op jit(solution)/shard_map/ppermute | solution.py:514
  33.8 7.1 %collective-permute-start.9 = (f32[32,128]{1,0:T(8,128)S(1)}, f32[32,128]{1,0:T(8,128)S(1)}, u32[]{:S(2)}, u32[]{:S(2)}) collective-permute-start(f32[32,128]{1,0:T(8,128)S(1)} %get-tuple-element.52), channel_id=1, source_target_pairs={{0,1},{1,0},{2,3},{3,2},{4,5},{5,4},{6,7},{7,6},{8,9},{9,8},{10,11... | collective-permute-start | bytes 49160 | tf_op jit(solution)/shard_map/ppermute | solution.py:510
  33.9 7.0 %collective-permute-start.10 = (f32[32,128]{1,0:T(8,128)S(1)}, f32[32,128]{1,0:T(8,128)S(1)}, u32[]{:S(2)}, u32[]{:S(2)}) collective-permute-start(f32[32,128]{1,0:T(8,128)S(1)} %get-tuple-element.53), channel_id=1, source_target_pairs={{1,2},{2,1},{3,4},{4,3},{5,6},{6,5},{7,8},{8,7},{9,10},{10,9},{11,... | collective-permute-start | bytes 49160 | tf_op jit(solution)/shard_map/ppermute | solution.py:510
  37.2 3.7 %collective-permute-start.11 = (f32[8,128]{1,0:T(8,128)S(1)}, f32[8,128]{1,0:T(8,128)S(1)}, u32[]{:S(2)}, u32[]{:S(2)}) collective-permute-start(f32[8,128]{1,0:T(8,128)S(1)} %get-tuple-element.54), channel_id=1, source_target_pairs={{0,16},{16,0},{1,17},{17,1},{2,18},{18,2},{3,19},{19,3},{4,20},{20... | collective-permute-start | bytes 12296 | tf_op jit(solution)/shard_map/ppermute | solution.py:514
  40.9 11.4 %copy-start.3 = (f32[1,5,16,4096]{3,2,1,0:T(8,128)S(1)}, f32[1,5,16,4096]{3,2,1,0:T(8,128)}, u32[]{:S(2)}) copy-start(f32[1,5,16,4096]{3,2,1,0:T(8,128)} %param.4) | copy-start | bytes 3932164
  44.6 6.5 %collective-permute-start.12 = (f32[320,128]{1,0:T(8,128)S(1)}, f32[320,128]{1,0:T(8,128)S(1)}, u32[]{:S(2)}, u32[]{:S(2)}) collective-permute-start(f32[320,128]{1,0:T(8,128)S(1)} %get-tuple-element.60), channel_id=1, source_target_pairs={{0,1},{1,0},{2,3},{3,2},{4,5},{5,4},{6,7},{7,6},{8,9},{9,8},{10,11... | collective-permute-start | bytes 491528 | tf_op jit(solution)/shard_map/ppermute | solution.py:510
  44.7 7.6 %collective-permute-start.13 = (f32[320,128]{1,0:T(8,128)S(1)}, f32[320,128]{1,0:T(8,128)S(1)}, u32[]{:S(2)}, u32[]{:S(2)}) collective-permute-start(f32[320,128]{1,0:T(8,128)S(1)} %get-tuple-element.61), channel_id=1, source_target_pairs={{1,2},{2,1},{3,4},{4,3},{5,6},{6,5},{7,8},{8,7},{9,10},{10,9},{11,... | collective-permute-start | bytes 491528 | tf_op jit(solution)/shard_map/ppermute | solution.py:510
  47.2 3.8 %collective-permute-start.14 = (f32[40,128]{1,0:T(8,128)S(1)}, f32[40,128]{1,0:T(8,128)S(1)}, u32[]{:S(2)}, u32[]{:S(2)}) collective-permute-start(f32[40,128]{1,0:T(8,128)S(1)} %get-tuple-element.62), channel_id=1, source_target_pairs={{0,16},{16,0},{1,17},{17,1},{2,18},{18,2},{3,19},{19,3},{4,20},{20... | collective-permute-start | bytes 61448 | tf_op jit(solution)/shard_map/ppermute | solution.py:514
  57.9 7.2 %collective-permute-start.15 = (f32[32,128]{1,0:T(8,128)S(1)}, f32[32,128]{1,0:T(8,128)S(1)}, u32[]{:S(2)}, u32[]{:S(2)}) collective-permute-start(f32[32,128]{1,0:T(8,128)S(1)} %get-tuple-element.63), channel_id=1, source_target_pairs={{0,1},{1,0},{2,3},{3,2},{4,5},{5,4},{6,7},{7,6},{8,9},{9,8},{10,11... | collective-permute-start | bytes 49160 | tf_op jit(solution)/shard_map/ppermute | solution.py:510
  59.2 5.9 %collective-permute-start.16 = (f32[32,128]{1,0:T(8,128)S(1)}, f32[32,128]{1,0:T(8,128)S(1)}, u32[]{:S(2)}, u32[]{:S(2)}) collective-permute-start(f32[32,128]{1,0:T(8,128)S(1)} %get-tuple-element.64), channel_id=1, source_target_pairs={{1,2},{2,1},{3,4},{4,3},{5,6},{6,5},{7,8},{8,7},{9,10},{10,9},{11,... | collective-permute-start | bytes 49160 | tf_op jit(solution)/shard_map/ppermute | solution.py:510
  61.5 3.7 %collective-permute-start.17 = (f32[8,128]{1,0:T(8,128)S(1)}, f32[8,128]{1,0:T(8,128)S(1)}, u32[]{:S(2)}, u32[]{:S(2)}) collective-permute-start(f32[8,128]{1,0:T(8,128)S(1)} %get-tuple-element.65), channel_id=1, source_target_pairs={{0,16},{16,0},{1,17},{17,1},{2,18},{18,2},{3,19},{19,3},{4,20},{20... | collective-permute-start | bytes 12296 | tf_op jit(solution)/shard_map/ppermute | solution.py:514
  65.7 6.9 %collective-permute-start.18 = (f32[32,128]{1,0:T(8,128)S(1)}, f32[32,128]{1,0:T(8,128)S(1)}, u32[]{:S(2)}, u32[]{:S(2)}) collective-permute-start(f32[32,128]{1,0:T(8,128)S(1)} %get-tuple-element.68), channel_id=1, source_target_pairs={{0,1},{1,0},{2,3},{3,2},{4,5},{5,4},{6,7},{7,6},{8,9},{9,8},{10,11... | collective-permute-start | bytes 49160 | tf_op jit(solution)/shard_map/ppermute | solution.py:510
  65.8 6.9 %collective-permute-start.19 = (f32[32,128]{1,0:T(8,128)S(1)}, f32[32,128]{1,0:T(8,128)S(1)}, u32[]{:S(2)}, u32[]{:S(2)}) collective-permute-start(f32[32,128]{1,0:T(8,128)S(1)} %get-tuple-element.69), channel_id=1, source_target_pairs={{1,2},{2,1},{3,4},{4,3},{5,6},{6,5},{7,8},{8,7},{9,10},{10,9},{11,... | collective-permute-start | bytes 49160 | tf_op jit(solution)/shard_map/ppermute | solution.py:510
  69.0 3.7 %collective-permute-start.20 = (f32[8,128]{1,0:T(8,128)S(1)}, f32[8,128]{1,0:T(8,128)S(1)}, u32[]{:S(2)}, u32[]{:S(2)}) collective-permute-start(f32[8,128]{1,0:T(8,128)S(1)} %get-tuple-element.70), channel_id=1, source_target_pairs={{0,16},{16,0},{1,17},{17,1},{2,18},{18,2},{3,19},{19,3},{4,20},{20... | collective-permute-start | bytes 12296 | tf_op jit(solution)/shard_map/ppermute | solution.py:514
  73.1 6.5 %collective-permute-start.21 = (f32[32,128]{1,0:T(8,128)S(1)}, f32[32,128]{1,0:T(8,128)S(1)}, u32[]{:S(2)}, u32[]{:S(2)}) collective-permute-start(f32[32,128]{1,0:T(8,128)S(1)} %get-tuple-element.71), channel_id=1, source_target_pairs={{0,1},{1,0},{2,3},{3,2},{4,5},{5,4},{6,7},{7,6},{8,9},{9,8},{10,11... | collective-permute-start | bytes 49160 | tf_op jit(solution)/shard_map/ppermute | solution.py:510
  73.2 6.4 %collective-permute-start.22 = (f32[32,128]{1,0:T(8,128)S(1)}, f32[32,128]{1,0:T(8,128)S(1)}, u32[]{:S(2)}, u32[]{:S(2)}) collective-permute-start(f32[32,128]{1,0:T(8,128)S(1)} %get-tuple-element.72), channel_id=1, source_target_pairs={{1,2},{2,1},{3,4},{4,3},{5,6},{6,5},{7,8},{8,7},{9,10},{10,9},{11,... | collective-permute-start | bytes 49160 | tf_op jit(solution)/shard_map/ppermute | solution.py:510
  76.0 3.7 %collective-permute-start.23 = (f32[8,128]{1,0:T(8,128)S(1)}, f32[8,128]{1,0:T(8,128)S(1)}, u32[]{:S(2)}, u32[]{:S(2)}) collective-permute-start(f32[8,128]{1,0:T(8,128)S(1)} %get-tuple-element.73), channel_id=1, source_target_pairs={{0,16},{16,0},{1,17},{17,1},{2,18},{18,2},{3,19},{19,3},{4,20},{20... | collective-permute-start | bytes 12296 | tf_op jit(solution)/shard_map/ppermute | solution.py:514

commit v3 on v2

v3 whole, which is shorter than its diff:
```python
import functools
import math

import jax
import jax.numpy as jnp
import numpy as np
from jax import lax
from jax.experimental import pallas as pl
from jax.experimental.pallas import tpu as pltpu
from jax.sharding import PartitionSpec as P

NX = 64
NY = 64
FIELDS = 5
SECTIONS = 2
ITERS = 3

COURANT = 0.1
DIFFUSION = 0.05
STOICHIOMETRY = 2.0
EXPANSION = 1.0

LANES = 128
HALF = NY
TILES = NX // 2
ROWS = 32
ZERO_ROW = 8
F32 = jnp.float32
BF16 = jnp.bfloat16
UNROLL = 16
MIB = 1 << 20
MICROSECOND = 8_000_000


def sine(n):
    i = np.arange(n, dtype=np.float64) + 1
    return np.sqrt(2.0 / (n + 1)) * np.sin(np.pi * i[:, None] * i[None, :] / (n + 1))


def modes(n):
    i = np.arange(n, dtype=np.float64) + 1
    return 2.0 - 2.0 * np.cos(np.pi * i / (n + 1))


def both(low, high):
    return np.concatenate([np.broadcast_to(low, low.shape[:-1] + (HALF,)), np.broadcast_to(high, high.shape[:-1] + (HALF,))], axis=-1)


def split(table):
    table = np.asarray(table, np.float32)
    high = table.astype(BF16)
    low = (table - high.astype(np.float32)).astype(BF16)
    return high, low


def tables(height):
    sz, sx, sy = sine(height), sine(NX), sine(NY)
    lz, lx, ly = modes(height), modes(NX), modes(NY)
    half = height // 2
    coef = both(sz[0::2, :half, None], sz[1::2, :half, None])
    edge = coef[:, 0]
    lam = lx[None, :, None] + both(lz[0::2, None, None], lz[1::2, None, None]) + np.concatenate([ly, ly])[None, None, :]
    inv = 1.0 / lam
    cross = edge[:, None, :] * sx[:, 0][None, :, None] * inv
    diag_z = (edge[:, None, :] ** 2 * inv).sum(0)
    diag_x = (sx[:, 0][None, :, None] ** 2 * inv).sum(1)
    order = np.concatenate([np.arange(0, NX, 2), np.arange(1, NX, 2)])
    fwd_hi, fwd_lo = split(sx[:, order])
    bwd_hi, bwd_lo = split(sx[order, :])
    ky = np.kron(np.eye(2), sy)
    ky_hi, ky_lo = split(ky)
    to_a = np.zeros((half, half, LANES))
    to_b = np.zeros((half, half, LANES))
    from_a = np.zeros((half, half, LANES))
    from_b = np.zeros((half, half, LANES))
    for r in range(half):
        to_a[r] = both(sz[0::2, r][:, None], sz[1::2, half + r][:, None])
        to_b[r] = both(sz[0::2, half + r][:, None], sz[1::2, r][:, None])
        from_a[r] = both(sz[2 * r, :half][:, None], sz[2 * r + 1, half:][:, None])
        from_b[r] = both(sz[2 * r + 1, :half][:, None], sz[2 * r, half:][:, None])
    hi = lambda high, low: np.concatenate([high, high, low, np.zeros_like(low)], axis=1)
    wide = lambda m: np.concatenate([m[:, :LANES], m[:, LANES:]], axis=0)
    parts = dict(
        coef=coef.reshape(half * half, LANES),
        inv=inv.reshape(half * NX, LANES),
        cross=cross.reshape(half * NX, LANES),
        diag_z=diag_z,
        diag_x=diag_x,
        col_x=np.broadcast_to(sx[:, :1], (NX, LANES)),
        edge=edge,
        fwd=wide(hi(fwd_hi, fwd_lo)),
        bwd=wide(hi(bwd_hi, bwd_lo)),
        ky_hi=ky_hi,
        ky_lo=ky_lo,
        plane=np.stack([to_a, to_b, from_a, from_b]).reshape(4 * half * half, LANES),
    )
    places, at = {}, 0
    for name, part in parts.items():
        places[name] = (at, at + part.shape[0])
        at += part.shape[0]
    return np.concatenate([np.asarray(p, np.float32) for p in parts.values()], axis=0), places


class Tables:
    def __init__(self, ref, places):
        self.ref, self.places = ref, places

    def __getitem__(self, name):
        first, last = self.places[name]
        return self.ref[first:last]

    def row(self, name, i):
        first = self.places[name][0] + i
        return self.ref[first : first + 1]

    def block(self, name, i, n):
        first = self.places[name][0] + i * n
        return self.ref[first : first + n]

    def wide(self, name):
        both_halves = self[name].astype(BF16)
        n = both_halves.shape[0] // 2
        return jnp.concatenate([both_halves[:n], both_halves[n:]], axis=1)


def lower_half(shape):
    return lax.broadcasted_iota(jnp.int32, shape, len(shape) - 1) < HALF


def swap_halves(v):
    return pltpu.roll(v, HALF, axis=v.ndim - 1)


def hi_lo(v):
    high = v.astype(BF16)
    return high, (v - high.astype(F32)).astype(BF16)


def y_transform(v, tab):
    high, low = hi_lo(v)
    table = tab["ky_hi"].astype(BF16)
    return jnp.dot(
        jnp.concatenate([high, low], axis=1), jnp.concatenate([table, table], axis=0), preferred_element_type=F32
    ) + jnp.dot(high, tab["ky_lo"].astype(BF16), preferred_element_type=F32)


def x_transform(table, v):
    high, low = hi_lo(v)
    return jnp.dot(table, jnp.concatenate([high, low, high, jnp.zeros_like(high)], axis=0), preferred_element_type=F32)


def mix_rows(v, tab, first):
    swapped = swap_halves(v)
    half = v.shape[0]
    out = jnp.zeros_like(v)
    for r in range(half):
        a = tab.block("plane", first * half + r, half)
        b = tab.block("plane", (first + 1) * half + r, half)
        out = out + a * v[r : r + 1] + b * swapped[r : r + 1]
    return out


def gather(plane, mapping):
    half = plane.shape[0]
    bits = int(math.log2(half))
    ybits = int(math.log2(NY))
    row = (mapping >> ybits) & (half - 1)
    lane = ((mapping >> (ybits + bits)) << ybits) | (mapping & (NY - 1))
    out = jnp.zeros_like(plane)
    for r in range(half):
        source = jnp.broadcast_to(plane[r : r + 1], plane.shape)
        out = jnp.where(row == r, jnp.take_along_axis(source, lane, axis=1), out)
    return out


def position():
    is_fine = lax.axis_index("grp") == 0
    even = lax.rem(lax.axis_index("mesh"), 2) == 0
    return is_fine, even


def row_sign(is_fine, shape):
    odd = lax.rem(lax.broadcasted_iota(jnp.int32, shape, 0), 2) == 1
    return jnp.where(jnp.logical_and(odd, is_fine), -1.0, 1.0).astype(F32)


def pack_trace(full):
    n = full.shape[0] // 2
    return jnp.where(lower_half((n, LANES)), full[:n], full[n:])


def unpack_trace(packed):
    swapped = swap_halves(packed)
    low = lower_half(packed.shape)
    return jnp.concatenate([jnp.where(low, packed, swapped), jnp.where(low, swapped, packed)], axis=0)


def send_traces(u, even, to_even, to_odd):
    other = swap_halves(u)
    low = lower_half(u.shape)
    evens = jnp.where(low, u, other)
    odds = jnp.where(low, other, u)
    sign = jnp.where(even, 1.0, -1.0).astype(F32)
    to_even[...] = pack_trace(evens - sign * odds)
    to_odd[...] = pack_trace(evens + sign * odds)


def ghost_low_high(from_even, from_odd, even):
    a, b = unpack_trace(from_even[...]), unpack_trace(from_odd[...])
    return jnp.where(even, b, a), jnp.where(even, a, b)


def send_plane(y, tab, plane_out):
    plane_out[...] = mix_rows(y_transform(y, tab), tab, 2)


def x_ghost_tiles(ghost, is_fine):
    swapped = swap_halves(ghost)
    west = jnp.concatenate([swapped, ghost], axis=0)
    east = jnp.concatenate([ghost, swapped], axis=0)
    zero = jnp.zeros_like(west)
    return jnp.where(is_fine, zero, west), jnp.where(is_fine, east, zero)


def east_west(centre, before, after, low):
    east = swap_halves(jnp.where(low, after, centre))
    west = swap_halves(jnp.where(low, centre, before))
    return east, west


def north_south(centre):
    y = lax.broadcasted_iota(jnp.int32, centre.shape, 1) & (NY - 1)
    north = jnp.where(y == NY - 1, 0.0, pltpu.roll(centre, LANES - 1, axis=1))
    south = jnp.where(y == 0, 0.0, pltpu.roll(centre, 1, axis=1))
    return north, south


def strided(first, count, stride):
    return pl.ds(first, count, stride=stride)


def tile_lanes(t):
    return pl.ds(pl.multiple_of(t * LANES, LANES), LANES)


def pack_planes(state, planes, half, is_fine):
    low = lower_half((half, LANES))
    for f in range(FIELDS):
        first = state[f, :, 0:LANES]
        last = state[f, :, (TILES - 1) * LANES : TILES * LANES]
        fine = jnp.where(low, swap_halves(last[:half]), last[half:])
        coarse = jnp.where(low, first[:half], swap_halves(first[half:]))
        planes[f * half : (f + 1) * half] = jnp.where(is_fine, fine, coarse)


def pack_layers(value, f, t, height, even, to_even, to_odd):
    for k in range(2):
        bottom = value[k : k + 1]
        top = value[height - 2 + k : height - 1 + k]
        row = pl.ds((2 * f + k) * TILES + t, 1)
        to_even[row] = jnp.where(even, top, bottom)
        to_odd[row] = jnp.where(even, bottom, top)


def pack_kernel(height, state, to_even, to_odd, planes):
    is_fine, even = position()
    pack_planes(state, planes, height // 2, is_fine)

    def tile(t, _):
        for f in range(FIELDS):
            pack_layers(state[f, :, tile_lanes(t)], f, t, height, even, to_even, to_odd)
        return 0

    lax.fori_loop(0, TILES, tile, 0, unroll=UNROLL)


def z_mix(src, dst, tab, half, inverse):
    def chunk(r, _):
        rows = pl.ds(pl.multiple_of(r * 8, 8), 8)
        parts = [src[j, rows] for j in range(half)]
        for i in range(half):
            total = None
            for j in range(half):
                k = j * half + i if inverse else i * half + j
                term = tab.row("coef", k) * parts[j]
                total = term if total is None else total + term
            dst[i, rows] = total
        return 0

    lax.fori_loop(0, NX // 8, chunk, 0, unroll=8)


def base_kernel(height, places, current, burn, table, pad_a, pad_b, spectrum, trace, facet, source, folded, mixed):
    tab = Tables(table, places)
    is_fine, _ = position()
    half = height // 2
    tile_low = lower_half((height, LANES))
    z = lax.broadcasted_iota(jnp.int32, (height, LANES), 0)

    def tile(t, _):
        lanes = tile_lanes(t)
        row = pl.ds(pl.multiple_of((t + 1) * ROWS + ZERO_ROW, 8), height)
        u, v, w, fuel, oxygen = [current[f, :, lanes] for f in range(FIELDS)]
        pad_a[0, row], pad_a[1, row], pad_a[2, row] = u, v, w
        pad_b[0, row], pad_b[1, row] = fuel, oxygen
        before = jnp.where(t == 0, 0.0, current[0, :, tile_lanes(jnp.maximum(t - 1, 0))])
        after = jnp.where(t == TILES - 1, 0.0, current[0, :, tile_lanes(jnp.minimum(t + 1, TILES - 1))])
        east, west = east_west(u, before, after, tile_low)
        north, south = north_south(v)
        above = jnp.where(z == height - 1, 0.0, pltpu.roll(w, height - 1, axis=0))
        below = jnp.where(z == 0, 0.0, pltpu.roll(w, 1, axis=0))
        reaction = burn[:, lanes] * fuel * oxygen
        divergence = (east - west) + (north - south) + (above - below)
        source[pl.ds(pl.multiple_of(t * height, height), height)] = EXPANSION * reaction - 0.5 * divergence
        return 0

    lax.fori_loop(0, TILES, tile, 0, unroll=UNROLL)

    low = lower_half((TILES, LANES))
    for q in range(half):
        a = source[strided(q, TILES, height)]
        b = source[strided(height - 1 - q, TILES, height)]
        total, delta = a + b, a - b
        folded[q, 0:TILES] = jnp.where(low, total, swap_halves(delta))
        folded[q, TILES : 2 * TILES] = jnp.where(low, swap_halves(total), delta)

    z_mix(folded, mixed, tab, half, False)
    wide = jnp.concatenate([mixed[p] for p in range(half)], axis=1)
    wide = x_transform(tab.wide("fwd"), wide)
    tall = jnp.concatenate([wide[:, p * LANES : (p + 1) * LANES] for p in range(half)], axis=0)
    mixed[...] = y_transform(tall, tab).reshape(half, NX, LANES)

    column = tab["col_x"] * row_sign(is_fine, (NX, LANES))
    u0 = jnp.zeros((NX, LANES), F32)
    for p in range(half):
        solved = mixed[p] * tab.block("inv", p, NX)
        spectrum[p] = solved
        u0 = u0 + tab.row("edge", p) * solved
        facet[p : p + 1] = jnp.sum(column * solved, axis=0, keepdims=True)
    trace[...] = u0


def ghost_modes(plane, mapping, tab):
    return y_transform(mix_rows(gather(plane, mapping), tab, 0), tab)


def respond(layers, side, trace, facet, cross_rows, tab, half, is_fine):
    sign = row_sign(is_fine, (NX, LANES))
    signed = sign * layers
    cross_sum = jnp.zeros((NX, LANES), F32)
    for p in range(half):
        cross = tab.block("cross", p, NX)
        cross_sum = cross_sum + cross * side[p : p + 1]
        cross_rows[p : p + 1] = jnp.sum(cross * signed, axis=0, keepdims=True)
    u = trace[...] + tab["diag_z"] * layers + sign * cross_sum
    return u, facet[...] + tab["diag_x"] * side + cross_rows[...]


def add_kernel(height, places, from_even, from_odd, planes, mapping, trace, facet, table, *outs):
    layers_out, side_out, trace_out, facet_out, to_even, to_odd, plane_out, cross_rows = outs
    tab = Tables(table, places)
    is_fine, even = position()
    half = height // 2
    first = slice(2 * 2 * TILES, (2 * 2 + 1) * TILES)
    second = slice((2 * 2 + 1) * TILES, (2 * 2 + 2) * TILES)
    below = jnp.where(even, from_odd[second], from_even[second])
    above = jnp.where(even, from_even[first], from_odd[first])
    low = lower_half((TILES, LANES))
    pair = jnp.concatenate(
        [jnp.where(low, below, swap_halves(above)), jnp.where(low, swap_halves(below), above)], axis=0
    )
    pair = y_transform(x_transform(tab.wide("fwd"), pair), tab)
    other = swap_halves(pair)
    layers = 0.5 * jnp.where(lower_half((NX, LANES)), pair - other, pair + other)
    side = jnp.where(is_fine, -0.5, 0.5).astype(F32) * ghost_modes(planes[0:half], mapping[...], tab)
    u, y = respond(layers, side, trace, facet, cross_rows, tab, half, is_fine)
    layers_out[...] = layers
    side_out[...] = side
    trace_out[...] = u
    facet_out[...] = y
    send_traces(u, even, to_even, to_odd)
    send_plane(y, tab, plane_out)


def step_kernel(height, places, last, *refs):
    from_even, from_odd, plane_in, mapping, trace, facet, table, *outs = refs
    cross_rows = outs.pop()
    tab = Tables(table, places)
    to_even, to_odd, plane_out = outs[-3:]
    is_fine, even = position()
    half = height // 2
    low_ghost, high_ghost = ghost_low_high(from_even, from_odd, even)
    layers = jnp.where(lower_half((NX, LANES)), low_ghost + high_ghost, low_ghost - high_ghost)
    side = ghost_modes(plane_in[...], mapping[...], tab)
    if last:
        outs[0][...] = layers
        outs[1][...] = side
    u, y = respond(layers, side, trace, facet, cross_rows, tab, half, is_fine)
    send_traces(u, even, to_even, to_odd)
    send_plane(y, tab, plane_out)


def tend_kernel(height, fields, second, *refs):
    refs = list(refs)
    pad_in, current, burn, from_even, from_odd, planes, mapping = refs[:7]
    initial = refs[7] if second else None
    predicted, pad = refs[-2:]
    is_fine, even = position()
    half = height // 2
    tile_low = lower_half((height, LANES))
    tiled = pad.reshape(len(fields), TILES + 2, ROWS, LANES)
    for i, f in enumerate(fields):
        ghost = gather(planes[f * half : (f + 1) * half], mapping[...])
        west, east = x_ghost_tiles(ghost, is_fine)
        pad[i, ZERO_ROW : ZERO_ROW + height] = west
        last = (TILES + 1) * ROWS + ZERO_ROW
        pad[i, last : last + height] = east
        for k in range(2):
            rows = slice((2 * f + k) * TILES, (2 * f + k + 1) * TILES)
            below = jnp.where(even, from_odd[rows], from_even[rows])
            above = jnp.where(even, from_even[rows], from_odd[rows])
            pad[i, strided(ROWS + ZERO_ROW - 2 + k, TILES, ROWS)] = below
            pad[i, strided(ROWS + ZERO_ROW + height + k, TILES, ROWS)] = above

    def tile(t, _):
        lanes = tile_lanes(t)

        def at(i, dz=0, dt=0):
            return tiled[i, t + 1 + dt, ZERO_ROW + dz : ZERO_ROW + dz + height]

        cu = current[0, :, lanes] * (-0.5 * COURANT)
        cv = current[1, :, lanes] * (-0.5 * COURANT)
        cw = current[2, :, lanes] * (-COURANT / 12.0)
        if 3 in fields:
            reaction = burn[:, lanes] * current[3, :, lanes] * current[4, :, lanes]
        for i, f in enumerate(fields):
            centre = at(i)
            east, west = east_west(centre, at(i, 0, -1), at(i, 0, 1), tile_low)
            north, south = north_south(centre)
            above, below = at(i, 1), at(i, -1)
            above_two, below_two = at(i, 2), at(i, -2)
            dz = above - below
            change = cu * (east - west) + cv * (north - south) + cw * (8.0 * dz - (above_two - below_two))
            change = change + DIFFUSION * ((east + west) + (north + south) + (above + below) - 6.0 * centre)
            if f == 3:
                change = change - reaction
            if f == 4:
                change = change - STOICHIOMETRY * reaction
            if second:
                predicted[i, :, lanes] = 0.5 * (initial[f, :, lanes] + centre + change)
            else:
                predicted[i, :, lanes] = centre + change
        return 0

    lax.fori_loop(0, TILES, tile, 0, unroll=UNROLL)


def unfold(v):
    low = lower_half((TILES, LANES))
    top, bottom = v[:TILES], v[TILES:]
    return jnp.where(low, top, swap_halves(bottom)), jnp.where(low, swap_halves(top), bottom)


def inverse_kernel(height, places, spectrum, layers_a, side_a, layers_b, side_b, table, pad, tall, mixed, unmixed):
    tab = Tables(table, places)
    is_fine, _ = position()
    half = height // 2
    column = tab["col_x"] * row_sign(is_fine, (NX, LANES))
    layers = layers_a[...] + layers_b[...]
    side = side_a[...] + side_b[...]
    for p in range(half):
        push = tab.row("edge", p) * layers + column * side[p : p + 1]
        tall[p * NX : (p + 1) * NX] = spectrum[p] + push * tab.block("inv", p, NX)
    cells = y_transform(tall[...], tab)
    wide = jnp.concatenate([cells[p * NX : (p + 1) * NX] for p in range(half)], axis=1)
    wide = x_transform(tab.wide("bwd"), wide)
    for p in range(half):
        mixed[p] = wide[:, p * LANES : (p + 1) * LANES]
    z_mix(mixed, unmixed, tab, half, True)
    first = ROWS + ZERO_ROW
    for q in range(half):
        evens, odds = unfold(unmixed[q])
        pad[strided(first + q, TILES, ROWS)] = evens + odds
        pad[strided(first + height - 1 - q, TILES, ROWS)] = evens - odds


def correct_kernel(height, places, final, *refs):
    refs = list(refs)
    from_even, from_odd, plane_in, mapping, pad_in, flow, scalars, table = refs[:8]
    pad = refs[-1]
    state = refs[8]
    is_fine, even = position()
    half = height // 2
    tab = Tables(table, places)
    low_ghost, high_ghost = ghost_low_high(from_even, from_odd, even)
    pair = jnp.where(lower_half((NX, LANES)), low_ghost, high_ghost)
    below, above = unfold(x_transform(tab.wide("bwd"), y_transform(pair, tab)))
    first = ROWS + ZERO_ROW
    pad[strided(first - 1, TILES, ROWS)] = below
    pad[strided(first + height, TILES, ROWS)] = above
    west, east = x_ghost_tiles(gather(plane_in[...], mapping[...]), is_fine)
    pad[ZERO_ROW : ZERO_ROW + height] = west
    last = (TILES + 1) * ROWS + ZERO_ROW
    pad[last : last + height] = east
    tile_low = lower_half((height, LANES))
    tiled = pad.reshape(TILES + 2, ROWS, LANES)

    def tile(t, _):
        lanes = tile_lanes(t)

        def at(dz=0, dt=0):
            return tiled[t + 1 + dt, ZERO_ROW + dz : ZERO_ROW + dz + height]

        centre = at()
        east, west = east_west(centre, at(0, -1), at(0, 1), tile_low)
        north, south = north_south(centre)
        slopes = (east - west, north - south, at(1) - at(-1))
        for f in range(FIELDS):
            if f < 3:
                value = flow[f, :, lanes] - 0.5 * slopes[f]
            else:
                value = scalars[f - 3, :, lanes]
            state[f, :, lanes] = value
            if not final:
                pack_layers(value, f, t, height, even, refs[9], refs[10])
        if final:
            refs[9][:, lanes] = centre
        return 0

    lax.fori_loop(0, TILES, tile, 0, unroll=UNROLL)
    if not final:
        pack_planes(state, refs[11], half, is_fine)


def swap_pairs(x, parity):
    count = lax.axis_size("mesh")
    route = []
    for low in range(parity, count - 1, 2):
        route += [(low, low + 1), (low + 1, low)]
    return lax.ppermute(x, "mesh", route)


def swap_partner(x):
    return lax.ppermute(x, "grp", [(0, 1), (1, 0)])


def exchange(to_even, to_odd, plane):
    return swap_pairs(to_even, 0), swap_pairs(to_odd, 1), swap_partner(plane)


def call(body, outs, scratch, name, mib, cost, aliases=None):
    return pl.pallas_call(
        body,
        out_shape=outs,
        scratch_shapes=[pltpu.VMEM(s, F32) for s in scratch],
        input_output_aliases=aliases or {},
        compiler_params=pltpu.CompilerParams(vmem_limit_bytes=mib * MIB),
        cost_estimate=pl.CostEstimate(flops=int(cost * MICROSECOND), bytes_accessed=0, transcendentals=0),
        name=name,
    )


def shards(state, burn_rate, face_map):
    height = state.shape[2]
    half = height // 2
    cells = NX * NY
    table, places = tables(height)
    table = jnp.asarray(table)
    shape = lambda *s: jax.ShapeDtypeStruct(s, F32)
    bind = functools.partial
    halo = shape(2 * FIELDS * TILES, LANES)
    packed = shape(NX // 2, LANES)
    plane = shape(half, LANES)
    planes_shape = shape(FIELDS * half, LANES)
    layer = shape(NX, LANES)
    spectral = shape(half, NX, LANES)
    padded = lambda *n: shape(*n, (TILES + 2) * ROWS, LANES)
    initial = state[0]
    burning = burn_rate[0]
    by_row = face_map[0, 0].reshape(height, NY)
    mapping = jnp.concatenate([by_row[:half], by_row[half:]], axis=1)
    groups = ((0, 1, 2), (3, 4))

    packets = call(bind(pack_kernel, height), (halo, halo, planes_shape), (), "pack", 8, 0.5)(initial)
    current = initial
    for section in range(SECTIONS):
        second = section > 0
        final = section == SECTIONS - 1
        halos = exchange(*packets)
        *pads, spectrum, trace, facet = call(
            bind(base_kernel, height, places),
            (padded(3), padded(2), spectral, layer, plane),
            ((TILES * height, LANES), (half, NX, LANES), (half, NX, LANES)),
            "base",
            16,
            3,
        )(current, burning, table)
        layers_a, side_a, trace, facet, *packets = call(
            bind(add_kernel, height, places),
            (layer, plane, layer, plane, packed, packed, plane),
            ((half, LANES),),
            "add",
            4,
            1,
        )(*halos, mapping, trace, facet, table)
        predicted = [
            call(
                bind(tend_kernel, height, fields, second),
                (shape(len(fields), height, cells), padded(len(fields))),
                (),
                "tend",
                16,
                2,
                {0: 1},
            )(pad, current, burning, *halos, mapping, *((initial,) if second else ()))[0]
            for fields, pad in zip(groups, pads)
        ]
        for sweep in range(ITERS - 1):
            last = sweep == ITERS - 2
            received = exchange(*packets)
            if sweep < len(predicted):
                received, predicted[sweep] = lax.optimization_barrier((received, predicted[sweep]))
            *kept, to_even, to_odd, plane_out = call(
                bind(step_kernel, height, places, last),
                ((layer, plane) if last else ()) + (packed, packed, plane),
                ((half, LANES),),
                "step",
                4,
                0.5,
            )(*received, mapping, trace, facet, table)
            packets = (to_even, to_odd, plane_out)
        received = exchange(*packets)
        pressure = call(
            bind(inverse_kernel, height, places),
            padded(),
            ((half * NX, LANES), (half, NX, LANES), (half, NX, LANES)),
            "inverse",
            8,
            2,
        )(spectrum, layers_a, side_a, *kept, table)
        current, *packets = call(
            bind(correct_kernel, height, places, final),
            (shape(FIELDS, height, cells),) + ((shape(height, cells),) if final else (halo, halo, planes_shape)) + (padded(),),
            (),
            "correct",
            16,
            2,
            {4: 2 if final else 4},
        )(*received, mapping, pressure, *predicted, table)
        packets = packets[:-1]
    return current[None], packets[0][None]


def solution(mesh):
    placed = (P("grp", None, "mesh", None), P("grp", "mesh", None), P("grp", "mesh", None))
    return jax.shard_map(
        shards,
        mesh=mesh,
        in_specs=placed,
        out_specs=(P("grp", None, "mesh", None), P("grp", "mesh", None)),
        check_vma=False,
    )
```

time: 84.6 us -> 67.4 us (0.80)
  waiting for transfers between devices: 27.1 us -> 8.12 us
  starting transfers between devices: 31.5 us -> 40.2 us
  Pallas kernels: 21.9 us -> 14.8 us
    ppermute x8, waiting for transfers between devices: 21.9 us -> 7.74 us  [swap_partner(): return lax.ppermute(x, 'grp', [(0, 1), (1, 0)])]
    pallas_call x9 -> x17, Pallas kernels: 21.9 us -> 14.8 us  [the longest x4 4.47 us: shards(): call(bind(tend_kernel, height, fields, second), (shape(len(fields), heigh...]
    ppermute x8, starting transfers between devices: 5.59 us -> 12.6 us  [swap_partner(): return lax.ppermute(x, 'grp', [(0, 1), (1, 0)])]
    ppermute x16, waiting for transfers between devices: 5.23 us -> 0.38 us  [swap_pairs(): return lax.ppermute(x, 'mesh', route)]
    ppermute x16, starting transfers between devices: 25.9 us -> 27.6 us  [swap_pairs(): return lax.ppermute(x, 'mesh', route)]
  transfers between devices with their start and end apart: 24 -> 24, of which waited for: 9 -> 8; matrix products, arithmetic and copies ran while one was open for 0% -> 0% of each run, Pallas kernels for 0% -> 12%
where the time goes in v3:
time: 67.4 us; the launch traced here: 67 us
  starting transfers between devices  40.2 us (60%)
  Pallas kernels  14.8 us (22%)
  waiting for transfers between devices  8.12 us (12%)
  local copies, waits for them, and re-layouts  2.91 us (4%)
  between operations  0.91 us (1%)
    ppermute x16, starting transfers between devices, swap_pairs(): return lax.ppermute(x, 'mesh', route)  27.6 us
    ppermute x8, starting transfers between devices, swap_partner(): return lax.ppermute(x, 'grp', [(0, 1), (1, 0)])  12.6 us
    ppermute x8, waiting for transfers between devices, swap_partner(): return lax.ppermute(x, 'grp', [(0, 1), (1, 0)])  7.74 us
    pallas_call x4, Pallas kernels, shards(): call(bind(tend_kernel, height, fields, second), (shape(len(fields), heigh...  4.47 us
    pallas_call x2, Pallas kernels, shards(): call(bind(correct_kernel, height, places, final), (shape(FIELDS, height,...  3.01 us
    unnamed x12, local copies, waits for them, and re-layouts  2.74 us
    pallas_call x2, Pallas kernels, shards(): call(bind(base_kernel, height, places), (padded(3), padded(2), spectral,...  2.22 us
    pallas_call x4, Pallas kernels, shards(): call(bind(step_kernel, height, places, last), ((layer, plane) if last els...  1.99 us
  transfers between devices with their start and end apart: 24, of which 8 were waited for; matrix products, arithmetic and copies ran while one was open for 0% of the time, Pallas kernels for 12%

profile of v3, /device:TPU:24, one launch (start us, length us, event | category | flops | bytes accessed | tf_op | source)
XLA Modules:
  0.0 67.0 jit_solution(5121270332876307831)
XLA Ops:
  0.7 1.4 %copy-done.1 = f32[1,5,16,4096]{3,2,1,0:T(8,128)S(1)} copy-done((f32[1,5,16,4096]{3,2,1,0:T(8,128)S(1)}, f32[1,5,16,4096]{3,2,1,0:T(8,128)}, u32[]{:S(2)}) %copy-start.1) | copy-done | bytes 1310744
  2.5 3.4 %collective-permute-start.1 = (f32[320,128]{1,0:T(8,128)S(1)}, f32[320,128]{1,0:T(8,128)S(1)}, u32[]{:S(2)}, u32[]{:S(2)}) collective-permute-start(f32[320,128]{1,0:T(8,128)S(1)} %get-tuple-element.72), channel_id=1, source_target_pairs={{1,2},{2,1},{3,4},{4,3},{5,6},{6,5},{7,8},{8,7},{9,10},{10,9},{11,... | collective-permute-start | bytes 491528 | tf_op jit(solution)/shard_map/ppermute | solution.py:540
  5.9 1.6 %collective-permute-start.2 = (f32[40,128]{1,0:T(8,128)S(1)}, f32[40,128]{1,0:T(8,128)S(1)}, u32[]{:S(2)}, u32[]{:S(2)}) collective-permute-start(f32[40,128]{1,0:T(8,128)S(1)} %get-tuple-element.73), channel_id=1, source_target_pairs={{0,16},{16,0},{1,17},{17,1},{2,18},{18,2},{3,19},{19,3},{4,20},{20... | collective-permute-start | bytes 61448 | tf_op jit(solution)/shard_map/ppermute | solution.py:544
  7.7 1.3 %copy-done.2 = f32[1,5,16,4096]{3,2,1,0:T(8,128)S(1)} copy-done((f32[1,5,16,4096]{3,2,1,0:T(8,128)S(1)}, f32[1,5,16,4096]{3,2,1,0:T(8,128)}, u32[]{:S(2)}) %copy-start.2) | copy-done | bytes 1310744
  9.0 1.1 %base.2 = (f32[3,1088,128]{2,1,0:T(8,128)S(1)}, f32[2,1088,128]{2,1,0:T(8,128)S(1)}, f32[8,64,128]{2,1,0:T(8,128)S(1)}, f32[64,128]{1,0:T(8,128)S(1)}, f32[8,128]{1,0:T(8,128)S(1)}) custom-call(f32[5,16,4096]{2,1,0:T(8,128)S(1)} %bitcast.5, f32[16,4096]{1,0:T(8,128)S(1)} %bitcast.10, f32[2000,128]{1,0:T(8,128)S(1)} %copy-done), custom_call_target="tpu_custom_call" | custom-call | flops 24000000 | tf_op jit(solution)/shard_map/base/pallas_call | solution.py:590
  10.9 1.2 %collective-permute-start.3 = (f32[32,128]{1,0:T(8,128)S(1)}, f32[32,128]{1,0:T(8,128)S(1)}, u32[]{:S(2)}, u32[]{:S(2)}) collective-permute-start(f32[32,128]{1,0:T(8,128)S(1)} %get-tuple-element.76), channel_id=1, source_target_pairs={{0,1},{1,0},{2,3},{3,2},{4,5},{5,4},{6,7},{7,6},{8,9},{9,8},{10,11... | collective-permute-start | bytes 49160 | tf_op jit(solution)/shard_map/ppermute | solution.py:540
  12.1 2.9 %collective-permute-start.4 = (f32[32,128]{1,0:T(8,128)S(1)}, f32[32,128]{1,0:T(8,128)S(1)}, u32[]{:S(2)}, u32[]{:S(2)}) collective-permute-start(f32[32,128]{1,0:T(8,128)S(1)} %get-tuple-element.77), channel_id=1, source_target_pairs={{1,2},{2,1},{3,4},{4,3},{5,6},{6,5},{7,8},{8,7},{9,10},{10,9},{11,... | collective-permute-start | bytes 49160 | tf_op jit(solution)/shard_map/ppermute | solution.py:540
  15.0 1.6 %collective-permute-start.5 = (f32[8,128]{1,0:T(8,128)S(1)}, f32[8,128]{1,0:T(8,128)S(1)}, u32[]{:S(2)}, u32[]{:S(2)}) collective-permute-start(f32[8,128]{1,0:T(8,128)S(1)} %get-tuple-element.78), channel_id=1, source_target_pairs={{0,16},{16,0},{1,17},{17,1},{2,18},{18,2},{3,19},{19,3},{4,20},{20... | collective-permute-start | bytes 12296 | tf_op jit(solution)/shard_map/ppermute | solution.py:544
  16.6 1.3 %tend.4 = (f32[3,16,4096]{2,1,0:T(8,128)S(1)}, f32[3,1088,128]{2,1,0:T(8,128)S(1)}) custom-call(f32[3,1088,128]{2,1,0:T(8,128)S(1)} %get-tuple-element.79.refs_0_, f32[5,16,4096]{2,1,0:T(8,128)S(1)} %bitcast.6, f32[16,4096]{1,0:T(8,128)S(1)} %bitcast.11, f32[320,128]{1,0:T(8,128)S(1)} %collective-permute-done.from_even.refs_3_, ...), custom_call_target="tpu_custom_call", output_to_operand_aliasing={{1}: (0, {})} | custom-call | flops 16000000 | tf_op jit(solution)/shard_map/tend/pallas_call | solution.py:607
  19.3 2.5 %collective-permute-start.7 = (f32[32,128]{1,0:T(8,128)S(1)}, f32[32,128]{1,0:T(8,128)S(1)}, u32[]{:S(2)}, u32[]{:S(2)}) collective-permute-start(f32[32,128]{1,0:T(8,128)S(1)} %get-tuple-element.87), channel_id=1, source_target_pairs={{1,2},{2,1},{3,4},{4,3},{5,6},{6,5},{7,8},{8,7},{9,10},{10,9},{11,... | collective-permute-start | bytes 49160 | tf_op jit(solution)/shard_map/ppermute | solution.py:540
  21.8 1.6 %collective-permute-start.8 = (f32[8,128]{1,0:T(8,128)S(1)}, f32[8,128]{1,0:T(8,128)S(1)}, u32[]{:S(2)}, u32[]{:S(2)}) collective-permute-start(f32[8,128]{1,0:T(8,128)S(1)} %get-tuple-element.88), channel_id=1, source_target_pairs={{0,16},{16,0},{1,17},{17,1},{2,18},{18,2},{3,19},{19,3},{4,20},{20... | collective-permute-start | bytes 12296 | tf_op jit(solution)/shard_map/ppermute | solution.py:544
  24.4 1.1 %collective-permute-done.8.refs_2_ = f32[8,128]{1,0:T(8,128)S(1)} collective-permute-done((f32[8,128]{1,0:T(8,128)S(1)}, f32[8,128]{1,0:T(8,128)S(1)}, u32[]{:S(2)}, u32[]{:S(2)}) %collective-permute-start.8) | collective-permute-done | bytes 4128 | tf_op jit(solution)/shard_map/ppermute | solution.py:544
  26.0 3.0 %collective-permute-start.10 = (f32[32,128]{1,0:T(8,128)S(1)}, f32[32,128]{1,0:T(8,128)S(1)}, u32[]{:S(2)}, u32[]{:S(2)}) collective-permute-start(f32[32,128]{1,0:T(8,128)S(1)} %get-tuple-element.95), channel_id=1, source_target_pairs={{1,2},{2,1},{3,4},{4,3},{5,6},{6,5},{7,8},{8,7},{9,10},{10,9},{11,... | collective-permute-start | bytes 49160 | tf_op jit(solution)/shard_map/ppermute | solution.py:540
  29.6 1.5 %collective-permute-start.11 = (f32[8,128]{1,0:T(8,128)S(1)}, f32[8,128]{1,0:T(8,128)S(1)}, u32[]{:S(2)}, u32[]{:S(2)}) collective-permute-start(f32[8,128]{1,0:T(8,128)S(1)} %get-tuple-element.96), channel_id=1, source_target_pairs={{0,16},{16,0},{1,17},{17,1},{2,18},{18,2},{3,19},{19,3},{4,20},{20... | collective-permute-start | bytes 12296 | tf_op jit(solution)/shard_map/ppermute | solution.py:544
  31.8 1.4 %collective-permute-done.11.refs_2_ = f32[8,128]{1,0:T(8,128)S(1)} collective-permute-done((f32[8,128]{1,0:T(8,128)S(1)}, f32[8,128]{1,0:T(8,128)S(1)}, u32[]{:S(2)}, u32[]{:S(2)}) %collective-permute-start.11) | collective-permute-done | bytes 4128 | tf_op jit(solution)/shard_map/ppermute | solution.py:544
  33.2 1.0 %correct.2 = (f32[5,16,4096]{2,1,0:T(8,128)S(1)}, f32[320,128]{1,0:T(8,128)S(1)}, f32[320,128]{1,0:T(8,128)S(1)}, f32[40,128]{1,0:T(8,128)S(1)}, f32[1088,128]{1,0:T(8,128)S(1)}) custom-call(f32[32,128]{1,0:T(8,128)S(1)} %collective-permute-done.9.refs_0_, f32[32,128]{1,0:T(8,128)S(1)} %collective-permute-done.10.refs_1_, ...), custom_call_target="tpu_custom_call", output_to_operand_aliasing={{4}: (4, {})} | custom-call | flops 16000000 | tf_op jit(solution)/shard_map/correct/pallas_call | solution.py:641
  34.3 3.4 %collective-permute-start.13 = (f32[320,128]{1,0:T(8,128)S(1)}, f32[320,128]{1,0:T(8,128)S(1)}, u32[]{:S(2)}, u32[]{:S(2)}) collective-permute-start(f32[320,128]{1,0:T(8,128)S(1)} %get-tuple-element.105), channel_id=1, source_target_pairs={{1,2},{2,1},{3,4},{4,3},{5,6},{6,5},{7,8},{8,7},{9,10},{10,9},{11,... | collective-permute-start | bytes 491528 | tf_op jit(solution)/shard_map/ppermute | solution.py:540
  37.8 1.6 %collective-permute-start.14 = (f32[40,128]{1,0:T(8,128)S(1)}, f32[40,128]{1,0:T(8,128)S(1)}, u32[]{:S(2)}, u32[]{:S(2)}) collective-permute-start(f32[40,128]{1,0:T(8,128)S(1)} %get-tuple-element.106), channel_id=1, source_target_pairs={{0,16},{16,0},{1,17},{17,1},{2,18},{18,2},{3,19},{19,3},{4,20},{20... | collective-permute-start | bytes 61448 | tf_op jit(solution)/shard_map/ppermute | solution.py:544
  39.3 1.1 %base.3 = (f32[3,1088,128]{2,1,0:T(8,128)S(1)}, f32[2,1088,128]{2,1,0:T(8,128)S(1)}, f32[8,64,128]{2,1,0:T(8,128)S(1)}, f32[64,128]{1,0:T(8,128)S(1)}, f32[8,128]{1,0:T(8,128)S(1)}) custom-call(f32[5,16,4096]{2,1,0:T(8,128)S(1)} %get-tuple-element.107.current.refs_1_, f32[16,4096]{1,0:T(8,128)S(1)} %bitcast.13, f32[2000,128]{1,0:T(8,128)S(1)} %copy-done), custom_call_target="tpu_custom_call" | custom-call | flops 24000000 | tf_op jit(solution)/shard_map/base/pallas_call | solution.py:590
  40.5 1.1 %collective-permute-done.14.planes.refs_5_ = f32[40,128]{1,0:T(8,128)S(1)} collective-permute-done((f32[40,128]{1,0:T(8,128)S(1)}, f32[40,128]{1,0:T(8,128)S(1)}, u32[]{:S(2)}, u32[]{:S(2)}) %collective-permute-start.14) | collective-permute-done | bytes 20512 | tf_op jit(solution)/shard_map/ppermute | solution.py:544
  42.6 1.3 %collective-permute-start.15 = (f32[32,128]{1,0:T(8,128)S(1)}, f32[32,128]{1,0:T(8,128)S(1)}, u32[]{:S(2)}, u32[]{:S(2)}) collective-permute-start(f32[32,128]{1,0:T(8,128)S(1)} %get-tuple-element.110), channel_id=1, source_target_pairs={{0,1},{1,0},{2,3},{3,2},{4,5},{5,4},{6,7},{7,6},{8,9},{9,8},{10,11... | collective-permute-start | bytes 49160 | tf_op jit(solution)/shard_map/ppermute | solution.py:540
  43.9 3.0 %collective-permute-start.16 = (f32[32,128]{1,0:T(8,128)S(1)}, f32[32,128]{1,0:T(8,128)S(1)}, u32[]{:S(2)}, u32[]{:S(2)}) collective-permute-start(f32[32,128]{1,0:T(8,128)S(1)} %get-tuple-element.111), channel_id=1, source_target_pairs={{1,2},{2,1},{3,4},{4,3},{5,6},{6,5},{7,8},{8,7},{9,10},{10,9},{11,... | collective-permute-start | bytes 49160 | tf_op jit(solution)/shard_map/ppermute | solution.py:540
  46.9 1.6 %collective-permute-start.17 = (f32[8,128]{1,0:T(8,128)S(1)}, f32[8,128]{1,0:T(8,128)S(1)}, u32[]{:S(2)}, u32[]{:S(2)}) collective-permute-start(f32[8,128]{1,0:T(8,128)S(1)} %get-tuple-element.112), channel_id=1, source_target_pairs={{0,16},{16,0},{1,17},{17,1},{2,18},{18,2},{3,19},{19,3},{4,20},{20... | collective-permute-start | bytes 12296 | tf_op jit(solution)/shard_map/ppermute | solution.py:544
  48.5 1.3 %tend.6 = (f32[3,16,4096]{2,1,0:T(8,128)S(1)}, f32[3,1088,128]{2,1,0:T(8,128)S(1)}) custom-call(f32[3,1088,128]{2,1,0:T(8,128)S(1)} %get-tuple-element.113.refs_0_, f32[5,16,4096]{2,1,0:T(8,128)S(1)} %get-tuple-element.107.current.refs_1_, f32[16,4096]{1,0:T(8,128)S(1)} %bitcast.14, ...), custom_call_target="tpu_custom_call", output_to_operand_aliasing={{1}: (0, {})} | custom-call | flops 16000000 | tf_op jit(solution)/shard_map/tend/pallas_call | solution.py:607
  51.2 2.5 %collective-permute-start.19 = (f32[32,128]{1,0:T(8,128)S(1)}, f32[32,128]{1,0:T(8,128)S(1)}, u32[]{:S(2)}, u32[]{:S(2)}) collective-permute-start(f32[32,128]{1,0:T(8,128)S(1)} %get-tuple-element.121), channel_id=1, source_target_pairs={{1,2},{2,1},{3,4},{4,3},{5,6},{6,5},{7,8},{8,7},{9,10},{10,9},{11,... | collective-permute-start | bytes 49160 | tf_op jit(solution)/shard_map/ppermute | solution.py:540
  53.7 1.6 %collective-permute-start.20 = (f32[8,128]{1,0:T(8,128)S(1)}, f32[8,128]{1,0:T(8,128)S(1)}, u32[]{:S(2)}, u32[]{:S(2)}) collective-permute-start(f32[8,128]{1,0:T(8,128)S(1)} %get-tuple-element.122), channel_id=1, source_target_pairs={{0,16},{16,0},{1,17},{17,1},{2,18},{18,2},{3,19},{19,3},{4,20},{20... | collective-permute-start | bytes 12296 | tf_op jit(solution)/shard_map/ppermute | solution.py:544
  55.2 1.0 %tend.7 = (f32[2,16,4096]{2,1,0:T(8,128)S(1)}, f32[2,1088,128]{2,1,0:T(8,128)S(1)}) custom-call(f32[2,1088,128]{2,1,0:T(8,128)S(1)} %get-tuple-element.123.refs_0_, f32[5,16,4096]{2,1,0:T(8,128)S(1)} %get-tuple-element.107.current.refs_1_, f32[16,4096]{1,0:T(8,128)S(1)} %bitcast.15, ...), custom_call_target="tpu_custom_call", output_to_operand_aliasing={{1}: (0, {})} | custom-call | flops 16000000 | tf_op jit(solution)/shard_map/tend/pallas_call | solution.py:607
  56.2 1.1 %collective-permute-done.20.refs_2_ = f32[8,128]{1,0:T(8,128)S(1)} collective-permute-done((f32[8,128]{1,0:T(8,128)S(1)}, f32[8,128]{1,0:T(8,128)S(1)}, u32[]{:S(2)}, u32[]{:S(2)}) %collective-permute-start.20) | collective-permute-done | bytes 4128 | tf_op jit(solution)/shard_map/ppermute | solution.py:544
  57.9 3.4 %collective-permute-start.22 = (f32[32,128]{1,0:T(8,128)S(1)}, f32[32,128]{1,0:T(8,128)S(1)}, u32[]{:S(2)}, u32[]{:S(2)}) collective-permute-start(f32[32,128]{1,0:T(8,128)S(1)} %get-tuple-element.129), channel_id=1, source_target_pairs={{1,2},{2,1},{3,4},{4,3},{5,6},{6,5},{7,8},{8,7},{9,10},{10,9},{11,... | collective-permute-start | bytes 49160 | tf_op jit(solution)/shard_map/ppermute | solution.py:540
  61.4 1.6 %collective-permute-start.23 = (f32[8,128]{1,0:T(8,128)S(1)}, f32[8,128]{1,0:T(8,128)S(1)}, u32[]{:S(2)}, u32[]{:S(2)}) collective-permute-start(f32[8,128]{1,0:T(8,128)S(1)} %get-tuple-element.130), channel_id=1, source_target_pairs={{0,16},{16,0},{1,17},{17,1},{2,18},{18,2},{3,19},{19,3},{4,20},{20... | collective-permute-start | bytes 12296 | tf_op jit(solution)/shard_map/ppermute | solution.py:544
  63.6 1.4 %collective-permute-done.23.refs_2_ = f32[8,128]{1,0:T(8,128)S(1)} collective-permute-done((f32[8,128]{1,0:T(8,128)S(1)}, f32[8,128]{1,0:T(8,128)S(1)}, u32[]{:S(2)}, u32[]{:S(2)}) %collective-permute-start.23) | collective-permute-done | bytes 4128 | tf_op jit(solution)/shard_map/ppermute | solution.py:544
  65.0 2.0 %correct.3 = (f32[5,16,4096]{2,1,0:T(8,128)}, f32[16,4096]{1,0:T(8,128)}, f32[1088,128]{1,0:T(8,128)S(1)}) custom-call(f32[32,128]{1,0:T(8,128)S(1)} %collective-permute-done.21.refs_0_, f32[32,128]{1,0:T(8,128)S(1)} %collective-permute-done.22.refs_1_, f32[8,128]{1,0:T(8,128)S(1)} %collective-permute-done.23.refs_2_, ...), custom_call_target="tpu_custom_call", output_to_operand_aliasing={{2}: (4, {})} | custom-call | flops 16000000 | tf_op jit(solution)/shard_map/correct/pallas_call | solution.py:641
  (49 shorter events, 9.3 us)
Async XLA Ops:
  0.6 7.1 %copy-start = (f32[2000,128]{1,0:T(8,128)S(1)}, f32[2000,128]{1,0:T(8,128)}, u32[]{:S(2)}) copy-start(f32[2000,128]{1,0:T(8,128)} %constant.2.clone.table.refs_6_.refs_7_) | copy-start | bytes 3072004
  0.6 1.4 %copy-start.1 = (f32[1,5,16,4096]{3,2,1,0:T(8,128)S(1)}, f32[1,5,16,4096]{3,2,1,0:T(8,128)}, u32[]{:S(2)}) copy-start(f32[1,5,16,4096]{3,2,1,0:T(8,128)} %param.4) | copy-start | bytes 3932164
  2.0 5.4 %copy-start.5 = (s32[1,1,1024]{2,1,0:T(1,128)S(1)}, s32[1,1,1024]{2,1,0:T(1,128)}, u32[]{:S(2)}) copy-start(s32[1,1,1024]{2,1,0:T(1,128)} %param.6) | copy-start | bytes 12292
  2.0 5.7 %copy-start.4 = (f32[1,16,4096]{2,1,0:T(8,128)S(1)}, f32[1,16,4096]{2,1,0:T(8,128)}, u32[]{:S(2)}) copy-start(f32[1,16,4096]{2,1,0:T(8,128)} %param.5) | copy-start | bytes 786436
  2.4 7.8 %collective-permute-start = (f32[320,128]{1,0:T(8,128)S(1)}, f32[320,128]{1,0:T(8,128)S(1)}, u32[]{:S(2)}, u32[]{:S(2)}) collective-permute-start(f32[320,128]{1,0:T(8,128)S(1)} %get-tuple-element.71), channel_id=1, source_target_pairs={{0,1},{1,0},{2,3},{3,2},{4,5},{5,4},{6,7},{7,6},{8,9},{9,8},{10,11... | collective-permute-start | bytes 491528 | tf_op jit(solution)/shard_map/ppermute | solution.py:540
  2.5 7.7 %collective-permute-start.1 = (f32[320,128]{1,0:T(8,128)S(1)}, f32[320,128]{1,0:T(8,128)S(1)}, u32[]{:S(2)}, u32[]{:S(2)}) collective-permute-start(f32[320,128]{1,0:T(8,128)S(1)} %get-tuple-element.72), channel_id=1, source_target_pairs={{1,2},{2,1},{3,4},{4,3},{5,6},{6,5},{7,8},{8,7},{9,10},{10,9},{11,... | collective-permute-start | bytes 491528 | tf_op jit(solution)/shard_map/ppermute | solution.py:540
  5.9 4.3 %collective-permute-start.2 = (f32[40,128]{1,0:T(8,128)S(1)}, f32[40,128]{1,0:T(8,128)S(1)}, u32[]{:S(2)}, u32[]{:S(2)}) collective-permute-start(f32[40,128]{1,0:T(8,128)S(1)} %get-tuple-element.73), channel_id=1, source_target_pairs={{0,16},{16,0},{1,17},{17,1},{2,18},{18,2},{3,19},{19,3},{4,20},{20... | collective-permute-start | bytes 61448 | tf_op jit(solution)/shard_map/ppermute | solution.py:544
  7.7 1.3 %copy-start.2 = (f32[1,5,16,4096]{3,2,1,0:T(8,128)S(1)}, f32[1,5,16,4096]{3,2,1,0:T(8,128)}, u32[]{:S(2)}) copy-start(f32[1,5,16,4096]{3,2,1,0:T(8,128)} %param.4) | copy-start | bytes 3932164
  10.9 7.8 %collective-permute-start.3 = (f32[32,128]{1,0:T(8,128)S(1)}, f32[32,128]{1,0:T(8,128)S(1)}, u32[]{:S(2)}, u32[]{:S(2)}) collective-permute-start(f32[32,128]{1,0:T(8,128)S(1)} %get-tuple-element.76), channel_id=1, source_target_pairs={{0,1},{1,0},{2,3},{3,2},{4,5},{5,4},{6,7},{7,6},{8,9},{9,8},{10,11... | collective-permute-start | bytes 49160 | tf_op jit(solution)/shard_map/ppermute | solution.py:540
  12.1 6.6 %collective-permute-start.4 = (f32[32,128]{1,0:T(8,128)S(1)}, f32[32,128]{1,0:T(8,128)S(1)}, u32[]{:S(2)}, u32[]{:S(2)}) collective-permute-start(f32[32,128]{1,0:T(8,128)S(1)} %get-tuple-element.77), channel_id=1, source_target_pairs={{1,2},{2,1},{3,4},{4,3},{5,6},{6,5},{7,8},{8,7},{9,10},{10,9},{11,... | collective-permute-start | bytes 49160 | tf_op jit(solution)/shard_map/ppermute | solution.py:540
  15.0 3.7 %collective-permute-start.5 = (f32[8,128]{1,0:T(8,128)S(1)}, f32[8,128]{1,0:T(8,128)S(1)}, u32[]{:S(2)}, u32[]{:S(2)}) collective-permute-start(f32[8,128]{1,0:T(8,128)S(1)} %get-tuple-element.78), channel_id=1, source_target_pairs={{0,16},{16,0},{1,17},{17,1},{2,18},{18,2},{3,19},{19,3},{4,20},{20... | collective-permute-start | bytes 12296 | tf_op jit(solution)/shard_map/ppermute | solution.py:544
  19.2 6.3 %collective-permute-start.6 = (f32[32,128]{1,0:T(8,128)S(1)}, f32[32,128]{1,0:T(8,128)S(1)}, u32[]{:S(2)}, u32[]{:S(2)}) collective-permute-start(f32[32,128]{1,0:T(8,128)S(1)} %get-tuple-element.86), channel_id=1, source_target_pairs={{0,1},{1,0},{2,3},{3,2},{4,5},{5,4},{6,7},{7,6},{8,9},{9,8},{10,11... | collective-permute-start | bytes 49160 | tf_op jit(solution)/shard_map/ppermute | solution.py:540
  19.3 6.2 %collective-permute-start.7 = (f32[32,128]{1,0:T(8,128)S(1)}, f32[32,128]{1,0:T(8,128)S(1)}, u32[]{:S(2)}, u32[]{:S(2)}) collective-permute-start(f32[32,128]{1,0:T(8,128)S(1)} %get-tuple-element.87), channel_id=1, source_target_pairs={{1,2},{2,1},{3,4},{4,3},{5,6},{6,5},{7,8},{8,7},{9,10},{10,9},{11,... | collective-permute-start | bytes 49160 | tf_op jit(solution)/shard_map/ppermute | solution.py:540
  21.8 3.7 %collective-permute-start.8 = (f32[8,128]{1,0:T(8,128)S(1)}, f32[8,128]{1,0:T(8,128)S(1)}, u32[]{:S(2)}, u32[]{:S(2)}) collective-permute-start(f32[8,128]{1,0:T(8,128)S(1)} %get-tuple-element.88), channel_id=1, source_target_pairs={{0,16},{16,0},{1,17},{17,1},{2,18},{18,2},{3,19},{19,3},{4,20},{20... | collective-permute-start | bytes 12296 | tf_op jit(solution)/shard_map/ppermute | solution.py:544
  26.0 7.2 %collective-permute-start.10 = (f32[32,128]{1,0:T(8,128)S(1)}, f32[32,128]{1,0:T(8,128)S(1)}, u32[]{:S(2)}, u32[]{:S(2)}) collective-permute-start(f32[32,128]{1,0:T(8,128)S(1)} %get-tuple-element.95), channel_id=1, source_target_pairs={{1,2},{2,1},{3,4},{4,3},{5,6},{6,5},{7,8},{8,7},{9,10},{10,9},{11,... | collective-permute-start | bytes 49160 | tf_op jit(solution)/shard_map/ppermute | solution.py:540
  29.0 4.2 %collective-permute-start.9 = (f32[32,128]{1,0:T(8,128)S(1)}, f32[32,128]{1,0:T(8,128)S(1)}, u32[]{:S(2)}, u32[]{:S(2)}) collective-permute-start(f32[32,128]{1,0:T(8,128)S(1)} %get-tuple-element.94), channel_id=1, source_target_pairs={{0,1},{1,0},{2,3},{3,2},{4,5},{5,4},{6,7},{7,6},{8,9},{9,8},{10,11... | collective-permute-start | bytes 49160 | tf_op jit(solution)/shard_map/ppermute | solution.py:540
  29.6 3.6 %collective-permute-start.11 = (f32[8,128]{1,0:T(8,128)S(1)}, f32[8,128]{1,0:T(8,128)S(1)}, u32[]{:S(2)}, u32[]{:S(2)}) collective-permute-start(f32[8,128]{1,0:T(8,128)S(1)} %get-tuple-element.96), channel_id=1, source_target_pairs={{0,16},{16,0},{1,17},{17,1},{2,18},{18,2},{3,19},{19,3},{4,20},{20... | collective-permute-start | bytes 12296 | tf_op jit(solution)/shard_map/ppermute | solution.py:544
  34.2 7.4 %collective-permute-start.12 = (f32[320,128]{1,0:T(8,128)S(1)}, f32[320,128]{1,0:T(8,128)S(1)}, u32[]{:S(2)}, u32[]{:S(2)}) collective-permute-start(f32[320,128]{1,0:T(8,128)S(1)} %get-tuple-element.104), channel_id=1, source_target_pairs={{0,1},{1,0},{2,3},{3,2},{4,5},{5,4},{6,7},{7,6},{8,9},{9,8},{10,11... | collective-permute-start | bytes 491528 | tf_op jit(solution)/shard_map/ppermute | solution.py:540
  34.3 7.6 %collective-permute-start.13 = (f32[320,128]{1,0:T(8,128)S(1)}, f32[320,128]{1,0:T(8,128)S(1)}, u32[]{:S(2)}, u32[]{:S(2)}) collective-permute-start(f32[320,128]{1,0:T(8,128)S(1)} %get-tuple-element.105), channel_id=1, source_target_pairs={{1,2},{2,1},{3,4},{4,3},{5,6},{6,5},{7,8},{8,7},{9,10},{10,9},{11,... | collective-permute-start | bytes 491528 | tf_op jit(solution)/shard_map/ppermute | solution.py:540
  37.8 3.8 %collective-permute-start.14 = (f32[40,128]{1,0:T(8,128)S(1)}, f32[40,128]{1,0:T(8,128)S(1)}, u32[]{:S(2)}, u32[]{:S(2)}) collective-permute-start(f32[40,128]{1,0:T(8,128)S(1)} %get-tuple-element.106), channel_id=1, source_target_pairs={{0,16},{16,0},{1,17},{17,1},{2,18},{18,2},{3,19},{19,3},{4,20},{20... | collective-permute-start | bytes 61448 | tf_op jit(solution)/shard_map/ppermute | solution.py:544
  40.5 8.0 %copy-start.3 = (f32[1,5,16,4096]{3,2,1,0:T(8,128)S(1)}, f32[1,5,16,4096]{3,2,1,0:T(8,128)}, u32[]{:S(2)}) copy-start(f32[1,5,16,4096]{3,2,1,0:T(8,128)} %param.4) | copy-start | bytes 3932164
  42.6 8.0 %collective-permute-start.15 = (f32[32,128]{1,0:T(8,128)S(1)}, f32[32,128]{1,0:T(8,128)S(1)}, u32[]{:S(2)}, u32[]{:S(2)}) collective-permute-start(f32[32,128]{1,0:T(8,128)S(1)} %get-tuple-element.110), channel_id=1, source_target_pairs={{0,1},{1,0},{2,3},{3,2},{4,5},{5,4},{6,7},{7,6},{8,9},{9,8},{10,11... | collective-permute-start | bytes 49160 | tf_op jit(solution)/shard_map/ppermute | solution.py:540
  43.9 6.6 %collective-permute-start.16 = (f32[32,128]{1,0:T(8,128)S(1)}, f32[32,128]{1,0:T(8,128)S(1)}, u32[]{:S(2)}, u32[]{:S(2)}) collective-permute-start(f32[32,128]{1,0:T(8,128)S(1)} %get-tuple-element.111), channel_id=1, source_target_pairs={{1,2},{2,1},{3,4},{4,3},{5,6},{6,5},{7,8},{8,7},{9,10},{10,9},{11,... | collective-permute-start | bytes 49160 | tf_op jit(solution)/shard_map/ppermute | solution.py:540
  46.9 3.7 %collective-permute-start.17 = (f32[8,128]{1,0:T(8,128)S(1)}, f32[8,128]{1,0:T(8,128)S(1)}, u32[]{:S(2)}, u32[]{:S(2)}) collective-permute-start(f32[8,128]{1,0:T(8,128)S(1)} %get-tuple-element.112), channel_id=1, source_target_pairs={{0,16},{16,0},{1,17},{17,1},{2,18},{18,2},{3,19},{19,3},{4,20},{20... | collective-permute-start | bytes 12296 | tf_op jit(solution)/shard_map/ppermute | solution.py:544
  51.1 6.2 %collective-permute-start.18 = (f32[32,128]{1,0:T(8,128)S(1)}, f32[32,128]{1,0:T(8,128)S(1)}, u32[]{:S(2)}, u32[]{:S(2)}) collective-permute-start(f32[32,128]{1,0:T(8,128)S(1)} %get-tuple-element.120), channel_id=1, source_target_pairs={{0,1},{1,0},{2,3},{3,2},{4,5},{5,4},{6,7},{7,6},{8,9},{9,8},{10,11... | collective-permute-start | bytes 49160 | tf_op jit(solution)/shard_map/ppermute | solution.py:540
  51.2 6.2 %collective-permute-start.19 = (f32[32,128]{1,0:T(8,128)S(1)}, f32[32,128]{1,0:T(8,128)S(1)}, u32[]{:S(2)}, u32[]{:S(2)}) collective-permute-start(f32[32,128]{1,0:T(8,128)S(1)} %get-tuple-element.121), channel_id=1, source_target_pairs={{1,2},{2,1},{3,4},{4,3},{5,6},{6,5},{7,8},{8,7},{9,10},{10,9},{11,... | collective-permute-start | bytes 49160 | tf_op jit(solution)/shard_map/ppermute | solution.py:540
  53.7 3.7 %collective-permute-start.20 = (f32[8,128]{1,0:T(8,128)S(1)}, f32[8,128]{1,0:T(8,128)S(1)}, u32[]{:S(2)}, u32[]{:S(2)}) collective-permute-start(f32[8,128]{1,0:T(8,128)S(1)} %get-tuple-element.122), channel_id=1, source_target_pairs={{0,16},{16,0},{1,17},{17,1},{2,18},{18,2},{3,19},{19,3},{4,20},{20... | collective-permute-start | bytes 12296 | tf_op jit(solution)/shard_map/ppermute | solution.py:544
  57.8 7.2 %collective-permute-start.21 = (f32[32,128]{1,0:T(8,128)S(1)}, f32[32,128]{1,0:T(8,128)S(1)}, u32[]{:S(2)}, u32[]{:S(2)}) collective-permute-start(f32[32,128]{1,0:T(8,128)S(1)} %get-tuple-element.128), channel_id=1, source_target_pairs={{0,1},{1,0},{2,3},{3,2},{4,5},{5,4},{6,7},{7,6},{8,9},{9,8},{10,11... | collective-permute-start | bytes 49160 | tf_op jit(solution)/shard_map/ppermute | solution.py:540
  57.9 7.1 %collective-permute-start.22 = (f32[32,128]{1,0:T(8,128)S(1)}, f32[32,128]{1,0:T(8,128)S(1)}, u32[]{:S(2)}, u32[]{:S(2)}) collective-permute-start(f32[32,128]{1,0:T(8,128)S(1)} %get-tuple-element.129), channel_id=1, source_target_pairs={{1,2},{2,1},{3,4},{4,3},{5,6},{6,5},{7,8},{8,7},{9,10},{10,9},{11,... | collective-permute-start | bytes 49160 | tf_op jit(solution)/shard_map/ppermute | solution.py:540
  61.4 3.7 %collective-permute-start.23 = (f32[8,128]{1,0:T(8,128)S(1)}, f32[8,128]{1,0:T(8,128)S(1)}, u32[]{:S(2)}, u32[]{:S(2)}) collective-permute-start(f32[8,128]{1,0:T(8,128)S(1)} %get-tuple-element.130), channel_id=1, source_target_pairs={{0,16},{16,0},{1,17},{17,1},{2,18},{18,2},{3,19},{19,3},{4,20},{20... | collective-permute-start | bytes 12296 | tf_op jit(solution)/shard_map/ppermute | solution.py:544
